TPU v7x, 256 devices: a whole 4x4x8 slice. The times are simulated.
256 devices in a mesh: fsdp: 16 (over z, y_hi), cols: 16 (over y_lo, x, core).
Axes of the slice: x: 4, y: 4 (y_hi: 2, y_lo: 2; y = y_hi * 2 + y_lo), z: 8, core: 2. Of those that a mesh axis runs over, the one named last changes fastest.
Arguments:
- train_gate: bfloat16 [3584, 14336], P('fsdp', 'cols'), may hold values from -0.09375 to 0.09375
- low_gate: bfloat16 [3584, 16], P('fsdp'), may hold values from -0.09375 to 0.09375
- high_gate: bfloat16 [16, 14336], P(None, 'cols'), may hold values from -1.5 to 1.5
- train_up: bfloat16 [3584, 14336], P('fsdp', 'cols'), may hold values from -0.09375 to 0.09375
- low_up: bfloat16 [3584, 16], P('fsdp'), may hold values from -0.09375 to 0.09375
- high_up: bfloat16 [16, 14336], P(None, 'cols'), may hold values from -1.5 to 1.5
- train_down: bfloat16 [14336, 3584], P('cols', 'fsdp'), may hold values from -0.046875 to 0.046875
- low_down: bfloat16 [14336, 16], P('cols'), may hold values from -0.046875 to 0.046875
- high_down: bfloat16 [16, 3584], P(None, 'fsdp'), may hold values from -1.5 to 1.5
- norm_train: float32 [3584], P(('fsdp', 'cols')), may hold values from 0.25 to 1.75
- norm_step: float32 [3584], P(('fsdp', 'cols')), may hold values from -0.3 to 0.3
Outputs:
- serving_gate: bfloat16 [3584, 14336], P(None, 'cols')
- serving_up: bfloat16 [3584, 14336], P(None, 'cols')
- serving_down: bfloat16 [14336, 3584], P('cols')
- serve_norm: bfloat16 [3584], replicated
All inputs are finite; a program needn't handle non-finite values.
Results may differ from a plain program's by a relative error of at most 0.001.
Values may be sent and summed in bfloat16 or wider, within the bound.
No kernel may reach another device: no remote copies, remote signals or barrier semaphores. Data moves between devices by JAX's collectives and lax.ppermute only.
A program may use at most 128 MiB of HBM per device.

v0:
```python
import jax
import jax.numpy as jnp
from jax import lax
from jax.sharding import PartitionSpec as P

mix_rate = 1.0


def rows_first(arrays, axis, dims):
    turned = [jnp.moveaxis(a, dim, 0) for a, dim in zip(arrays, dims)]
    both = jnp.concatenate([t.reshape(len(t), -1) for t in turned], axis=1)
    out, at, outs = (lax.all_gather(both, axis, axis=0, tiled=True), 0, [])
    for t, dim in zip(turned, dims):
        slab = out[:, at : at + t[0].size].reshape(-1, *t.shape[1:])
        outs.append(jnp.moveaxis(slab, 0, dim))
        at += t[0].size
    return tuple(outs)


def per_device(
    train_gate,
    low_gate,
    high_gate,
    train_up,
    low_up,
    high_up,
    train_down,
    low_down,
    high_down,
    norm_train,
    norm_step,
):
    whole_gate = train_gate.astype(jnp.float32) + mix_rate * jnp.dot(
        low_gate, high_gate, preferred_element_type=jnp.float32
    )
    whole_up = train_up.astype(jnp.float32) + mix_rate * jnp.dot(
        low_up, high_up, preferred_element_type=jnp.float32
    )
    whole_down = train_down.astype(jnp.float32) + mix_rate * jnp.dot(
        low_down, high_down, preferred_element_type=jnp.float32
    )
    narrow_gate, narrow_up, narrow_down = (
        whole_gate.astype(jnp.bfloat16),
        whole_up.astype(jnp.bfloat16),
        whole_down.astype(jnp.bfloat16),
    )
    serving_gate, serving_up, serving_down = rows_first(
        (narrow_gate, narrow_up, narrow_down), "fsdp", (0, 0, 1)
    )
    serve_norm = lax.all_gather(
        (norm_train + norm_step).astype(jnp.bfloat16), ("fsdp", "cols"), axis=0, tiled=True
    )
    return (serving_gate, serving_up, serving_down, serve_norm)


def solution(mesh):
    return jax.shard_map(
        per_device,
        mesh=mesh,
        in_specs=(
            P("fsdp", "cols"),
            P("fsdp", None),
            P(None, "cols"),
            P("fsdp", "cols"),
            P("fsdp", None),
            P(None, "cols"),
            P("cols", "fsdp"),
            P("cols", None),
            P(None, "fsdp"),
            P(("fsdp", "cols")),
            P(("fsdp", "cols")),
        ),
        out_specs=(P(None, "cols"), P(None, "cols"), P("cols", None), P()),
        check_vma=False,
    )
```

profile of v0, /device:TPU:1, one launch (start us, length us, event | category | flops | bytes accessed | tf_op | source)
XLA Modules:
  0.0 301.7 jit_solution(67208381330792148)
XLA Ops:
  7.2 0.0 copy-start
  7.2 0.0 all-gather.2.cloned.1.call-start
  7.2 0.7 copy-done
  7.9 1.3 fusion
  9.2 1.3 fusion.1
  10.6 0.0 copy-start.1
  10.6 0.0 copy-start.2
  10.6 1.4 fusion.3
  12.0 1.1 pad_maximum_fusion
  13.1 0.0 all-gather.2.cloned.1.call-update
  13.1 0.0 copy-done.1
  13.1 0.0 copy-done.2
  13.1 0.2 dynamic-update-slice
  13.4 189.9 %all-reduce = bf16[3584]{0:T(1024)(128)(2,1)} all-reduce(bf16[3584]{0:T(1024)(128)(2,1)S(1)} %dynamic-update-slice), channel_id=1, replica_groups=mesh['fsdp'=16,'cols'=16] {'fsdp','cols'}, use_global_device_ids=true, to_apply=%add | all-reduce | flops 3584 | bytes 14336
  203.3 67.5 %all-gather.2.cloned.1.call-done = bf16[3584,2688]{1,0:T(8,128)(2,1)} async-done(((bf16[224,2688]{1,0:T(8,128)(2,1)}), bf16[3584,2688]{1,0:T(8,128)(2,1)}) %all-gather.2.cloned.1.call-update) | async-done | bytes 19267600 | tf_op jit(solution)/shard_map/all_gather | solution.py:12
  270.8 14.6 %slice_bitcast_fusion = (bf16[896,3584]{0,1:T(8,128)(2,1)}, bf16[3584,896]{1,0:T(8,128)(2,1)}, bf16[3584,896]{1,0:T(8,128)(2,1)}) fusion(bf16[3584,2688]{1,0:T(8,128)(2,1)} %all-gather.2.cloned.1.call-done), kind=kLoop, calls=%fused_computation | loop fusion | bytes 38535168 | tf_op jit(solution)/shard_map/transpose | solution.py:15
  285.4 9.5 %copy.15 = bf16[896,3584]{1,0:T(8,128)(2,1)} copy(bf16[896,3584]{0,1:T(8,128)(2,1)} %get-tuple-element.8) | data formatting | bytes 12845056
  (2 shorter events, 0.0 us)
Async XLA Ops:
  7.2 0.8 copy-start
  7.2 263.6 %all-gather.2.cloned.1.call-start = ((), (), s32[]{:S(2)}) async-start(), calls=%async_computation | async-start | bytes 20471808 | tf_op jit(solution)/shard_map/all_gather | solution.py:12
  10.6 2.5 copy-start.1
  10.6 2.5 copy-start.2
Sparse Core Ops, SparseCore 0:
  13.2 257.5 all-gather.1
where the time goes:
time: 302 us
  blocking collectives  190 us (63%)
  waiting for transfers between devices  67.5 us (22%)
  local copies, waits for them, and re-layouts  25.1 us (8%)
  between operations  14.1 us (5%)
  matrix products  4 us (1%)
    unnamed x1, blocking collectives  190 us
    all_gather x1, waiting for transfers between devices, rows_first(): out, at, outs = (lax.all_gather(both, axis, axis=0, tiled=True), 0, [])  67.5 us
    transpose x1, local copies, waits for them, and re-layouts, rows_first(): outs.append(jnp.moveaxis(slab, 0, dim))  14.6 us
    unnamed x9, local copies, waits for them, and re-layouts  10.5 us
  transfers between devices with their start and end apart: 1, of which 1 were waited for; matrix products, arithmetic and copies ran while one was open for 0% of the time, Pallas kernels for 0%

commit v1 on v0

v1 whole, which is shorter than its diff:
```python
import jax
import jax.numpy as jnp
from jax import lax
from jax.experimental import pallas as pl
from jax.experimental.pallas import tpu as pltpu
from jax.sharding import PartitionSpec as P


mix_rate = 1.0
Z, H = 8, 2
ROWS, COLS = 224, 896

ROUNDS = (
    ((0, 0), (0, 0), (0, 0)),
    ((1, 0), (-1, 0), (1, 0)),
    ((2, 0), (-2, 0), (-2, 0)),
    ((3, 0), (-2, 1), (2, 0)),
    ((2, 1), (-3, 1), (-1, 0)),
)
UP = [(z * H + h, (z + 1) % Z * H + h) for z in range(Z) for h in range(H)]
DOWN = [(z * H + h, (z - 1) % Z * H + h) for z in range(Z) for h in range(H)]
ACROSS = [(z * H + h, z * H + 1 - h) for z in range(Z) for h in range(H)]
HOPS = (UP, DOWN, ACROSS)


def reached(direction, place):
    dz, h = place
    return ((dz + 1, h), (dz - 1, h), (dz, 1 - h))[direction]


def merged(base, low, high):
    return (
        base.astype(jnp.float32)
        + mix_rate * jnp.dot(low, high, preferred_element_type=jnp.float32)
    ).astype(jnp.bfloat16)


def exchange(stage, total):
    name, bit = stage
    got = lax.ppermute(total, name, [(i, i ^ bit) for i in range(16)])
    return total + got


STAGES = (
    ("fsdp", 8),
    ("cols", 1),
    ("cols", 2),
    ("cols", 4),
    ("cols", 8),
    ("fsdp", 1),
    ("fsdp", 2),
    ("fsdp", 4),
)


def gather_norm(own):
    at = lax.axis_index("fsdp") * 16 + lax.axis_index("cols")
    total = lax.dynamic_update_slice(
        jnp.zeros((3584,), own.dtype), own, (at.astype(jnp.uint32) * 14,)
    )
    for stage in STAGES:
        total = exchange(stage, total)
    return total


def per_device(
    train_gate,
    low_gate,
    high_gate,
    train_up,
    low_up,
    high_up,
    train_down,
    low_down,
    high_down,
    norm_train,
    norm_step,
):
    me = lax.axis_index("fsdp").astype(jnp.uint32)

    def slot(place):
        return (((me >> 1) + (Z - place[0])) & 7) * 2 + ((me & 1) ^ place[1])

    serve_norm = gather_norm((norm_train + norm_step).astype(jnp.bfloat16))
    own_down = merged(train_down.T, high_down.T, low_down.T)
    own_gate = merged(train_gate, low_gate, high_gate)
    own_up = merged(train_up, low_up, high_up)
    own = (jnp.stack([own_down, own_gate]), own_up[None])
    own = lax.optimization_barrier(own)
    held = [{(0, 0): piece} for piece in own]
    for senders in ROUNDS:
        for k in range(len(own)):
            for direction, place in enumerate(senders):
                got = lax.ppermute(held[k][place], "fsdp", HOPS[direction])
                held[k][reached(direction, place)] = got
    zero = jnp.uint32(0)
    stacks = [empty() for _ in range(3)]
    for place in held[0]:
        parts = (held[0][place][:1], held[0][place][1:], held[1][place])
        for i, part in enumerate(parts):
            stacks[i] = lax.dynamic_update_slice(
                stacks[i], part, (slot(place), zero, zero)
            )
    down, gate, up = (stack.reshape(3584, COLS) for stack in stacks)
    return gate, up, down.T, serve_norm


def empty():
    return pl.pallas_call(
        lambda out_ref: None,
        out_specs=pl.BlockSpec(memory_space=pltpu.HBM),
        out_shape=jax.ShapeDtypeStruct((16, ROWS, COLS), jnp.bfloat16),
        compiler_params=pltpu.CompilerParams(has_side_effects=True),
        name="empty",
    )()


def solution(mesh):
    return jax.shard_map(
        per_device,
        mesh=mesh,
        in_specs=(
            P("fsdp", "cols"),
            P("fsdp", None),
            P(None, "cols"),
            P("fsdp", "cols"),
            P("fsdp", None),
            P(None, "cols"),
            P("cols", "fsdp"),
            P("cols", None),
            P(None, "fsdp"),
            P(("fsdp", "cols")),
            P(("fsdp", "cols")),
        ),
        out_specs=(P(None, "cols"), P(None, "cols"), P("cols", None), P()),
        check_vma=False,
    )
```

time: 302 us -> 212 us (0.70)
  the two profiles are of different devices: /device:TPU:1 before, /device:TPU:6 now
where the time goes in v1:
time: 212 us
  waiting for transfers between devices  101 us (48%)
  starting transfers between devices  66.5 us (31%)
  local copies, waits for them, and re-layouts  37.8 us (18%)
  matrix products  3.98 us (2%)
    ppermute x30, waiting for transfers between devices, per_device(): got = lax.ppermute(held[k][place], 'fsdp', HOPS[direction])  84.2 us
    ppermute x30, starting transfers between devices, per_device(): got = lax.ppermute(held[k][place], 'fsdp', HOPS[direction])  50 us
    dynamic_update_slice x31, local copies, waits for them, and re-layouts, per_device(): lax.dynamic_update_slice(stacks[i], part, (slot(place), zero, zero))  27.9 us
    ppermute x8, waiting for transfers between devices, exchange(): got = lax.ppermute(total, name, [(i, i ^ bit) for i in range(16)])  17.2 us
    ppermute x8, starting transfers between devices, exchange(): got = lax.ppermute(total, name, [(i, i ^ bit) for i in range(16)])  16.6 us
    reshape x1, local copies, waits for them, and re-layouts, per_device(): down, gate, up = (stack.reshape(3584, COLS) for stack in stacks)  9.52 us
  transfers between devices with their start and end apart: 38, of which 17 were waited for; matrix products, arithmetic and copies ran while one was open for 15% of the time, Pallas kernels for 0%

profile of v1, /device:TPU:6, one launch (start us, length us, event | category | flops | bytes accessed | tf_op | source)
XLA Modules:
  0.0 212.0 jit_solution(553739694599458604)
XLA Ops:
  1.5 7.2 %collective-permute-start.30 = (bf16[3584]{0:T(1024)(128)(2,1)S(1)}, bf16[3584]{0:T(1024)(128)(2,1)S(1)}, u32[]{:S(2)}, u32[]{:S(2)}) collective-permute-start(bf16[3584]{0:T(1024)(128)(2,1)S(1)} %dynamic_update_slice.197), channel_id=1, source_target_pairs={{0,128},{16,144},{32,160},{48,176},{64,192},{80,208},{96,224},{112... | collective-permute-start | bytes 21512 | tf_op jit(solution)/shard_map/ppermute | solution.py:40
  14.0 2.2 %collective-permute-start.16 = (bf16[1,224,896]{2,1,0:T(8,128)(2,1)S(1)}, bf16[1,224,896]{2,1,0:T(8,128)(2,1)S(1)}, u32[]{:S(2)}, u32[]{:S(2)}) collective-permute-start(bf16[1,224,896]{2,1,0:T(8,128)(2,1)S(1)} %fusion.3), channel_id=1, source_target_pairs={{0,224},{16,240},{32,0},{48,16},{64,32},{80,48},{96,64},{112,80},{... | collective-permute-start | bytes 1204232 | tf_op jit(solution)/shard_map/ppermute | solution.py:94
  18.5 2.8 %collective-permute-done.32 = bf16[3584]{0:T(1024)(128)(2,1)S(1)} collective-permute-done((bf16[3584]{0:T(1024)(128)(2,1)S(1)}, bf16[3584]{0:T(1024)(128)(2,1)S(1)}, u32[]{:S(2)}, u32[]{:S(2)}) %collective-permute-start.32) | collective-permute-done | bytes 7200 | tf_op jit(solution)/shard_map/ppermute | solution.py:40
  22.8 3.7 %collective-permute-done.33 = bf16[3584]{0:T(1024)(128)(2,1)S(1)} collective-permute-done((bf16[3584]{0:T(1024)(128)(2,1)S(1)}, bf16[3584]{0:T(1024)(128)(2,1)S(1)}, u32[]{:S(2)}, u32[]{:S(2)}) %collective-permute-start.33) | collective-permute-done | bytes 7200 | tf_op jit(solution)/shard_map/ppermute | solution.py:40
  28.1 2.1 collective-permute-done.34
  30.2 3.2 %collective-permute-start.35 = (bf16[3584]{0:T(1024)(128)(2,1)S(1)}, bf16[3584]{0:T(1024)(128)(2,1)S(1)}, u32[]{:S(2)}, u32[]{:S(2)}) collective-permute-start(bf16[3584]{0:T(1024)(128)(2,1)S(1)} %add.220), channel_id=1, source_target_pairs={{0,16},{16,0},{32,48},{48,32},{64,80},{80,64},{96,112},{112,96},{1... | collective-permute-start | bytes 21512 | tf_op jit(solution)/shard_map/ppermute | solution.py:40
  36.1 3.5 %collective-permute-done.36 = bf16[3584]{0:T(1024)(128)(2,1)S(1)} collective-permute-done((bf16[3584]{0:T(1024)(128)(2,1)S(1)}, bf16[3584]{0:T(1024)(128)(2,1)S(1)}, u32[]{:S(2)}, u32[]{:S(2)}) %collective-permute-start.36) | collective-permute-done | bytes 7200 | tf_op jit(solution)/shard_map/ppermute | solution.py:40
  42.3 2.0 collective-permute-done.37
  44.3 3.2 %collective-permute-start.17 = (bf16[1,224,896]{2,1,0:T(8,128)(2,1)S(1)}, bf16[1,224,896]{2,1,0:T(8,128)(2,1)S(1)}, u32[]{:S(2)}, u32[]{:S(2)}) collective-permute-start(bf16[1,224,896]{2,1,0:T(8,128)(2,1)S(1)} %fusion.3), channel_id=1, source_target_pairs={{0,16},{16,0},{32,48},{48,32},{64,80},{80,64},{96,112},{112,96},{1... | collective-permute-start | bytes 1204232 | tf_op jit(solution)/shard_map/ppermute | solution.py:94
  49.4 2.5 %collective-permute-start.19 = (bf16[1,224,896]{2,1,0:T(8,128)(2,1)S(1)}, bf16[1,224,896]{2,1,0:T(8,128)(2,1)S(1)}, u32[]{:S(2)}, u32[]{:S(2)}) collective-permute-start(bf16[1,224,896]{2,1,0:T(8,128)(2,1)S(1)} %collective-permute-done.16), channel_id=1, source_target_pairs={{0,224},{16,240},{32,0},{48,16},{64,32},{80,48},{96,64},{112,80},{... | collective-permute-start | bytes 1204232 | tf_op jit(solution)/shard_map/ppermute | solution.py:94
  54.5 3.4 %collective-permute-done.17 = bf16[1,224,896]{2,1,0:T(8,128)(2,1)S(1)} collective-permute-done((bf16[1,224,896]{2,1,0:T(8,128)(2,1)S(1)}, bf16[1,224,896]{2,1,0:T(8,128)(2,1)S(1)}, u32[]{:S(2)}, u32[]{:S(2)}) %collective-permute-start.17) | collective-permute-done | bytes 401440 | tf_op jit(solution)/shard_map/ppermute | solution.py:94
  57.9 2.5 %collective-permute-start.18 = (bf16[1,224,896]{2,1,0:T(8,128)(2,1)}, bf16[1,224,896]{2,1,0:T(8,128)(2,1)S(1)}, u32[]{:S(2)}, u32[]{:S(2)}) collective-permute-start(bf16[1,224,896]{2,1,0:T(8,128)(2,1)} %collective-permute-done.15), channel_id=1, source_target_pairs={{0,32},{16,48},{32,64},{48,80},{64,96},{80,112},{96,128},{112,144}... | collective-permute-start | bytes 1204232 | tf_op jit(solution)/shard_map/ppermute | solution.py:94
  61.2 3.2 %collective-permute-start.20 = (bf16[1,224,896]{2,1,0:T(8,128)(2,1)}, bf16[1,224,896]{2,1,0:T(8,128)(2,1)S(1)}, u32[]{:S(2)}, u32[]{:S(2)}) collective-permute-start(bf16[1,224,896]{2,1,0:T(8,128)(2,1)} %collective-permute-done.15), channel_id=1, source_target_pairs={{0,16},{16,0},{32,48},{48,32},{64,80},{80,64},{96,112},{112,96},{1... | collective-permute-start | bytes 1204232 | tf_op jit(solution)/shard_map/ppermute | solution.py:94
  65.3 3.4 %collective-permute-done.19 = bf16[1,224,896]{2,1,0:T(8,128)(2,1)S(1)} collective-permute-done((bf16[1,224,896]{2,1,0:T(8,128)(2,1)S(1)}, bf16[1,224,896]{2,1,0:T(8,128)(2,1)S(1)}, u32[]{:S(2)}, u32[]{:S(2)}) %collective-permute-start.19) | collective-permute-done | bytes 401440 | tf_op jit(solution)/shard_map/ppermute | solution.py:94
  70.9 4.2 %collective-permute-done.2 = bf16[2,224,896]{2,1,0:T(8,128)(2,1)S(1)} collective-permute-done((bf16[2,224,896]{2,1,0:T(8,128)(2,1)S(1)}, bf16[2,224,896]{2,1,0:T(8,128)(2,1)S(1)}, u32[]{:S(2)}, u32[]{:S(2)}) %collective-permute-start.2) | collective-permute-done | bytes 802848 | tf_op jit(solution)/shard_map/ppermute | solution.py:94
  75.1 3.2 %collective-permute-start.23 = (bf16[1,224,896]{2,1,0:T(8,128)(2,1)S(1)}, bf16[1,224,896]{2,1,0:T(8,128)(2,1)S(1)}, u32[]{:S(2)}, u32[]{:S(2)}) collective-permute-start(bf16[1,224,896]{2,1,0:T(8,128)(2,1)S(1)} %collective-permute-done.19), channel_id=1, source_target_pairs={{0,16},{16,0},{32,48},{48,32},{64,80},{80,64},{96,112},{112,96},{1... | collective-permute-start | bytes 1204232 | tf_op jit(solution)/shard_map/ppermute | solution.py:94
  78.3 2.5 %collective-permute-start.21 = (bf16[1,224,896]{2,1,0:T(8,128)(2,1)S(1)}, bf16[1,224,896]{2,1,0:T(8,128)(2,1)S(1)}, u32[]{:S(2)}, u32[]{:S(2)}) collective-permute-start(bf16[1,224,896]{2,1,0:T(8,128)(2,1)S(1)} %collective-permute-done.18), channel_id=1, source_target_pairs={{0,32},{16,48},{32,64},{48,80},{64,96},{80,112},{96,128},{112,144}... | collective-permute-start | bytes 1204232 | tf_op jit(solution)/shard_map/ppermute | solution.py:94
  83.7 2.4 %collective-permute-start.4 = (bf16[2,224,896]{2,1,0:T(8,128)(2,1)S(1)}, bf16[2,224,896]{2,1,0:T(8,128)(2,1)S(1)}, u32[]{:S(2)}, u32[]{:S(2)}) collective-permute-start(bf16[2,224,896]{2,1,0:T(8,128)(2,1)S(1)} %collective-permute-done.1), channel_id=1, source_target_pairs={{0,224},{16,240},{32,0},{48,16},{64,32},{80,48},{96,64},{112,80},{... | collective-permute-start | bytes 2408456 | tf_op jit(solution)/shard_map/ppermute | solution.py:94
  86.9 5.1 %collective-permute-done.21 = bf16[1,224,896]{2,1,0:T(8,128)(2,1)S(1)} collective-permute-done((bf16[1,224,896]{2,1,0:T(8,128)(2,1)S(1)}, bf16[1,224,896]{2,1,0:T(8,128)(2,1)S(1)}, u32[]{:S(2)}, u32[]{:S(2)}) %collective-permute-start.21) | collective-permute-done | bytes 401440 | tf_op jit(solution)/shard_map/ppermute | solution.py:94
  92.0 3.2 %collective-permute-start.26 = (bf16[1,224,896]{2,1,0:T(8,128)(2,1)S(1)}, bf16[1,224,896]{2,1,0:T(8,128)(2,1)S(1)}, u32[]{:S(2)}, u32[]{:S(2)}) collective-permute-start(bf16[1,224,896]{2,1,0:T(8,128)(2,1)S(1)} %collective-permute-done.18), channel_id=1, source_target_pairs={{0,16},{16,0},{32,48},{48,32},{64,80},{80,64},{96,112},{112,96},{1... | collective-permute-start | bytes 1204232 | tf_op jit(solution)/shard_map/ppermute | solution.py:94
  98.6 7.0 %collective-permute-done.26 = bf16[1,224,896]{2,1,0:T(8,128)(2,1)S(1)} collective-permute-done((bf16[1,224,896]{2,1,0:T(8,128)(2,1)S(1)}, bf16[1,224,896]{2,1,0:T(8,128)(2,1)S(1)}, u32[]{:S(2)}, u32[]{:S(2)}) %collective-permute-start.26) | collective-permute-done | bytes 401440 | tf_op jit(solution)/shard_map/ppermute | solution.py:94
  107.4 2.5 %collective-permute-start.6 = (bf16[2,224,896]{2,1,0:T(8,128)(2,1)S(1)}, bf16[2,224,896]{2,1,0:T(8,128)(2,1)S(1)}, u32[]{:S(2)}, u32[]{:S(2)}) collective-permute-start(bf16[2,224,896]{2,1,0:T(8,128)(2,1)S(1)} %collective-permute-done.3), channel_id=1, source_target_pairs={{0,32},{16,48},{32,64},{48,80},{64,96},{80,112},{96,128},{112,144}... | collective-permute-start | bytes 2408456 | tf_op jit(solution)/shard_map/ppermute | solution.py:94
  111.6 7.4 %collective-permute-done.24 = bf16[1,224,896]{2,1,0:T(8,128)(2,1)S(1)} collective-permute-done((bf16[1,224,896]{2,1,0:T(8,128)(2,1)S(1)}, bf16[1,224,896]{2,1,0:T(8,128)(2,1)S(1)}, u32[]{:S(2)}, u32[]{:S(2)}) %collective-permute-start.24) | collective-permute-done | bytes 401440 | tf_op jit(solution)/shard_map/ppermute | solution.py:94
  119.0 3.2 %collective-permute-start.8 = (bf16[2,224,896]{2,1,0:T(8,128)(2,1)S(1)}, bf16[2,224,896]{2,1,0:T(8,128)(2,1)S(1)}, u32[]{:S(2)}, u32[]{:S(2)}) collective-permute-start(bf16[2,224,896]{2,1,0:T(8,128)(2,1)S(1)} %collective-permute-done.4), channel_id=1, source_target_pairs={{0,16},{16,0},{32,48},{48,32},{64,80},{80,64},{96,112},{112,96},{1... | collective-permute-start | bytes 2408456 | tf_op jit(solution)/shard_map/ppermute | solution.py:94
  123.0 3.0 %collective-permute-start.11 = (bf16[2,224,896]{2,1,0:T(8,128)(2,1)S(1)}, bf16[2,224,896]{2,1,0:T(8,128)(2,1)S(1)}, u32[]{:S(2)}, u32[]{:S(2)}) collective-permute-start(bf16[2,224,896]{2,1,0:T(8,128)(2,1)S(1)} %collective-permute-done.3), channel_id=1, source_target_pairs={{0,16},{16,0},{32,48},{48,32},{64,80},{80,64},{96,112},{112,96},{1... | collective-permute-start | bytes 2408456 | tf_op jit(solution)/shard_map/ppermute | solution.py:94
  130.6 32.3 %collective-permute-done.29 = bf16[1,224,896]{2,1,0:T(8,128)(2,1)S(1)} collective-permute-done((bf16[1,224,896]{2,1,0:T(8,128)(2,1)S(1)}, bf16[1,224,896]{2,1,0:T(8,128)(2,1)S(1)}, u32[]{:S(2)}, u32[]{:S(2)}) %collective-permute-start.29) | collective-permute-done | bytes 401440 | tf_op jit(solution)/shard_map/ppermute | solution.py:94
  162.9 3.2 %collective-permute-start.14 = (bf16[2,224,896]{2,1,0:T(8,128)(2,1)S(1)}, bf16[2,224,896]{2,1,0:T(8,128)(2,1)S(1)}, u32[]{:S(2)}, u32[]{:S(2)}) collective-permute-start(bf16[2,224,896]{2,1,0:T(8,128)(2,1)S(1)} %collective-permute-done.1), channel_id=1, source_target_pairs={{0,16},{16,0},{32,48},{48,32},{64,80},{80,64},{96,112},{112,96},{1... | collective-permute-start | bytes 2408456 | tf_op jit(solution)/shard_map/ppermute | solution.py:94
  166.1 3.2 %collective-permute-start.10 = (bf16[2,224,896]{2,1,0:T(8,128)(2,1)S(1)}, bf16[2,224,896]{2,1,0:T(8,128)(2,1)S(1)}, u32[]{:S(2)}, u32[]{:S(2)}) collective-permute-start(bf16[2,224,896]{2,1,0:T(8,128)(2,1)S(1)} %collective-permute-done.8), channel_id=1, source_target_pairs={{0,224},{16,240},{32,0},{48,16},{64,32},{80,48},{96,64},{112,80},{... | collective-permute-start | bytes 2408456 | tf_op jit(solution)/shard_map/ppermute | solution.py:94
  172.9 14.2 %collective-permute-done.10 = bf16[2,224,896]{2,1,0:T(8,128)(2,1)S(1)} collective-permute-done((bf16[2,224,896]{2,1,0:T(8,128)(2,1)S(1)}, bf16[2,224,896]{2,1,0:T(8,128)(2,1)S(1)}, u32[]{:S(2)}, u32[]{:S(2)}) %collective-permute-start.10) | collective-permute-done | bytes 802848 | tf_op jit(solution)/shard_map/ppermute | solution.py:94
  187.2 3.7 %collective-permute-start.13 = (bf16[2,224,896]{2,1,0:T(8,128)(2,1)S(1)}, bf16[2,224,896]{2,1,0:T(8,128)(2,1)S(1)}, u32[]{:S(2)}, u32[]{:S(2)}) collective-permute-start(bf16[2,224,896]{2,1,0:T(8,128)(2,1)S(1)} %collective-permute-done.10), channel_id=1, source_target_pairs={{0,224},{16,240},{32,0},{48,16},{64,32},{80,48},{96,64},{112,80},{... | collective-permute-start | bytes 2408456 | tf_op jit(solution)/shard_map/ppermute | solution.py:94
  194.7 5.9 %collective-permute-done.13 = bf16[2,224,896]{2,1,0:T(8,128)(2,1)S(1)} collective-permute-done((bf16[2,224,896]{2,1,0:T(8,128)(2,1)S(1)}, bf16[2,224,896]{2,1,0:T(8,128)(2,1)S(1)}, u32[]{:S(2)}, u32[]{:S(2)}) %collective-permute-start.13) | collective-permute-done | bytes 802848 | tf_op jit(solution)/shard_map/ppermute | solution.py:94
  202.4 9.5 %copy.15 = bf16[3584,896]{0,1:T(8,128)(2,1)} copy(bf16[3584,896]{1,0:T(8,128)(2,1)} %bitcast.18) | data formatting | bytes 12845056 | tf_op jit(solution)/shard_map/reshape | solution.py:104
  (97 shorter events, 50.6 us)
Async XLA Ops:
  1.5 14.7 %collective-permute-start.30 = (bf16[3584]{0:T(1024)(128)(2,1)S(1)}, bf16[3584]{0:T(1024)(128)(2,1)S(1)}, u32[]{:S(2)}, u32[]{:S(2)}) collective-permute-start(bf16[3584]{0:T(1024)(128)(2,1)S(1)} %dynamic_update_slice.197), channel_id=1, source_target_pairs={{0,128},{16,144},{32,160},{48,176},{64,192},{80,208},{96,224},{112... | collective-permute-start | bytes 21512 | tf_op jit(solution)/shard_map/ppermute | solution.py:40
  12.9 36.2 %collective-permute-start.15 = (bf16[1,224,896]{2,1,0:T(8,128)(2,1)S(1)}, bf16[1,224,896]{2,1,0:T(8,128)(2,1)}, u32[]{:S(2)}, u32[]{:S(2)}) collective-permute-start(bf16[1,224,896]{2,1,0:T(8,128)(2,1)S(1)} %fusion.3), channel_id=1, source_target_pairs={{0,32},{16,48},{32,64},{48,80},{64,96},{80,112},{96,128},{112,144}... | collective-permute-start | bytes 1204232 | tf_op jit(solution)/shard_map/ppermute | solution.py:94
  14.0 35.5 %collective-permute-start.16 = (bf16[1,224,896]{2,1,0:T(8,128)(2,1)S(1)}, bf16[1,224,896]{2,1,0:T(8,128)(2,1)S(1)}, u32[]{:S(2)}, u32[]{:S(2)}) collective-permute-start(bf16[1,224,896]{2,1,0:T(8,128)(2,1)S(1)} %fusion.3), channel_id=1, source_target_pairs={{0,224},{16,240},{32,0},{48,16},{64,32},{80,48},{96,64},{112,80},{... | collective-permute-start | bytes 1204232 | tf_op jit(solution)/shard_map/ppermute | solution.py:94
  16.2 45.0 %collective-permute-start = (bf16[2,224,896]{2,1,0:T(8,128)(2,1)S(1)}, bf16[2,224,896]{2,1,0:T(8,128)(2,1)S(1)}, u32[]{:S(2)}, u32[]{:S(2)}) collective-permute-start(bf16[2,224,896]{2,1,0:T(8,128)(2,1)S(1)} %pad_maximum_fusion), channel_id=1, source_target_pairs={{0,32},{16,48},{32,64},{48,80},{64,96},{80,112},{96,128},{112,144}... | collective-permute-start | bytes 2408456 | tf_op jit(solution)/shard_map/ppermute | solution.py:94
  21.3 5.2 %collective-permute-start.33 = (bf16[3584]{0:T(1024)(128)(2,1)S(1)}, bf16[3584]{0:T(1024)(128)(2,1)S(1)}, u32[]{:S(2)}, u32[]{:S(2)}) collective-permute-start(bf16[3584]{0:T(1024)(128)(2,1)S(1)} %add.218), channel_id=1, source_target_pairs={{0,4},{1,5},{2,6},{3,7},{4,0},{5,1},{6,2},{7,3},{8,12},{9,13},{10,... | collective-permute-start | bytes 21512 | tf_op jit(solution)/shard_map/ppermute | solution.py:40
  41.1 24.2 %collective-permute-start.1 = (bf16[2,224,896]{2,1,0:T(8,128)(2,1)S(1)}, bf16[2,224,896]{2,1,0:T(8,128)(2,1)S(1)}, u32[]{:S(2)}, u32[]{:S(2)}) collective-permute-start(bf16[2,224,896]{2,1,0:T(8,128)(2,1)S(1)} %pad_maximum_fusion), channel_id=1, source_target_pairs={{0,224},{16,240},{32,0},{48,16},{64,32},{80,48},{96,64},{112,80},{... | collective-permute-start | bytes 2408456 | tf_op jit(solution)/shard_map/ppermute | solution.py:94
  44.3 13.7 %collective-permute-start.17 = (bf16[1,224,896]{2,1,0:T(8,128)(2,1)S(1)}, bf16[1,224,896]{2,1,0:T(8,128)(2,1)S(1)}, u32[]{:S(2)}, u32[]{:S(2)}) collective-permute-start(bf16[1,224,896]{2,1,0:T(8,128)(2,1)S(1)} %fusion.3), channel_id=1, source_target_pairs={{0,16},{16,0},{32,48},{48,32},{64,80},{80,64},{96,112},{112,96},{1... | collective-permute-start | bytes 1204232 | tf_op jit(solution)/shard_map/ppermute | solution.py:94
  49.1 26.0 %collective-permute-start.2 = (bf16[2,224,896]{2,1,0:T(8,128)(2,1)S(1)}, bf16[2,224,896]{2,1,0:T(8,128)(2,1)S(1)}, u32[]{:S(2)}, u32[]{:S(2)}) collective-permute-start(bf16[2,224,896]{2,1,0:T(8,128)(2,1)S(1)} %pad_maximum_fusion), channel_id=1, source_target_pairs={{0,16},{16,0},{32,48},{48,32},{64,80},{80,64},{96,112},{112,96},{1... | collective-permute-start | bytes 2408456 | tf_op jit(solution)/shard_map/ppermute | solution.py:94
  49.4 19.3 %collective-permute-start.19 = (bf16[1,224,896]{2,1,0:T(8,128)(2,1)S(1)}, bf16[1,224,896]{2,1,0:T(8,128)(2,1)S(1)}, u32[]{:S(2)}, u32[]{:S(2)}) collective-permute-start(bf16[1,224,896]{2,1,0:T(8,128)(2,1)S(1)} %collective-permute-done.16), channel_id=1, source_target_pairs={{0,224},{16,240},{32,0},{48,16},{64,32},{80,48},{96,64},{112,80},{... | collective-permute-start | bytes 1204232 | tf_op jit(solution)/shard_map/ppermute | solution.py:94
  57.9 20.4 %collective-permute-start.18 = (bf16[1,224,896]{2,1,0:T(8,128)(2,1)}, bf16[1,224,896]{2,1,0:T(8,128)(2,1)S(1)}, u32[]{:S(2)}, u32[]{:S(2)}) collective-permute-start(bf16[1,224,896]{2,1,0:T(8,128)(2,1)} %collective-permute-done.15), channel_id=1, source_target_pairs={{0,32},{16,48},{32,64},{48,80},{64,96},{80,112},{96,128},{112,144}... | collective-permute-start | bytes 1204232 | tf_op jit(solution)/shard_map/ppermute | solution.py:94
  61.2 22.5 %collective-permute-start.20 = (bf16[1,224,896]{2,1,0:T(8,128)(2,1)}, bf16[1,224,896]{2,1,0:T(8,128)(2,1)S(1)}, u32[]{:S(2)}, u32[]{:S(2)}) collective-permute-start(bf16[1,224,896]{2,1,0:T(8,128)(2,1)} %collective-permute-done.15), channel_id=1, source_target_pairs={{0,16},{16,0},{32,48},{48,32},{64,80},{80,64},{96,112},{112,96},{1... | collective-permute-start | bytes 1204232 | tf_op jit(solution)/shard_map/ppermute | solution.py:94
  65.3 40.7 %collective-permute-start.3 = (bf16[2,224,896]{2,1,0:T(8,128)(2,1)S(1)}, bf16[2,224,896]{2,1,0:T(8,128)(2,1)S(1)}, u32[]{:S(2)}, u32[]{:S(2)}) collective-permute-start(bf16[2,224,896]{2,1,0:T(8,128)(2,1)S(1)} %collective-permute-done), channel_id=1, source_target_pairs={{0,32},{16,48},{32,64},{48,80},{64,96},{80,112},{96,128},{112,144}... | collective-permute-start | bytes 2408456 | tf_op jit(solution)/shard_map/ppermute | solution.py:94
  68.7 28.0 %collective-permute-start.22 = (bf16[1,224,896]{2,1,0:T(8,128)(2,1)S(1)}, bf16[1,224,896]{2,1,0:T(8,128)(2,1)S(1)}, u32[]{:S(2)}, u32[]{:S(2)}) collective-permute-start(bf16[1,224,896]{2,1,0:T(8,128)(2,1)S(1)} %collective-permute-done.19), channel_id=1, source_target_pairs={{0,224},{16,240},{32,0},{48,16},{64,32},{80,48},{96,64},{112,80},{... | collective-permute-start | bytes 1204232 | tf_op jit(solution)/shard_map/ppermute | solution.py:94
  75.1 21.9 %collective-permute-start.23 = (bf16[1,224,896]{2,1,0:T(8,128)(2,1)S(1)}, bf16[1,224,896]{2,1,0:T(8,128)(2,1)S(1)}, u32[]{:S(2)}, u32[]{:S(2)}) collective-permute-start(bf16[1,224,896]{2,1,0:T(8,128)(2,1)S(1)} %collective-permute-done.19), channel_id=1, source_target_pairs={{0,16},{16,0},{32,48},{48,32},{64,80},{80,64},{96,112},{112,96},{1... | collective-permute-start | bytes 1204232 | tf_op jit(solution)/shard_map/ppermute | solution.py:94
  78.3 13.6 %collective-permute-start.21 = (bf16[1,224,896]{2,1,0:T(8,128)(2,1)S(1)}, bf16[1,224,896]{2,1,0:T(8,128)(2,1)S(1)}, u32[]{:S(2)}, u32[]{:S(2)}) collective-permute-start(bf16[1,224,896]{2,1,0:T(8,128)(2,1)S(1)} %collective-permute-done.18), channel_id=1, source_target_pairs={{0,32},{16,48},{32,64},{48,80},{64,96},{80,112},{96,128},{112,144}... | collective-permute-start | bytes 1204232 | tf_op jit(solution)/shard_map/ppermute | solution.py:94
  83.7 23.7 %collective-permute-start.4 = (bf16[2,224,896]{2,1,0:T(8,128)(2,1)S(1)}, bf16[2,224,896]{2,1,0:T(8,128)(2,1)S(1)}, u32[]{:S(2)}, u32[]{:S(2)}) collective-permute-start(bf16[2,224,896]{2,1,0:T(8,128)(2,1)S(1)} %collective-permute-done.1), channel_id=1, source_target_pairs={{0,224},{16,240},{32,0},{48,16},{64,32},{80,48},{96,64},{112,80},{... | collective-permute-start | bytes 2408456 | tf_op jit(solution)/shard_map/ppermute | solution.py:94
  92.0 13.7 %collective-permute-start.26 = (bf16[1,224,896]{2,1,0:T(8,128)(2,1)S(1)}, bf16[1,224,896]{2,1,0:T(8,128)(2,1)S(1)}, u32[]{:S(2)}, u32[]{:S(2)}) collective-permute-start(bf16[1,224,896]{2,1,0:T(8,128)(2,1)S(1)} %collective-permute-done.18), channel_id=1, source_target_pairs={{0,16},{16,0},{32,48},{48,32},{64,80},{80,64},{96,112},{112,96},{1... | collective-permute-start | bytes 1204232 | tf_op jit(solution)/shard_map/ppermute | solution.py:94
  96.7 26.3 %collective-permute-start.5 = (bf16[2,224,896]{2,1,0:T(8,128)(2,1)S(1)}, bf16[2,224,896]{2,1,0:T(8,128)(2,1)S(1)}, u32[]{:S(2)}, u32[]{:S(2)}) collective-permute-start(bf16[2,224,896]{2,1,0:T(8,128)(2,1)S(1)} %collective-permute-done), channel_id=1, source_target_pairs={{0,16},{16,0},{32,48},{48,32},{64,80},{80,64},{96,112},{112,96},{1... | collective-permute-start | bytes 2408456 | tf_op jit(solution)/shard_map/ppermute | solution.py:94
  97.1 12.9 %collective-permute-start.25 = (bf16[1,224,896]{2,1,0:T(8,128)(2,1)S(1)}, bf16[1,224,896]{2,1,0:T(8,128)(2,1)S(1)}, u32[]{:S(2)}, u32[]{:S(2)}) collective-permute-start(bf16[1,224,896]{2,1,0:T(8,128)(2,1)S(1)} %collective-permute-done.23), channel_id=1, source_target_pairs={{0,224},{16,240},{32,0},{48,16},{64,32},{80,48},{96,64},{112,80},{... | collective-permute-start | bytes 1204232 | tf_op jit(solution)/shard_map/ppermute | solution.py:94
  105.6 13.4 %collective-permute-start.24 = (bf16[1,224,896]{2,1,0:T(8,128)(2,1)S(1)}, bf16[1,224,896]{2,1,0:T(8,128)(2,1)S(1)}, u32[]{:S(2)}, u32[]{:S(2)}) collective-permute-start(bf16[1,224,896]{2,1,0:T(8,128)(2,1)S(1)} %collective-permute-done.21), channel_id=1, source_target_pairs={{0,32},{16,48},{32,64},{48,80},{64,96},{80,112},{96,128},{112,144}... | collective-permute-start | bytes 1204232 | tf_op jit(solution)/shard_map/ppermute | solution.py:94
  106.1 21.5 %collective-permute-start.27 = (bf16[1,224,896]{2,1,0:T(8,128)(2,1)S(1)}, bf16[1,224,896]{2,1,0:T(8,128)(2,1)S(1)}, u32[]{:S(2)}, u32[]{:S(2)}) collective-permute-start(bf16[1,224,896]{2,1,0:T(8,128)(2,1)S(1)} %collective-permute-done.26), channel_id=1, source_target_pairs={{0,32},{16,48},{32,64},{48,80},{64,96},{80,112},{96,128},{112,144}... | collective-permute-start | bytes 1204232 | tf_op jit(solution)/shard_map/ppermute | solution.py:94
  107.4 58.6 %collective-permute-start.6 = (bf16[2,224,896]{2,1,0:T(8,128)(2,1)S(1)}, bf16[2,224,896]{2,1,0:T(8,128)(2,1)S(1)}, u32[]{:S(2)}, u32[]{:S(2)}) collective-permute-start(bf16[2,224,896]{2,1,0:T(8,128)(2,1)S(1)} %collective-permute-done.3), channel_id=1, source_target_pairs={{0,32},{16,48},{32,64},{48,80},{64,96},{80,112},{96,128},{112,144}... | collective-permute-start | bytes 2408456 | tf_op jit(solution)/shard_map/ppermute | solution.py:94
  109.9 18.2 %collective-permute-start.28 = (bf16[1,224,896]{2,1,0:T(8,128)(2,1)S(1)}, bf16[1,224,896]{2,1,0:T(8,128)(2,1)S(1)}, u32[]{:S(2)}, u32[]{:S(2)}) collective-permute-start(bf16[1,224,896]{2,1,0:T(8,128)(2,1)S(1)} %collective-permute-done.25), channel_id=1, source_target_pairs={{0,224},{16,240},{32,0},{48,16},{64,32},{80,48},{96,64},{112,80},{... | collective-permute-start | bytes 1204232 | tf_op jit(solution)/shard_map/ppermute | solution.py:94
  119.0 47.1 %collective-permute-start.8 = (bf16[2,224,896]{2,1,0:T(8,128)(2,1)S(1)}, bf16[2,224,896]{2,1,0:T(8,128)(2,1)S(1)}, u32[]{:S(2)}, u32[]{:S(2)}) collective-permute-start(bf16[2,224,896]{2,1,0:T(8,128)(2,1)S(1)} %collective-permute-done.4), channel_id=1, source_target_pairs={{0,16},{16,0},{32,48},{48,32},{64,80},{80,64},{96,112},{112,96},{1... | collective-permute-start | bytes 2408456 | tf_op jit(solution)/shard_map/ppermute | solution.py:94
  123.0 47.1 %collective-permute-start.11 = (bf16[2,224,896]{2,1,0:T(8,128)(2,1)S(1)}, bf16[2,224,896]{2,1,0:T(8,128)(2,1)S(1)}, u32[]{:S(2)}, u32[]{:S(2)}) collective-permute-start(bf16[2,224,896]{2,1,0:T(8,128)(2,1)S(1)} %collective-permute-done.3), channel_id=1, source_target_pairs={{0,16},{16,0},{32,48},{48,32},{64,80},{80,64},{96,112},{112,96},{1... | collective-permute-start | bytes 2408456 | tf_op jit(solution)/shard_map/ppermute | solution.py:94
  127.6 35.3 %collective-permute-start.29 = (bf16[1,224,896]{2,1,0:T(8,128)(2,1)S(1)}, bf16[1,224,896]{2,1,0:T(8,128)(2,1)S(1)}, u32[]{:S(2)}, u32[]{:S(2)}) collective-permute-start(bf16[1,224,896]{2,1,0:T(8,128)(2,1)S(1)} %collective-permute-done.16), channel_id=1, source_target_pairs={{0,16},{16,0},{32,48},{48,32},{64,80},{80,64},{96,112},{112,96},{1... | collective-permute-start | bytes 1204232 | tf_op jit(solution)/shard_map/ppermute | solution.py:94
  128.1 43.0 %collective-permute-start.7 = (bf16[2,224,896]{2,1,0:T(8,128)(2,1)S(1)}, bf16[2,224,896]{2,1,0:T(8,128)(2,1)S(1)}, u32[]{:S(2)}, u32[]{:S(2)}) collective-permute-start(bf16[2,224,896]{2,1,0:T(8,128)(2,1)S(1)} %collective-permute-done.4), channel_id=1, source_target_pairs={{0,224},{16,240},{32,0},{48,16},{64,32},{80,48},{96,64},{112,80},{... | collective-permute-start | bytes 2408456 | tf_op jit(solution)/shard_map/ppermute | solution.py:94
  162.9 38.6 %collective-permute-start.14 = (bf16[2,224,896]{2,1,0:T(8,128)(2,1)S(1)}, bf16[2,224,896]{2,1,0:T(8,128)(2,1)S(1)}, u32[]{:S(2)}, u32[]{:S(2)}) collective-permute-start(bf16[2,224,896]{2,1,0:T(8,128)(2,1)S(1)} %collective-permute-done.1), channel_id=1, source_target_pairs={{0,16},{16,0},{32,48},{48,32},{64,80},{80,64},{96,112},{112,96},{1... | collective-permute-start | bytes 2408456 | tf_op jit(solution)/shard_map/ppermute | solution.py:94
  166.1 24.8 %collective-permute-start.9 = (bf16[2,224,896]{2,1,0:T(8,128)(2,1)S(1)}, bf16[2,224,896]{2,1,0:T(8,128)(2,1)S(1)}, u32[]{:S(2)}, u32[]{:S(2)}) collective-permute-start(bf16[2,224,896]{2,1,0:T(8,128)(2,1)S(1)} %collective-permute-done.6), channel_id=1, source_target_pairs={{0,32},{16,48},{32,64},{48,80},{64,96},{80,112},{96,128},{112,144}... | collective-permute-start | bytes 2408456 | tf_op jit(solution)/shard_map/ppermute | solution.py:94
  166.1 21.1 %collective-permute-start.10 = (bf16[2,224,896]{2,1,0:T(8,128)(2,1)S(1)}, bf16[2,224,896]{2,1,0:T(8,128)(2,1)S(1)}, u32[]{:S(2)}, u32[]{:S(2)}) collective-permute-start(bf16[2,224,896]{2,1,0:T(8,128)(2,1)S(1)} %collective-permute-done.8), channel_id=1, source_target_pairs={{0,224},{16,240},{32,0},{48,16},{64,32},{80,48},{96,64},{112,80},{... | collective-permute-start | bytes 2408456 | tf_op jit(solution)/shard_map/ppermute | solution.py:94
  170.1 23.6 %collective-permute-start.12 = (bf16[2,224,896]{2,1,0:T(8,128)(2,1)S(1)}, bf16[2,224,896]{2,1,0:T(8,128)(2,1)S(1)}, u32[]{:S(2)}, u32[]{:S(2)}) collective-permute-start(bf16[2,224,896]{2,1,0:T(8,128)(2,1)S(1)} %collective-permute-done.11), channel_id=1, source_target_pairs={{0,32},{16,48},{32,64},{48,80},{64,96},{80,112},{96,128},{112,144}... | collective-permute-start | bytes 2408456 | tf_op jit(solution)/shard_map/ppermute | solution.py:94
  187.2 13.4 %collective-permute-start.13 = (bf16[2,224,896]{2,1,0:T(8,128)(2,1)S(1)}, bf16[2,224,896]{2,1,0:T(8,128)(2,1)S(1)}, u32[]{:S(2)}, u32[]{:S(2)}) collective-permute-start(bf16[2,224,896]{2,1,0:T(8,128)(2,1)S(1)} %collective-permute-done.10), channel_id=1, source_target_pairs={{0,224},{16,240},{32,0},{48,16},{64,32},{80,48},{96,64},{112,80},{... | collective-permute-start | bytes 2408456 | tf_op jit(solution)/shard_map/ppermute | solution.py:94
  (7 other events, 30.8 us)

commit v2 on v1

--- a/solution.py
+++ b/solution.py
@@ -42,18 +42,19 @@
 
 
 STAGES = (
-    ("fsdp", 8),
+    ("cols", 8),
     ("cols", 1),
     ("cols", 2),
     ("cols", 4),
-    ("cols", 8),
     ("fsdp", 1),
     ("fsdp", 2),
     ("fsdp", 4),
+    ("fsdp", 8),
 )
 
 
-def gather_norm(own):
+def gather_norm(norm_train, norm_step):
+    own = (norm_train + norm_step).astype(jnp.bfloat16)
     at = lax.axis_index("fsdp") * 16 + lax.axis_index("cols")
     total = lax.dynamic_update_slice(
         jnp.zeros((3584,), own.dtype), own, (at.astype(jnp.uint32) * 14,)
@@ -81,28 +82,40 @@
     def slot(place):
         return (((me >> 1) + (Z - place[0])) & 7) * 2 + ((me & 1) ^ place[1])
 
-    serve_norm = gather_norm((norm_train + norm_step).astype(jnp.bfloat16))
-    own_down = merged(train_down.T, high_down.T, low_down.T)
-    own_gate = merged(train_gate, low_gate, high_gate)
-    own_up = merged(train_up, low_up, high_up)
-    own = (jnp.stack([own_down, own_gate]), own_up[None])
-    own = lax.optimization_barrier(own)
+    serve_norm = gather_norm(norm_train, norm_step)
+    own_down = merged(train_down.T, high_down.T, low_down.T)[None]
+    own_rest = jnp.stack(
+        [
+            merged(train_gate, low_gate, high_gate),
+            merged(train_up, low_up, high_up),
+        ]
+    )
+    own = tuple(map(lax.optimization_barrier, (own_down, own_rest)))
+    zero = jnp.uint32(0)
+    down, gate, up = (empty() for _ in range(3))
+
+    def put(stack, piece, place):
+        return lax.dynamic_update_slice(stack, piece, (slot(place), zero, zero))
+
+    down = put(down, own[0], (0, 0))
+    gate = put(gate, own[1][:1], (0, 0))
+    up = put(up, own[1][1:], (0, 0))
     held = [{(0, 0): piece} for piece in own]
-    for senders in ROUNDS:
-        for k in range(len(own)):
+    for number, senders in enumerate(ROUNDS):
+        for k in range(2):
             for direction, place in enumerate(senders):
                 got = lax.ppermute(held[k][place], "fsdp", HOPS[direction])
-                held[k][reached(direction, place)] = got
-    zero = jnp.uint32(0)
-    stacks = [empty() for _ in range(3)]
-    for place in held[0]:
-        parts = (held[0][place][:1], held[0][place][1:], held[1][place])
-        for i, part in enumerate(parts):
-            stacks[i] = lax.dynamic_update_slice(
-                stacks[i], part, (slot(place), zero, zero)
-            )
-    down, gate, up = (stack.reshape(3584, COLS) for stack in stacks)
-    return gate, up, down.T, serve_norm
+                there = reached(direction, place)
+                held[k][there] = got
+                if k == 0:
+                    down = put(down, got, there)
+                else:
+                    gate = put(gate, got[:1], there)
+                    up = put(up, got[1:], there)
+            if (number, k) == (4, 0):
+                down = down.reshape(3584, COLS).T
+                gate, up, down = lax.optimization_barrier((gate, up, down))
+    return gate.reshape(3584, COLS), up.reshape(3584, COLS), down, serve_norm
 
 
 def empty():

time: 212 us -> 211 us (level)
  the two profiles are of different devices: /device:TPU:6 before, /device:TPU:8 now
where the time goes in v2:
time: 211 us
  starting transfers between devices  80.7 us (38%)
  waiting for transfers between devices  76.3 us (36%)
  local copies, waits for them, and re-layouts  47.6 us (23%)
  matrix products  3.98 us (2%)
    ppermute x30, starting transfers between devices, per_device(): got = lax.ppermute(held[k][place], 'fsdp', HOPS[direction])  62.7 us
    ppermute x30, waiting for transfers between devices, per_device(): got = lax.ppermute(held[k][place], 'fsdp', HOPS[direction])  56.3 us
    dynamic_update_slice x32, local copies, waits for them, and re-layouts, put(): return lax.dynamic_update_slice(stack, piece, (slot(place), zero, zero))  37.6 us
    ppermute x8, waiting for transfers between devices, exchange(): got = lax.ppermute(total, name, [(i, i ^ bit) for i in range(16)])  20 us
    ppermute x8, starting transfers between devices, exchange(): got = lax.ppermute(total, name, [(i, i ^ bit) for i in range(16)])  18.1 us
    reshape x1, local copies, waits for them, and re-layouts, per_device(): down = down.reshape(3584, COLS).T  9.52 us
  transfers between devices with their start and end apart: 38, of which 16 were waited for; matrix products, arithmetic and copies ran while one was open for 24% of the time, Pallas kernels for 0%

profile of v2, /device:TPU:8, one launch (start us, length us, event | category | flops | bytes accessed | tf_op | source)
XLA Modules:
  0.0 210.8 jit_solution(2504285993816252261)
XLA Ops:
  1.5 2.2 %collective-permute-start.30 = (bf16[3584]{0:T(1024)(128)(2,1)S(1)}, bf16[3584]{0:T(1024)(128)(2,1)S(1)}, u32[]{:S(2)}, u32[]{:S(2)}) collective-permute-start(bf16[3584]{0:T(1024)(128)(2,1)S(1)} %dynamic_update_slice.197), channel_id=1, source_target_pairs={{0,8},{1,9},{2,10},{3,11},{4,12},{5,13},{6,14},{7,15},{8,0},{9,1},... | collective-permute-start | bytes 21512 | tf_op jit(solution)/shard_map/ppermute | solution.py:40
  10.8 2.9 %collective-permute-start.33 = (bf16[3584]{0:T(1024)(128)(2,1)S(1)}, bf16[3584]{0:T(1024)(128)(2,1)S(1)}, u32[]{:S(2)}, u32[]{:S(2)}) collective-permute-start(bf16[3584]{0:T(1024)(128)(2,1)S(1)} %add.218), channel_id=1, source_target_pairs={{0,4},{1,5},{2,6},{3,7},{4,0},{5,1},{6,2},{7,3},{8,12},{9,13},{10,... | collective-permute-start | bytes 21512 | tf_op jit(solution)/shard_map/ppermute | solution.py:40
  16.0 2.2 %collective-permute-start.34 = (bf16[3584]{0:T(1024)(128)(2,1)S(1)}, bf16[3584]{0:T(1024)(128)(2,1)S(1)}, u32[]{:S(2)}, u32[]{:S(2)}) collective-permute-start(bf16[3584]{0:T(1024)(128)(2,1)S(1)} %add.219), channel_id=1, source_target_pairs={{0,16},{16,0},{32,48},{48,32},{64,80},{80,64},{96,112},{112,96},{1... | collective-permute-start | bytes 21512 | tf_op jit(solution)/shard_map/ppermute | solution.py:40
  21.5 4.0 %collective-permute-start.13 = (bf16[1,224,896]{2,1,0:T(8,128)(2,1)S(1)}, bf16[1,224,896]{2,1,0:T(8,128)(2,1)S(1)}, u32[]{:S(2)}, u32[]{:S(2)}) collective-permute-start(bf16[1,224,896]{2,1,0:T(8,128)(2,1)S(1)} %fusion.3), channel_id=1, source_target_pairs={{0,224},{16,240},{32,0},{48,16},{64,32},{80,48},{96,64},{112,80},{... | collective-permute-start | bytes 1204232 | tf_op jit(solution)/shard_map/ppermute | solution.py:107
  25.5 15.4 %collective-permute-done.35 = bf16[3584]{0:T(1024)(128)(2,1)S(1)} collective-permute-done((bf16[3584]{0:T(1024)(128)(2,1)S(1)}, bf16[3584]{0:T(1024)(128)(2,1)S(1)}, u32[]{:S(2)}, u32[]{:S(2)}) %collective-permute-start.35) | collective-permute-done | bytes 7200 | tf_op jit(solution)/shard_map/ppermute | solution.py:40
  40.9 3.3 %collective-permute-start.36 = (bf16[3584]{0:T(1024)(128)(2,1)S(1)}, bf16[3584]{0:T(1024)(128)(2,1)S(1)}, u32[]{:S(2)}, u32[]{:S(2)}) collective-permute-start(bf16[3584]{0:T(1024)(128)(2,1)S(1)} %add.221), channel_id=1, source_target_pairs={{0,64},{16,80},{32,96},{48,112},{64,0},{80,16},{96,32},{112,48},{1... | collective-permute-start | bytes 21512 | tf_op jit(solution)/shard_map/ppermute | solution.py:40
  45.8 6.1 %collective-permute-start.37 = (bf16[3584]{0:T(1024)(128)(2,1)S(1)}, bf16[3584]{0:T(1024)(128)(2,1)S(1)}, u32[]{:S(2)}, u32[]{:S(2)}) collective-permute-start(bf16[3584]{0:T(1024)(128)(2,1)S(1)} %add.222), channel_id=1, source_target_pairs={{0,128},{16,144},{32,160},{48,176},{64,192},{80,208},{96,224},{112... | collective-permute-start | bytes 21512 | tf_op jit(solution)/shard_map/ppermute | solution.py:40
  53.5 2.3 %collective-permute-start.14 = (bf16[1,224,896]{2,1,0:T(8,128)(2,1)S(1)}, bf16[1,224,896]{2,1,0:T(8,128)(2,1)}, u32[]{:S(2)}, u32[]{:S(2)}) collective-permute-start(bf16[1,224,896]{2,1,0:T(8,128)(2,1)S(1)} %fusion.3), channel_id=1, source_target_pairs={{0,16},{16,0},{32,48},{48,32},{64,80},{80,64},{96,112},{112,96},{1... | collective-permute-start | bytes 1204232 | tf_op jit(solution)/shard_map/ppermute | solution.py:107
  59.4 6.0 %collective-permute-start.16 = (bf16[1,224,896]{2,1,0:T(8,128)(2,1)S(1)}, bf16[1,224,896]{2,1,0:T(8,128)(2,1)S(1)}, u32[]{:S(2)}, u32[]{:S(2)}) collective-permute-start(bf16[1,224,896]{2,1,0:T(8,128)(2,1)S(1)} %collective-permute-done.13), channel_id=1, source_target_pairs={{0,224},{16,240},{32,0},{48,16},{64,32},{80,48},{96,64},{112,80},{... | collective-permute-start | bytes 1204232 | tf_op jit(solution)/shard_map/ppermute | solution.py:107
  71.7 2.3 %collective-permute-start.17 = (bf16[1,224,896]{2,1,0:T(8,128)(2,1)}, bf16[1,224,896]{2,1,0:T(8,128)(2,1)S(1)}, u32[]{:S(2)}, u32[]{:S(2)}) collective-permute-start(bf16[1,224,896]{2,1,0:T(8,128)(2,1)} %collective-permute-done.12), channel_id=1, source_target_pairs={{0,16},{16,0},{32,48},{48,32},{64,80},{80,64},{96,112},{112,96},{1... | collective-permute-start | bytes 1204232 | tf_op jit(solution)/shard_map/ppermute | solution.py:107
  75.7 3.7 %collective-permute-done.16 = bf16[1,224,896]{2,1,0:T(8,128)(2,1)S(1)} collective-permute-done((bf16[1,224,896]{2,1,0:T(8,128)(2,1)S(1)}, bf16[1,224,896]{2,1,0:T(8,128)(2,1)S(1)}, u32[]{:S(2)}, u32[]{:S(2)}) %collective-permute-start.16) | collective-permute-done | bytes 401440 | tf_op jit(solution)/shard_map/ppermute | solution.py:107
  81.1 3.2 %collective-permute-done.2 = bf16[2,224,896]{2,1,0:T(8,128)(2,1)S(1)} collective-permute-done((bf16[2,224,896]{2,1,0:T(8,128)(2,1)S(1)}, bf16[2,224,896]{2,1,0:T(8,128)(2,1)S(1)}, u32[]{:S(2)}, u32[]{:S(2)}) %collective-permute-start.2) | collective-permute-done | bytes 802848 | tf_op jit(solution)/shard_map/ppermute | solution.py:107
  84.4 2.3 %collective-permute-start.20 = (bf16[1,224,896]{2,1,0:T(8,128)(2,1)S(1)}, bf16[1,224,896]{2,1,0:T(8,128)(2,1)S(1)}, u32[]{:S(2)}, u32[]{:S(2)}) collective-permute-start(bf16[1,224,896]{2,1,0:T(8,128)(2,1)S(1)} %collective-permute-done.16), channel_id=1, source_target_pairs={{0,16},{16,0},{32,48},{48,32},{64,80},{80,64},{96,112},{112,96},{1... | collective-permute-start | bytes 1204232 | tf_op jit(solution)/shard_map/ppermute | solution.py:107
  86.7 2.7 %collective-permute-start.18 = (bf16[1,224,896]{2,1,0:T(8,128)(2,1)S(1)}, bf16[1,224,896]{2,1,0:T(8,128)(2,1)S(1)}, u32[]{:S(2)}, u32[]{:S(2)}) collective-permute-start(bf16[1,224,896]{2,1,0:T(8,128)(2,1)S(1)} %collective-permute-done.15), channel_id=1, source_target_pairs={{0,32},{16,48},{32,64},{48,80},{64,96},{80,112},{96,128},{112,144}... | collective-permute-start | bytes 1204232 | tf_op jit(solution)/shard_map/ppermute | solution.py:107
  92.9 5.6 %collective-permute-start.4 = (bf16[2,224,896]{2,1,0:T(8,128)(2,1)S(1)}, bf16[2,224,896]{2,1,0:T(8,128)(2,1)S(1)}, u32[]{:S(2)}, u32[]{:S(2)}) collective-permute-start(bf16[2,224,896]{2,1,0:T(8,128)(2,1)S(1)} %collective-permute-done.1), channel_id=1, source_target_pairs={{0,224},{16,240},{32,0},{48,16},{64,32},{80,48},{96,64},{112,80},{... | collective-permute-start | bytes 2408456 | tf_op jit(solution)/shard_map/ppermute | solution.py:107
  99.2 2.7 %collective-permute-done.18 = bf16[1,224,896]{2,1,0:T(8,128)(2,1)S(1)} collective-permute-done((bf16[1,224,896]{2,1,0:T(8,128)(2,1)S(1)}, bf16[1,224,896]{2,1,0:T(8,128)(2,1)S(1)}, u32[]{:S(2)}, u32[]{:S(2)}) %collective-permute-start.18) | collective-permute-done | bytes 401440 | tf_op jit(solution)/shard_map/ppermute | solution.py:107
  110.3 5.2 %collective-permute-done.23 = bf16[1,224,896]{2,1,0:T(8,128)(2,1)S(1)} collective-permute-done((bf16[1,224,896]{2,1,0:T(8,128)(2,1)S(1)}, bf16[1,224,896]{2,1,0:T(8,128)(2,1)S(1)}, u32[]{:S(2)}, u32[]{:S(2)}) %collective-permute-start.23) | collective-permute-done | bytes 401440 | tf_op jit(solution)/shard_map/ppermute | solution.py:107
  115.6 2.1 slice_dynamic-update-slice_fusion.14
  120.3 3.7 %collective-permute-start.25 = (bf16[1,224,896]{2,1,0:T(8,128)(2,1)S(1)}, bf16[1,224,896]{2,1,0:T(8,128)(2,1)S(1)}, u32[]{:S(2)}, u32[]{:S(2)}) collective-permute-start(bf16[1,224,896]{2,1,0:T(8,128)(2,1)S(1)} %collective-permute-done.22), channel_id=1, source_target_pairs={{0,224},{16,240},{32,0},{48,16},{64,32},{80,48},{96,64},{112,80},{... | collective-permute-start | bytes 1204232 | tf_op jit(solution)/shard_map/ppermute | solution.py:107
  124.9 4.0 %collective-permute-done.21 = bf16[1,224,896]{2,1,0:T(8,128)(2,1)S(1)} collective-permute-done((bf16[1,224,896]{2,1,0:T(8,128)(2,1)S(1)}, bf16[1,224,896]{2,1,0:T(8,128)(2,1)S(1)}, u32[]{:S(2)}, u32[]{:S(2)}) %collective-permute-start.21) | collective-permute-done | bytes 401440 | tf_op jit(solution)/shard_map/ppermute | solution.py:107
  131.7 2.2 %collective-permute-start.11 = (bf16[2,224,896]{2,1,0:T(8,128)(2,1)}, bf16[2,224,896]{2,1,0:T(8,128)(2,1)S(1)}, u32[]{:S(2)}, u32[]{:S(2)}) collective-permute-start(bf16[2,224,896]{2,1,0:T(8,128)(2,1)} %collective-permute-done.3), channel_id=1, source_target_pairs={{0,16},{16,0},{32,48},{48,32},{64,80},{80,64},{96,112},{112,96},{1... | collective-permute-start | bytes 2408456 | tf_op jit(solution)/shard_map/ppermute | solution.py:107
  136.8 2.8 %collective-permute-start.7 = (bf16[2,224,896]{2,1,0:T(8,128)(2,1)S(1)}, bf16[2,224,896]{2,1,0:T(8,128)(2,1)}, u32[]{:S(2)}, u32[]{:S(2)}) collective-permute-start(bf16[2,224,896]{2,1,0:T(8,128)(2,1)S(1)} %collective-permute-done.4), channel_id=1, source_target_pairs={{0,224},{16,240},{32,0},{48,16},{64,32},{80,48},{96,64},{112,80},{... | collective-permute-start | bytes 2408456 | tf_op jit(solution)/shard_map/ppermute | solution.py:107
  142.2 30.6 %collective-permute-done.26 = bf16[1,224,896]{2,1,0:T(8,128)(2,1)S(1)} collective-permute-done((bf16[1,224,896]{2,1,0:T(8,128)(2,1)S(1)}, bf16[1,224,896]{2,1,0:T(8,128)(2,1)S(1)}, u32[]{:S(2)}, u32[]{:S(2)}) %collective-permute-start.26) | collective-permute-done | bytes 401440 | tf_op jit(solution)/shard_map/ppermute | solution.py:107
  174.8 3.2 %collective-permute-start.10 = (bf16[2,224,896]{2,1,0:T(8,128)(2,1)}, bf16[2,224,896]{2,1,0:T(8,128)(2,1)}, u32[]{:S(2)}, u32[]{:S(2)}) collective-permute-start(bf16[2,224,896]{2,1,0:T(8,128)(2,1)} %collective-permute-done.8), channel_id=1, source_target_pairs={{0,224},{16,240},{32,0},{48,16},{64,32},{80,48},{96,64},{112,80},{... | collective-permute-start | bytes 2408456 | tf_op jit(solution)/shard_map/ppermute | solution.py:107
  178.8 9.5 %copy.15 = bf16[3584,896]{0,1:T(8,128)(2,1)} copy(bf16[3584,896]{1,0:T(8,128)(2,1)} %bitcast.18) | data formatting | bytes 12845056 | tf_op jit(solution)/shard_map/reshape | solution.py:116
  188.4 2.1 slice_dynamic-update-slice_fusion.11
  190.4 2.1 slice_dynamic-update-slice_fusion.10
  192.5 2.1 slice_dynamic-update-slice_fusion.9
  194.6 3.2 %collective-permute-start.28 = (bf16[2,224,896]{2,1,0:T(8,128)(2,1)}, bf16[2,224,896]{2,1,0:T(8,128)(2,1)S(1)}, u32[]{:S(2)}, u32[]{:S(2)}) collective-permute-start(bf16[2,224,896]{2,1,0:T(8,128)(2,1)} %collective-permute-done.10), channel_id=1, source_target_pairs={{0,224},{16,240},{32,0},{48,16},{64,32},{80,48},{96,64},{112,80},{... | collective-permute-start | bytes 2408456 | tf_op jit(solution)/shard_map/ppermute | solution.py:107
  197.8 2.1 slice_dynamic-update-slice_fusion.8
  202.9 2.7 %collective-permute-done.27 = bf16[2,224,896]{2,1,0:T(8,128)(2,1)S(1)} collective-permute-done((bf16[2,224,896]{2,1,0:T(8,128)(2,1)S(1)}, bf16[2,224,896]{2,1,0:T(8,128)(2,1)S(1)}, u32[]{:S(2)}, u32[]{:S(2)}) %collective-permute-start.27) | collective-permute-done | bytes 802848 | tf_op jit(solution)/shard_map/ppermute | solution.py:107
  208.8 2.1 slice_dynamic-update-slice_fusion
  (98 shorter events, 63.6 us)
Async XLA Ops:
  13.8 58.0 %collective-permute-start = (bf16[2,224,896]{2,1,0:T(8,128)(2,1)S(1)}, bf16[2,224,896]{2,1,0:T(8,128)(2,1)S(1)}, u32[]{:S(2)}, u32[]{:S(2)}) collective-permute-start(bf16[2,224,896]{2,1,0:T(8,128)(2,1)S(1)} %pad_maximum_fusion), channel_id=1, source_target_pairs={{0,32},{16,48},{32,64},{48,80},{64,96},{80,112},{96,128},{112,144}... | collective-permute-start | bytes 2408456 | tf_op jit(solution)/shard_map/ppermute | solution.py:107
  16.0 9.5 %collective-permute-start.34 = (bf16[3584]{0:T(1024)(128)(2,1)S(1)}, bf16[3584]{0:T(1024)(128)(2,1)S(1)}, u32[]{:S(2)}, u32[]{:S(2)}) collective-permute-start(bf16[3584]{0:T(1024)(128)(2,1)S(1)} %add.219), channel_id=1, source_target_pairs={{0,16},{16,0},{32,48},{48,32},{64,80},{80,64},{96,112},{112,96},{1... | collective-permute-start | bytes 21512 | tf_op jit(solution)/shard_map/ppermute | solution.py:40
  19.5 38.7 %collective-permute-start.12 = (bf16[1,224,896]{2,1,0:T(8,128)(2,1)S(1)}, bf16[1,224,896]{2,1,0:T(8,128)(2,1)}, u32[]{:S(2)}, u32[]{:S(2)}) collective-permute-start(bf16[1,224,896]{2,1,0:T(8,128)(2,1)S(1)} %fusion.3), channel_id=1, source_target_pairs={{0,32},{16,48},{32,64},{48,80},{64,96},{80,112},{96,128},{112,144}... | collective-permute-start | bytes 1204232 | tf_op jit(solution)/shard_map/ppermute | solution.py:107
  21.5 37.9 %collective-permute-start.13 = (bf16[1,224,896]{2,1,0:T(8,128)(2,1)S(1)}, bf16[1,224,896]{2,1,0:T(8,128)(2,1)S(1)}, u32[]{:S(2)}, u32[]{:S(2)}) collective-permute-start(bf16[1,224,896]{2,1,0:T(8,128)(2,1)S(1)} %fusion.3), channel_id=1, source_target_pairs={{0,224},{16,240},{32,0},{48,16},{64,32},{80,48},{96,64},{112,80},{... | collective-permute-start | bytes 1204232 | tf_op jit(solution)/shard_map/ppermute | solution.py:107
  25.5 15.4 %collective-permute-start.35 = (bf16[3584]{0:T(1024)(128)(2,1)S(1)}, bf16[3584]{0:T(1024)(128)(2,1)S(1)}, u32[]{:S(2)}, u32[]{:S(2)}) collective-permute-start(bf16[3584]{0:T(1024)(128)(2,1)S(1)} %add.220), channel_id=1, source_target_pairs={{0,32},{16,48},{32,0},{48,16},{64,96},{80,112},{96,64},{112,80},{1... | collective-permute-start | bytes 21512 | tf_op jit(solution)/shard_map/ppermute | solution.py:40
  51.9 23.1 %collective-permute-start.1 = (bf16[2,224,896]{2,1,0:T(8,128)(2,1)S(1)}, bf16[2,224,896]{2,1,0:T(8,128)(2,1)S(1)}, u32[]{:S(2)}, u32[]{:S(2)}) collective-permute-start(bf16[2,224,896]{2,1,0:T(8,128)(2,1)S(1)} %pad_maximum_fusion), channel_id=1, source_target_pairs={{0,224},{16,240},{32,0},{48,16},{64,32},{80,48},{96,64},{112,80},{... | collective-permute-start | bytes 2408456 | tf_op jit(solution)/shard_map/ppermute | solution.py:107
  53.5 14.5 %collective-permute-start.14 = (bf16[1,224,896]{2,1,0:T(8,128)(2,1)S(1)}, bf16[1,224,896]{2,1,0:T(8,128)(2,1)}, u32[]{:S(2)}, u32[]{:S(2)}) collective-permute-start(bf16[1,224,896]{2,1,0:T(8,128)(2,1)S(1)} %fusion.3), channel_id=1, source_target_pairs={{0,16},{16,0},{32,48},{48,32},{64,80},{80,64},{96,112},{112,96},{1... | collective-permute-start | bytes 1204232 | tf_op jit(solution)/shard_map/ppermute | solution.py:107
  58.2 26.2 %collective-permute-start.2 = (bf16[2,224,896]{2,1,0:T(8,128)(2,1)S(1)}, bf16[2,224,896]{2,1,0:T(8,128)(2,1)S(1)}, u32[]{:S(2)}, u32[]{:S(2)}) collective-permute-start(bf16[2,224,896]{2,1,0:T(8,128)(2,1)S(1)} %pad_maximum_fusion), channel_id=1, source_target_pairs={{0,16},{16,0},{32,48},{48,32},{64,80},{80,64},{96,112},{112,96},{1... | collective-permute-start | bytes 2408456 | tf_op jit(solution)/shard_map/ppermute | solution.py:107
  59.4 20.0 %collective-permute-start.16 = (bf16[1,224,896]{2,1,0:T(8,128)(2,1)S(1)}, bf16[1,224,896]{2,1,0:T(8,128)(2,1)S(1)}, u32[]{:S(2)}, u32[]{:S(2)}) collective-permute-start(bf16[1,224,896]{2,1,0:T(8,128)(2,1)S(1)} %collective-permute-done.13), channel_id=1, source_target_pairs={{0,224},{16,240},{32,0},{48,16},{64,32},{80,48},{96,64},{112,80},{... | collective-permute-start | bytes 1204232 | tf_op jit(solution)/shard_map/ppermute | solution.py:107
  68.0 18.6 %collective-permute-start.15 = (bf16[1,224,896]{2,1,0:T(8,128)(2,1)}, bf16[1,224,896]{2,1,0:T(8,128)(2,1)S(1)}, u32[]{:S(2)}, u32[]{:S(2)}) collective-permute-start(bf16[1,224,896]{2,1,0:T(8,128)(2,1)} %collective-permute-done.12), channel_id=1, source_target_pairs={{0,32},{16,48},{32,64},{48,80},{64,96},{80,112},{96,128},{112,144}... | collective-permute-start | bytes 1204232 | tf_op jit(solution)/shard_map/ppermute | solution.py:107
  71.7 21.1 %collective-permute-start.17 = (bf16[1,224,896]{2,1,0:T(8,128)(2,1)}, bf16[1,224,896]{2,1,0:T(8,128)(2,1)S(1)}, u32[]{:S(2)}, u32[]{:S(2)}) collective-permute-start(bf16[1,224,896]{2,1,0:T(8,128)(2,1)} %collective-permute-done.12), channel_id=1, source_target_pairs={{0,16},{16,0},{32,48},{48,32},{64,80},{80,64},{96,112},{112,96},{1... | collective-permute-start | bytes 1204232 | tf_op jit(solution)/shard_map/ppermute | solution.py:107
  75.0 40.6 %collective-permute-start.3 = (bf16[2,224,896]{2,1,0:T(8,128)(2,1)S(1)}, bf16[2,224,896]{2,1,0:T(8,128)(2,1)}, u32[]{:S(2)}, u32[]{:S(2)}) collective-permute-start(bf16[2,224,896]{2,1,0:T(8,128)(2,1)S(1)} %collective-permute-done), channel_id=1, source_target_pairs={{0,32},{16,48},{32,64},{48,80},{64,96},{80,112},{96,128},{112,144}... | collective-permute-start | bytes 2408456 | tf_op jit(solution)/shard_map/ppermute | solution.py:107
  79.4 26.1 %collective-permute-start.19 = (bf16[1,224,896]{2,1,0:T(8,128)(2,1)S(1)}, bf16[1,224,896]{2,1,0:T(8,128)(2,1)S(1)}, u32[]{:S(2)}, u32[]{:S(2)}) collective-permute-start(bf16[1,224,896]{2,1,0:T(8,128)(2,1)S(1)} %collective-permute-done.16), channel_id=1, source_target_pairs={{0,224},{16,240},{32,0},{48,16},{64,32},{80,48},{96,64},{112,80},{... | collective-permute-start | bytes 1204232 | tf_op jit(solution)/shard_map/ppermute | solution.py:107
  84.4 22.6 %collective-permute-start.20 = (bf16[1,224,896]{2,1,0:T(8,128)(2,1)S(1)}, bf16[1,224,896]{2,1,0:T(8,128)(2,1)S(1)}, u32[]{:S(2)}, u32[]{:S(2)}) collective-permute-start(bf16[1,224,896]{2,1,0:T(8,128)(2,1)S(1)} %collective-permute-done.16), channel_id=1, source_target_pairs={{0,16},{16,0},{32,48},{48,32},{64,80},{80,64},{96,112},{112,96},{1... | collective-permute-start | bytes 1204232 | tf_op jit(solution)/shard_map/ppermute | solution.py:107
  86.7 15.2 %collective-permute-start.18 = (bf16[1,224,896]{2,1,0:T(8,128)(2,1)S(1)}, bf16[1,224,896]{2,1,0:T(8,128)(2,1)S(1)}, u32[]{:S(2)}, u32[]{:S(2)}) collective-permute-start(bf16[1,224,896]{2,1,0:T(8,128)(2,1)S(1)} %collective-permute-done.15), channel_id=1, source_target_pairs={{0,32},{16,48},{32,64},{48,80},{64,96},{80,112},{96,128},{112,144}... | collective-permute-start | bytes 1204232 | tf_op jit(solution)/shard_map/ppermute | solution.py:107
  92.9 24.8 %collective-permute-start.4 = (bf16[2,224,896]{2,1,0:T(8,128)(2,1)S(1)}, bf16[2,224,896]{2,1,0:T(8,128)(2,1)S(1)}, u32[]{:S(2)}, u32[]{:S(2)}) collective-permute-start(bf16[2,224,896]{2,1,0:T(8,128)(2,1)S(1)} %collective-permute-done.1), channel_id=1, source_target_pairs={{0,224},{16,240},{32,0},{48,16},{64,32},{80,48},{96,64},{112,80},{... | collective-permute-start | bytes 2408456 | tf_op jit(solution)/shard_map/ppermute | solution.py:107
  101.9 13.7 %collective-permute-start.23 = (bf16[1,224,896]{2,1,0:T(8,128)(2,1)S(1)}, bf16[1,224,896]{2,1,0:T(8,128)(2,1)S(1)}, u32[]{:S(2)}, u32[]{:S(2)}) collective-permute-start(bf16[1,224,896]{2,1,0:T(8,128)(2,1)S(1)} %collective-permute-done.15), channel_id=1, source_target_pairs={{0,16},{16,0},{32,48},{48,32},{64,80},{80,64},{96,112},{112,96},{1... | collective-permute-start | bytes 1204232 | tf_op jit(solution)/shard_map/ppermute | solution.py:107
  105.5 26.2 %collective-permute-start.5 = (bf16[2,224,896]{2,1,0:T(8,128)(2,1)S(1)}, bf16[2,224,896]{2,1,0:T(8,128)(2,1)S(1)}, u32[]{:S(2)}, u32[]{:S(2)}) collective-permute-start(bf16[2,224,896]{2,1,0:T(8,128)(2,1)S(1)} %collective-permute-done), channel_id=1, source_target_pairs={{0,16},{16,0},{32,48},{48,32},{64,80},{80,64},{96,112},{112,96},{1... | collective-permute-start | bytes 2408456 | tf_op jit(solution)/shard_map/ppermute | solution.py:107
  107.0 13.2 %collective-permute-start.22 = (bf16[1,224,896]{2,1,0:T(8,128)(2,1)S(1)}, bf16[1,224,896]{2,1,0:T(8,128)(2,1)S(1)}, u32[]{:S(2)}, u32[]{:S(2)}) collective-permute-start(bf16[1,224,896]{2,1,0:T(8,128)(2,1)S(1)} %collective-permute-done.20), channel_id=1, source_target_pairs={{0,224},{16,240},{32,0},{48,16},{64,32},{80,48},{96,64},{112,80},{... | collective-permute-start | bytes 1204232 | tf_op jit(solution)/shard_map/ppermute | solution.py:107
  115.6 13.4 %collective-permute-start.21 = (bf16[1,224,896]{2,1,0:T(8,128)(2,1)S(1)}, bf16[1,224,896]{2,1,0:T(8,128)(2,1)S(1)}, u32[]{:S(2)}, u32[]{:S(2)}) collective-permute-start(bf16[1,224,896]{2,1,0:T(8,128)(2,1)S(1)} %collective-permute-done.18), channel_id=1, source_target_pairs={{0,32},{16,48},{32,64},{48,80},{64,96},{80,112},{96,128},{112,144}... | collective-permute-start | bytes 1204232 | tf_op jit(solution)/shard_map/ppermute | solution.py:107
  115.6 19.9 %collective-permute-start.24 = (bf16[1,224,896]{2,1,0:T(8,128)(2,1)S(1)}, bf16[1,224,896]{2,1,0:T(8,128)(2,1)S(1)}, u32[]{:S(2)}, u32[]{:S(2)}) collective-permute-start(bf16[1,224,896]{2,1,0:T(8,128)(2,1)S(1)} %collective-permute-done.23), channel_id=1, source_target_pairs={{0,32},{16,48},{32,64},{48,80},{64,96},{80,112},{96,128},{112,144}... | collective-permute-start | bytes 1204232 | tf_op jit(solution)/shard_map/ppermute | solution.py:107
  117.6 57.2 %collective-permute-start.6 = (bf16[2,224,896]{2,1,0:T(8,128)(2,1)}, bf16[2,224,896]{2,1,0:T(8,128)(2,1)}, u32[]{:S(2)}, u32[]{:S(2)}) collective-permute-start(bf16[2,224,896]{2,1,0:T(8,128)(2,1)} %collective-permute-done.3), channel_id=1, source_target_pairs={{0,32},{16,48},{32,64},{48,80},{64,96},{80,112},{96,128},{112,144}... | collective-permute-start | bytes 2408456 | tf_op jit(solution)/shard_map/ppermute | solution.py:107
  120.3 16.6 %collective-permute-start.25 = (bf16[1,224,896]{2,1,0:T(8,128)(2,1)S(1)}, bf16[1,224,896]{2,1,0:T(8,128)(2,1)S(1)}, u32[]{:S(2)}, u32[]{:S(2)}) collective-permute-start(bf16[1,224,896]{2,1,0:T(8,128)(2,1)S(1)} %collective-permute-done.22), channel_id=1, source_target_pairs={{0,224},{16,240},{32,0},{48,16},{64,32},{80,48},{96,64},{112,80},{... | collective-permute-start | bytes 1204232 | tf_op jit(solution)/shard_map/ppermute | solution.py:107
  128.9 45.9 %collective-permute-start.8 = (bf16[2,224,896]{2,1,0:T(8,128)(2,1)S(1)}, bf16[2,224,896]{2,1,0:T(8,128)(2,1)}, u32[]{:S(2)}, u32[]{:S(2)}) collective-permute-start(bf16[2,224,896]{2,1,0:T(8,128)(2,1)S(1)} %collective-permute-done.4), channel_id=1, source_target_pairs={{0,16},{16,0},{32,48},{48,32},{64,80},{80,64},{96,112},{112,96},{1... | collective-permute-start | bytes 2408456 | tf_op jit(solution)/shard_map/ppermute | solution.py:107
  131.7 56.6 %collective-permute-start.11 = (bf16[2,224,896]{2,1,0:T(8,128)(2,1)}, bf16[2,224,896]{2,1,0:T(8,128)(2,1)S(1)}, u32[]{:S(2)}, u32[]{:S(2)}) collective-permute-start(bf16[2,224,896]{2,1,0:T(8,128)(2,1)} %collective-permute-done.3), channel_id=1, source_target_pairs={{0,16},{16,0},{32,48},{48,32},{64,80},{80,64},{96,112},{112,96},{1... | collective-permute-start | bytes 2408456 | tf_op jit(solution)/shard_map/ppermute | solution.py:107
  135.5 37.3 %collective-permute-start.26 = (bf16[1,224,896]{2,1,0:T(8,128)(2,1)S(1)}, bf16[1,224,896]{2,1,0:T(8,128)(2,1)S(1)}, u32[]{:S(2)}, u32[]{:S(2)}) collective-permute-start(bf16[1,224,896]{2,1,0:T(8,128)(2,1)S(1)} %collective-permute-done.13), channel_id=1, source_target_pairs={{0,16},{16,0},{32,48},{48,32},{64,80},{80,64},{96,112},{112,96},{1... | collective-permute-start | bytes 1204232 | tf_op jit(solution)/shard_map/ppermute | solution.py:107
  136.8 53.6 %collective-permute-start.7 = (bf16[2,224,896]{2,1,0:T(8,128)(2,1)S(1)}, bf16[2,224,896]{2,1,0:T(8,128)(2,1)}, u32[]{:S(2)}, u32[]{:S(2)}) collective-permute-start(bf16[2,224,896]{2,1,0:T(8,128)(2,1)S(1)} %collective-permute-done.4), channel_id=1, source_target_pairs={{0,224},{16,240},{32,0},{48,16},{64,32},{80,48},{96,64},{112,80},{... | collective-permute-start | bytes 2408456 | tf_op jit(solution)/shard_map/ppermute | solution.py:107
  172.8 36.0 %collective-permute-start.29 = (bf16[2,224,896]{2,1,0:T(8,128)(2,1)S(1)}, bf16[2,224,896]{2,1,0:T(8,128)(2,1)}, u32[]{:S(2)}, u32[]{:S(2)}) collective-permute-start(bf16[2,224,896]{2,1,0:T(8,128)(2,1)S(1)} %collective-permute-done.1), channel_id=1, source_target_pairs={{0,16},{16,0},{32,48},{48,32},{64,80},{80,64},{96,112},{112,96},{1... | collective-permute-start | bytes 2408456 | tf_op jit(solution)/shard_map/ppermute | solution.py:107
  174.8 23.0 %collective-permute-start.9 = (bf16[2,224,896]{2,1,0:T(8,128)(2,1)}, bf16[2,224,896]{2,1,0:T(8,128)(2,1)}, u32[]{:S(2)}, u32[]{:S(2)}) collective-permute-start(bf16[2,224,896]{2,1,0:T(8,128)(2,1)} %collective-permute-done.6), channel_id=1, source_target_pairs={{0,32},{16,48},{32,64},{48,80},{64,96},{80,112},{96,128},{112,144}... | collective-permute-start | bytes 2408456 | tf_op jit(solution)/shard_map/ppermute | solution.py:107
  174.8 19.8 %collective-permute-start.10 = (bf16[2,224,896]{2,1,0:T(8,128)(2,1)}, bf16[2,224,896]{2,1,0:T(8,128)(2,1)}, u32[]{:S(2)}, u32[]{:S(2)}) collective-permute-start(bf16[2,224,896]{2,1,0:T(8,128)(2,1)} %collective-permute-done.8), channel_id=1, source_target_pairs={{0,224},{16,240},{32,0},{48,16},{64,32},{80,48},{96,64},{112,80},{... | collective-permute-start | bytes 2408456 | tf_op jit(solution)/shard_map/ppermute | solution.py:107
  188.4 17.2 %collective-permute-start.27 = (bf16[2,224,896]{2,1,0:T(8,128)(2,1)S(1)}, bf16[2,224,896]{2,1,0:T(8,128)(2,1)S(1)}, u32[]{:S(2)}, u32[]{:S(2)}) collective-permute-start(bf16[2,224,896]{2,1,0:T(8,128)(2,1)S(1)} %collective-permute-done.11), channel_id=1, source_target_pairs={{0,32},{16,48},{32,64},{48,80},{64,96},{80,112},{96,128},{112,144}... | collective-permute-start | bytes 2408456 | tf_op jit(solution)/shard_map/ppermute | solution.py:107
  194.6 13.2 %collective-permute-start.28 = (bf16[2,224,896]{2,1,0:T(8,128)(2,1)}, bf16[2,224,896]{2,1,0:T(8,128)(2,1)S(1)}, u32[]{:S(2)}, u32[]{:S(2)}) collective-permute-start(bf16[2,224,896]{2,1,0:T(8,128)(2,1)} %collective-permute-done.10), channel_id=1, source_target_pairs={{0,224},{16,240},{32,0},{48,16},{64,32},{80,48},{96,64},{112,80},{... | collective-permute-start | bytes 2408456 | tf_op jit(solution)/shard_map/ppermute | solution.py:107
  (7 other events, 31.8 us)

commit v3 on v2

--- a/solution.py
+++ b/solution.py
@@ -35,22 +35,21 @@
     ).astype(jnp.bfloat16)
 
 
-def exchange(stage, total):
-    name, bit = stage
-    got = lax.ppermute(total, name, [(i, i ^ bit) for i in range(16)])
-    return total + got
+STAGES = (
+    ("cols", (1,)),
+    ("cols", (2,)),
+    ("cols", (4,)),
+    ("y", (1, 2, 3)),
+    ("fsdp", (2, 4, 6)),
+    ("fsdp", (8,)),
+)
 
 
-STAGES = (
-    ("cols", 8),
-    ("cols", 1),
-    ("cols", 2),
-    ("cols", 4),
-    ("fsdp", 1),
-    ("fsdp", 2),
-    ("fsdp", 4),
-    ("fsdp", 8),
-)
+def flipped(name, bits):
+    if name != "y":
+        return name, [(i, i ^ bits) for i in range(16)]
+    high, low = bits >> 1, bits & 1
+    return ("fsdp", "cols"), [(i, i ^ (high * 16 + low * 8)) for i in range(256)]
 
 
 def gather_norm(norm_train, norm_step):
@@ -59,8 +58,11 @@
     total = lax.dynamic_update_slice(
         jnp.zeros((3584,), own.dtype), own, (at.astype(jnp.uint32) * 14,)
     )
-    for stage in STAGES:
-        total = exchange(stage, total)
+    for name, flips in STAGES:
+        got = [total]
+        for bits in flips:
+            got.append(lax.ppermute(total, *flipped(name, bits)))
+        total = sum(got[1:], got[0])
     return total
 
 
@@ -92,7 +94,7 @@
     )
     own = tuple(map(lax.optimization_barrier, (own_down, own_rest)))
     zero = jnp.uint32(0)
-    down, gate, up = (empty() for _ in range(3))
+    down, gate, up = empty(3)
 
     def put(stack, piece, place):
         return lax.dynamic_update_slice(stack, piece, (slot(place), zero, zero))
@@ -113,19 +115,45 @@
                     gate = put(gate, got[:1], there)
                     up = put(up, got[1:], there)
             if (number, k) == (4, 0):
-                down = down.reshape(3584, COLS).T
+                down = turned(
+                    pltpu.with_memory_space_constraint(
+                        down.reshape(3584, COLS), pltpu.HBM
+                    )
+                )
                 gate, up, down = lax.optimization_barrier((gate, up, down))
     return gate.reshape(3584, COLS), up.reshape(3584, COLS), down, serve_norm
 
 
-def empty():
+def empty(count):
     return pl.pallas_call(
-        lambda out_ref: None,
-        out_specs=pl.BlockSpec(memory_space=pltpu.HBM),
-        out_shape=jax.ShapeDtypeStruct((16, ROWS, COLS), jnp.bfloat16),
-        compiler_params=pltpu.CompilerParams(has_side_effects=True),
+        lambda *out_refs: None,
+        out_specs=[pl.BlockSpec(memory_space=pltpu.HBM)] * count,
+        out_shape=[pltpu.HBM((16, ROWS, COLS), jnp.bfloat16)] * count,
+        compiler_params=pltpu.CompilerParams(
+            has_side_effects=True, vmem_limit_bytes=1 << 20
+        ),
         name="empty",
     )()
+
+
+def turn_kernel(in_ref, out_ref):
+    out_ref[...] = in_ref[...].T
+
+
+def turned(x):
+    rows, cols = x.shape
+    return pl.pallas_call(
+        turn_kernel,
+        grid=(rows // 512,),
+        in_specs=[pl.BlockSpec((512, cols), lambda i: (i, 0))],
+        out_specs=pl.BlockSpec((cols, 512), lambda i: (0, i)),
+        out_shape=jax.ShapeDtypeStruct((cols, rows), x.dtype),
+        compiler_params=pltpu.CompilerParams(vmem_limit_bytes=16 << 20),
+        cost_estimate=pl.CostEstimate(
+            flops=1 << 33, bytes_accessed=4 * rows * cols, transcendentals=0
+        ),
+        name="turn",
+    )(x)
 
 
 def solution(mesh):

time: 211 us -> 204 us (0.967)
  the two profiles are of different devices: /device:TPU:8 before, /device:TPU:24 now
where the time goes in v3:
time: 204 us
  waiting for transfers between devices  92.6 us (45%)
  starting transfers between devices  65.9 us (32%)
  local copies, waits for them, and re-layouts  30.1 us (15%)
  Pallas kernels  8.83 us (4%)
  matrix products  3.97 us (2%)
    ppermute x30, waiting for transfers between devices, per_device(): got = lax.ppermute(held[k][place], 'fsdp', HOPS[direction])  74.3 us
    ppermute x30, starting transfers between devices, per_device(): got = lax.ppermute(held[k][place], 'fsdp', HOPS[direction])  45.3 us
    dynamic_update_slice x32, local copies, waits for them, and re-layouts, put(): return lax.dynamic_update_slice(stack, piece, (slot(place), zero, zero))  29.7 us
    ppermute x10, starting transfers between devices, gather_norm(): got.append(lax.ppermute(total, *flipped(name, bits)))  20.6 us
    ppermute x10, waiting for transfers between devices, gather_norm(): got.append(lax.ppermute(total, *flipped(name, bits)))  18.3 us
    pallas_call x1, Pallas kernels, turned(): pl.pallas_call(turn_kernel, grid=(rows // 512,), in_specs=[pl.BlockSpec((...  8.83 us
  transfers between devices with their start and end apart: 40, of which 22 were waited for; matrix products, arithmetic and copies ran while one was open for 16% of the time, Pallas kernels for 4%

profile of v3, /device:TPU:24, one launch (start us, length us, event | category | flops | bytes accessed | tf_op | source)
XLA Modules:
  0.0 203.7 jit_solution(5584470360459994030)
XLA Ops:
  6.7 3.0 %collective-permute-start.32 = (bf16[3584]{0:T(1024)(128)(2,1)S(1)}, bf16[3584]{0:T(1024)(128)(2,1)S(1)}, u32[]{:S(2)}, u32[]{:S(2)}) collective-permute-start(bf16[3584]{0:T(1024)(128)(2,1)S(1)} %add.223), channel_id=1, source_target_pairs={{0,4},{1,5},{2,6},{3,7},{4,0},{5,1},{6,2},{7,3},{8,12},{9,13},{10,... | collective-permute-start | bytes 21512 | tf_op jit(solution)/shard_map/ppermute | solution.py:64
  12.6 2.6 %collective-permute-start.34 = (bf16[3584]{0:T(1024)(128)(2,1)S(1)}, bf16[3584]{0:T(1024)(128)(2,1)S(1)}, u32[]{:S(2)}, u32[]{:S(2)}) collective-permute-start(bf16[3584]{0:T(1024)(128)(2,1)S(1)} %add.224), channel_id=1, source_target_pairs={{0,16},{1,17},{2,18},{3,19},{4,20},{5,21},{6,22},{7,23},{8,24},{9,... | collective-permute-start | bytes 21512 | tf_op jit(solution)/shard_map/ppermute | solution.py:64
  16.7 2.0 collective-permute-start
  20.7 4.5 %collective-permute-start.37 = (bf16[3584]{0:T(1024)(128)(2,1)S(1)}, bf16[3584]{0:T(1024)(128)(2,1)S(1)}, u32[]{:S(2)}, u32[]{:S(2)}) collective-permute-start(bf16[3584]{0:T(1024)(128)(2,1)S(1)} %add_add_fusion.1), channel_id=1, source_target_pairs={{0,64},{16,80},{32,96},{48,112},{64,0},{80,16},{96,32},{112,48},{1... | collective-permute-start | bytes 21512 | tf_op jit(solution)/shard_map/ppermute | solution.py:64
  27.2 10.0 %collective-permute-done.36 = bf16[3584]{0:T(1024)(128)(2,1)S(1)} collective-permute-done((bf16[3584]{0:T(1024)(128)(2,1)S(1)}, bf16[3584]{0:T(1024)(128)(2,1)S(1)}, u32[]{:S(2)}, u32[]{:S(2)}) %collective-permute-start.36) | collective-permute-done | bytes 7200 | tf_op jit(solution)/shard_map/ppermute | solution.py:64
  37.5 6.3 %collective-permute-start.39 = (bf16[3584]{0:T(1024)(128)(2,1)S(1)}, bf16[3584]{0:T(1024)(128)(2,1)S(1)}, u32[]{:S(2)}, u32[]{:S(2)}) collective-permute-start(bf16[3584]{0:T(1024)(128)(2,1)S(1)} %add_add_fusion), channel_id=1, source_target_pairs={{0,128},{16,144},{32,160},{48,176},{64,192},{80,208},{96,224},{112... | collective-permute-start | bytes 21512 | tf_op jit(solution)/shard_map/ppermute | solution.py:64
  43.8 1.7 collective-permute-start.1
  45.6 3.7 %collective-permute-done.39 = bf16[3584]{0:T(1024)(128)(2,1)S(1)} collective-permute-done((bf16[3584]{0:T(1024)(128)(2,1)S(1)}, bf16[3584]{0:T(1024)(128)(2,1)S(1)}, u32[]{:S(2)}, u32[]{:S(2)}) %collective-permute-start.39) | collective-permute-done | bytes 7200 | tf_op jit(solution)/shard_map/ppermute | solution.py:64
  51.7 3.5 %collective-permute-start.2 = (bf16[2,224,896]{2,1,0:T(8,128)(2,1)S(1)}, bf16[2,224,896]{2,1,0:T(8,128)(2,1)S(1)}, u32[]{:S(2)}, u32[]{:S(2)}) collective-permute-start(bf16[2,224,896]{2,1,0:T(8,128)(2,1)S(1)} %pad_maximum_fusion), channel_id=1, source_target_pairs={{0,16},{16,0},{32,48},{48,32},{64,80},{80,64},{96,112},{112,96},{1... | collective-permute-start | bytes 2408456 | tf_op jit(solution)/shard_map/ppermute | solution.py:109
  55.2 1.8 constant_dynamic-update-slice_fusion.14
  57.0 11.8 %collective-permute-done.13 = bf16[1,224,896]{2,1,0:T(8,128)(2,1)S(1)} collective-permute-done((bf16[1,224,896]{2,1,0:T(8,128)(2,1)S(1)}, bf16[1,224,896]{2,1,0:T(8,128)(2,1)S(1)}, u32[]{:S(2)}, u32[]{:S(2)}) %collective-permute-start.13) | collective-permute-done | bytes 401440 | tf_op jit(solution)/shard_map/ppermute | solution.py:109
  70.9 1.9 collective-permute-start.16
  72.9 1.8 constant_dynamic-update-slice_fusion.12
  76.8 2.9 %collective-permute-done.2 = bf16[2,224,896]{2,1,0:T(8,128)(2,1)S(1)} collective-permute-done((bf16[2,224,896]{2,1,0:T(8,128)(2,1)S(1)}, bf16[2,224,896]{2,1,0:T(8,128)(2,1)S(1)}, u32[]{:S(2)}, u32[]{:S(2)}) %collective-permute-start.2) | collective-permute-done | bytes 802848 | tf_op jit(solution)/shard_map/ppermute | solution.py:109
  79.8 2.6 %collective-permute-done.15 = bf16[1,224,896]{2,1,0:T(8,128)(2,1)S(1)} collective-permute-done((bf16[1,224,896]{2,1,0:T(8,128)(2,1)}, bf16[1,224,896]{2,1,0:T(8,128)(2,1)S(1)}, u32[]{:S(2)}, u32[]{:S(2)}) %collective-permute-start.15) | collective-permute-done | bytes 401440 | tf_op jit(solution)/shard_map/ppermute | solution.py:109
  83.1 3.1 %collective-permute-start.19 = (bf16[1,224,896]{2,1,0:T(8,128)(2,1)S(1)}, bf16[1,224,896]{2,1,0:T(8,128)(2,1)S(1)}, u32[]{:S(2)}, u32[]{:S(2)}) collective-permute-start(bf16[1,224,896]{2,1,0:T(8,128)(2,1)S(1)} %collective-permute-done.16), channel_id=1, source_target_pairs={{0,224},{16,240},{32,0},{48,16},{64,32},{80,48},{96,64},{112,80},{... | collective-permute-start | bytes 1204232 | tf_op jit(solution)/shard_map/ppermute | solution.py:109
  89.1 8.3 %collective-permute-done.18 = bf16[1,224,896]{2,1,0:T(8,128)(2,1)S(1)} collective-permute-done((bf16[1,224,896]{2,1,0:T(8,128)(2,1)S(1)}, bf16[1,224,896]{2,1,0:T(8,128)(2,1)S(1)}, u32[]{:S(2)}, u32[]{:S(2)}) %collective-permute-start.18) | collective-permute-done | bytes 401440 | tf_op jit(solution)/shard_map/ppermute | solution.py:109
  97.4 3.2 %collective-permute-start.23 = (bf16[1,224,896]{2,1,0:T(8,128)(2,1)S(1)}, bf16[1,224,896]{2,1,0:T(8,128)(2,1)S(1)}, u32[]{:S(2)}, u32[]{:S(2)}) collective-permute-start(bf16[1,224,896]{2,1,0:T(8,128)(2,1)S(1)} %collective-permute-done.15), channel_id=1, source_target_pairs={{0,16},{16,0},{32,48},{48,32},{64,80},{80,64},{96,112},{112,96},{1... | collective-permute-start | bytes 1204232 | tf_op jit(solution)/shard_map/ppermute | solution.py:109
  107.4 3.6 %collective-permute-done.23 = bf16[1,224,896]{2,1,0:T(8,128)(2,1)S(1)} collective-permute-done((bf16[1,224,896]{2,1,0:T(8,128)(2,1)S(1)}, bf16[1,224,896]{2,1,0:T(8,128)(2,1)S(1)}, u32[]{:S(2)}, u32[]{:S(2)}) %collective-permute-start.23) | collective-permute-done | bytes 401440 | tf_op jit(solution)/shard_map/ppermute | solution.py:109
  111.1 2.0 collective-permute-start.24
  115.0 3.9 %collective-permute-done.21 = bf16[1,224,896]{2,1,0:T(8,128)(2,1)S(1)} collective-permute-done((bf16[1,224,896]{2,1,0:T(8,128)(2,1)S(1)}, bf16[1,224,896]{2,1,0:T(8,128)(2,1)S(1)}, u32[]{:S(2)}, u32[]{:S(2)}) %collective-permute-start.21) | collective-permute-done | bytes 401440 | tf_op jit(solution)/shard_map/ppermute | solution.py:109
  118.9 2.1 %collective-permute-start.8 = (bf16[2,224,896]{2,1,0:T(8,128)(2,1)S(1)}, bf16[2,224,896]{2,1,0:T(8,128)(2,1)S(1)}, u32[]{:S(2)}, u32[]{:S(2)}) collective-permute-start(bf16[2,224,896]{2,1,0:T(8,128)(2,1)S(1)} %collective-permute-done.4), channel_id=1, source_target_pairs={{0,16},{16,0},{32,48},{48,32},{64,80},{80,64},{96,112},{112,96},{1... | collective-permute-start | bytes 2408456 | tf_op jit(solution)/shard_map/ppermute | solution.py:109
  121.0 3.2 %collective-permute-start.25 = (bf16[1,224,896]{2,1,0:T(8,128)(2,1)S(1)}, bf16[1,224,896]{2,1,0:T(8,128)(2,1)S(1)}, u32[]{:S(2)}, u32[]{:S(2)}) collective-permute-start(bf16[1,224,896]{2,1,0:T(8,128)(2,1)S(1)} %collective-permute-done.22), channel_id=1, source_target_pairs={{0,224},{16,240},{32,0},{48,16},{64,32},{80,48},{96,64},{112,80},{... | collective-permute-start | bytes 1204232 | tf_op jit(solution)/shard_map/ppermute | solution.py:109
  127.5 2.1 %collective-permute-start.26 = (bf16[1,224,896]{2,1,0:T(8,128)(2,1)S(1)}, bf16[1,224,896]{2,1,0:T(8,128)(2,1)S(1)}, u32[]{:S(2)}, u32[]{:S(2)}) collective-permute-start(bf16[1,224,896]{2,1,0:T(8,128)(2,1)S(1)} %collective-permute-done.13), channel_id=1, source_target_pairs={{0,16},{16,0},{32,48},{48,32},{64,80},{80,64},{96,112},{112,96},{1... | collective-permute-start | bytes 1204232 | tf_op jit(solution)/shard_map/ppermute | solution.py:109
  133.9 3.7 %collective-permute-start.7 = (bf16[2,224,896]{2,1,0:T(8,128)(2,1)S(1)}, bf16[2,224,896]{2,1,0:T(8,128)(2,1)S(1)}, u32[]{:S(2)}, u32[]{:S(2)}) collective-permute-start(bf16[2,224,896]{2,1,0:T(8,128)(2,1)S(1)} %collective-permute-done.4), channel_id=1, source_target_pairs={{0,224},{16,240},{32,0},{48,16},{64,32},{80,48},{96,64},{112,80},{... | collective-permute-start | bytes 2408456 | tf_op jit(solution)/shard_map/ppermute | solution.py:109
  138.3 15.8 %collective-permute-done.26 = bf16[1,224,896]{2,1,0:T(8,128)(2,1)S(1)} collective-permute-done((bf16[1,224,896]{2,1,0:T(8,128)(2,1)S(1)}, bf16[1,224,896]{2,1,0:T(8,128)(2,1)S(1)}, u32[]{:S(2)}, u32[]{:S(2)}) %collective-permute-start.26) | collective-permute-done | bytes 401440 | tf_op jit(solution)/shard_map/ppermute | solution.py:109
  154.1 3.2 %collective-permute-start.11 = (bf16[2,224,896]{2,1,0:T(8,128)(2,1)S(1)}, bf16[2,224,896]{2,1,0:T(8,128)(2,1)S(1)}, u32[]{:S(2)}, u32[]{:S(2)}) collective-permute-start(bf16[2,224,896]{2,1,0:T(8,128)(2,1)S(1)} %collective-permute-done.3), channel_id=1, source_target_pairs={{0,16},{16,0},{32,48},{48,32},{64,80},{80,64},{96,112},{112,96},{1... | collective-permute-start | bytes 2408456 | tf_op jit(solution)/shard_map/ppermute | solution.py:109
  158.1 3.2 %collective-permute-start.10 = (bf16[2,224,896]{2,1,0:T(8,128)(2,1)S(1)}, bf16[2,224,896]{2,1,0:T(8,128)(2,1)S(1)}, u32[]{:S(2)}, u32[]{:S(2)}) collective-permute-start(bf16[2,224,896]{2,1,0:T(8,128)(2,1)S(1)} %collective-permute-done.8), channel_id=1, source_target_pairs={{0,224},{16,240},{32,0},{48,16},{64,32},{80,48},{96,64},{112,80},{... | collective-permute-start | bytes 2408456 | tf_op jit(solution)/shard_map/ppermute | solution.py:109
  161.4 8.8 %turn.1 = bf16[896,3584]{1,0:T(8,128)(2,1)} custom-call(bf16[3584,896]{1,0:T(8,128)(2,1)} %bitcast.17), custom_call_target="tpu_custom_call" | custom-call | flops 8589934592 | bytes 12845056 | tf_op jit(solution)/shard_map/turn/pallas_call | solution.py:145
  170.2 13.4 %collective-permute-done.11 = bf16[2,224,896]{2,1,0:T(8,128)(2,1)S(1)} collective-permute-done((bf16[2,224,896]{2,1,0:T(8,128)(2,1)S(1)}, bf16[2,224,896]{2,1,0:T(8,128)(2,1)S(1)}, u32[]{:S(2)}, u32[]{:S(2)}) %collective-permute-start.11) | collective-permute-done | bytes 802848 | tf_op jit(solution)/shard_map/ppermute | solution.py:109
  186.4 3.2 %collective-permute-start.28 = (bf16[2,224,896]{2,1,0:T(8,128)(2,1)S(1)}, bf16[2,224,896]{2,1,0:T(8,128)(2,1)S(1)}, u32[]{:S(2)}, u32[]{:S(2)}) collective-permute-start(bf16[2,224,896]{2,1,0:T(8,128)(2,1)S(1)} %collective-permute-done.10), channel_id=1, source_target_pairs={{0,224},{16,240},{32,0},{48,16},{64,32},{80,48},{96,64},{112,80},{... | collective-permute-start | bytes 2408456 | tf_op jit(solution)/shard_map/ppermute | solution.py:109
  192.5 7.2 %collective-permute-done.27 = bf16[2,224,896]{2,1,0:T(8,128)(2,1)S(1)} collective-permute-done((bf16[2,224,896]{2,1,0:T(8,128)(2,1)S(1)}, bf16[2,224,896]{2,1,0:T(8,128)(2,1)S(1)}, u32[]{:S(2)}, u32[]{:S(2)}) %collective-permute-start.27) | collective-permute-done | bytes 802848 | tf_op jit(solution)/shard_map/ppermute | solution.py:109
  (98 shorter events, 52.7 us)
Async XLA Ops:
  16.7 58.0 %collective-permute-start = (bf16[2,224,896]{2,1,0:T(8,128)(2,1)S(1)}, bf16[2,224,896]{2,1,0:T(8,128)(2,1)S(1)}, u32[]{:S(2)}, u32[]{:S(2)}) collective-permute-start(bf16[2,224,896]{2,1,0:T(8,128)(2,1)S(1)} %pad_maximum_fusion), channel_id=1, source_target_pairs={{0,32},{16,48},{32,64},{48,80},{64,96},{80,112},{96,128},{112,144}... | collective-permute-start | bytes 2408456 | tf_op jit(solution)/shard_map/ppermute | solution.py:109
  20.1 17.0 %collective-permute-start.36 = (bf16[3584]{0:T(1024)(128)(2,1)S(1)}, bf16[3584]{0:T(1024)(128)(2,1)S(1)}, u32[]{:S(2)}, u32[]{:S(2)}) collective-permute-start(bf16[3584]{0:T(1024)(128)(2,1)S(1)} %add_add_fusion.1), channel_id=1, source_target_pairs={{0,32},{16,48},{32,0},{48,16},{64,96},{80,112},{96,64},{112,80},{1... | collective-permute-start | bytes 21512 | tf_op jit(solution)/shard_map/ppermute | solution.py:64
  20.7 16.6 %collective-permute-start.37 = (bf16[3584]{0:T(1024)(128)(2,1)S(1)}, bf16[3584]{0:T(1024)(128)(2,1)S(1)}, u32[]{:S(2)}, u32[]{:S(2)}) collective-permute-start(bf16[3584]{0:T(1024)(128)(2,1)S(1)} %add_add_fusion.1), channel_id=1, source_target_pairs={{0,64},{16,80},{32,96},{48,112},{64,0},{80,16},{96,32},{112,48},{1... | collective-permute-start | bytes 21512 | tf_op jit(solution)/shard_map/ppermute | solution.py:64
  25.2 12.3 %collective-permute-start.38 = (bf16[3584]{0:T(1024)(128)(2,1)S(1)}, bf16[3584]{0:T(1024)(128)(2,1)S(1)}, u32[]{:S(2)}, u32[]{:S(2)}) collective-permute-start(bf16[3584]{0:T(1024)(128)(2,1)S(1)} %add_add_fusion.1), channel_id=1, source_target_pairs={{0,96},{16,112},{32,64},{48,80},{64,32},{80,48},{96,0},{112,16},{1... | collective-permute-start | bytes 21512 | tf_op jit(solution)/shard_map/ppermute | solution.py:64
  26.5 25.2 %collective-permute-start.12 = (bf16[1,224,896]{2,1,0:T(8,128)(2,1)S(1)}, bf16[1,224,896]{2,1,0:T(8,128)(2,1)}, u32[]{:S(2)}, u32[]{:S(2)}) collective-permute-start(bf16[1,224,896]{2,1,0:T(8,128)(2,1)S(1)} %fusion.3), channel_id=1, source_target_pairs={{0,32},{16,48},{32,64},{48,80},{64,96},{80,112},{96,128},{112,144}... | collective-permute-start | bytes 1204232 | tf_op jit(solution)/shard_map/ppermute | solution.py:109
  43.8 31.9 %collective-permute-start.1 = (bf16[2,224,896]{2,1,0:T(8,128)(2,1)S(1)}, bf16[2,224,896]{2,1,0:T(8,128)(2,1)S(1)}, u32[]{:S(2)}, u32[]{:S(2)}) collective-permute-start(bf16[2,224,896]{2,1,0:T(8,128)(2,1)S(1)} %pad_maximum_fusion), channel_id=1, source_target_pairs={{0,224},{16,240},{32,0},{48,16},{64,32},{80,48},{96,64},{112,80},{... | collective-permute-start | bytes 2408456 | tf_op jit(solution)/shard_map/ppermute | solution.py:109
  45.4 23.4 %collective-permute-start.13 = (bf16[1,224,896]{2,1,0:T(8,128)(2,1)S(1)}, bf16[1,224,896]{2,1,0:T(8,128)(2,1)S(1)}, u32[]{:S(2)}, u32[]{:S(2)}) collective-permute-start(bf16[1,224,896]{2,1,0:T(8,128)(2,1)S(1)} %fusion.3), channel_id=1, source_target_pairs={{0,224},{16,240},{32,0},{48,16},{64,32},{80,48},{96,64},{112,80},{... | collective-permute-start | bytes 1204232 | tf_op jit(solution)/shard_map/ppermute | solution.py:109
  49.3 21.6 %collective-permute-start.14 = (bf16[1,224,896]{2,1,0:T(8,128)(2,1)S(1)}, bf16[1,224,896]{2,1,0:T(8,128)(2,1)}, u32[]{:S(2)}, u32[]{:S(2)}) collective-permute-start(bf16[1,224,896]{2,1,0:T(8,128)(2,1)S(1)} %fusion.3), channel_id=1, source_target_pairs={{0,16},{16,0},{32,48},{48,32},{64,80},{80,64},{96,112},{112,96},{1... | collective-permute-start | bytes 1204232 | tf_op jit(solution)/shard_map/ppermute | solution.py:109
  51.7 27.9 %collective-permute-start.2 = (bf16[2,224,896]{2,1,0:T(8,128)(2,1)S(1)}, bf16[2,224,896]{2,1,0:T(8,128)(2,1)S(1)}, u32[]{:S(2)}, u32[]{:S(2)}) collective-permute-start(bf16[2,224,896]{2,1,0:T(8,128)(2,1)S(1)} %pad_maximum_fusion), channel_id=1, source_target_pairs={{0,16},{16,0},{32,48},{48,32},{64,80},{80,64},{96,112},{112,96},{1... | collective-permute-start | bytes 2408456 | tf_op jit(solution)/shard_map/ppermute | solution.py:109
  68.8 13.6 %collective-permute-start.15 = (bf16[1,224,896]{2,1,0:T(8,128)(2,1)}, bf16[1,224,896]{2,1,0:T(8,128)(2,1)S(1)}, u32[]{:S(2)}, u32[]{:S(2)}) collective-permute-start(bf16[1,224,896]{2,1,0:T(8,128)(2,1)} %collective-permute-done.12), channel_id=1, source_target_pairs={{0,32},{16,48},{32,64},{48,80},{64,96},{80,112},{96,128},{112,144}... | collective-permute-start | bytes 1204232 | tf_op jit(solution)/shard_map/ppermute | solution.py:109
  70.9 12.2 %collective-permute-start.16 = (bf16[1,224,896]{2,1,0:T(8,128)(2,1)S(1)}, bf16[1,224,896]{2,1,0:T(8,128)(2,1)S(1)}, u32[]{:S(2)}, u32[]{:S(2)}) collective-permute-start(bf16[1,224,896]{2,1,0:T(8,128)(2,1)S(1)} %collective-permute-done.13), channel_id=1, source_target_pairs={{0,224},{16,240},{32,0},{48,16},{64,32},{80,48},{96,64},{112,80},{... | collective-permute-start | bytes 1204232 | tf_op jit(solution)/shard_map/ppermute | solution.py:109
  74.7 13.3 %collective-permute-start.17 = (bf16[1,224,896]{2,1,0:T(8,128)(2,1)}, bf16[1,224,896]{2,1,0:T(8,128)(2,1)S(1)}, u32[]{:S(2)}, u32[]{:S(2)}) collective-permute-start(bf16[1,224,896]{2,1,0:T(8,128)(2,1)} %collective-permute-done.12), channel_id=1, source_target_pairs={{0,16},{16,0},{32,48},{48,32},{64,80},{80,64},{96,112},{112,96},{1... | collective-permute-start | bytes 1204232 | tf_op jit(solution)/shard_map/ppermute | solution.py:109
  75.7 35.4 %collective-permute-start.3 = (bf16[2,224,896]{2,1,0:T(8,128)(2,1)S(1)}, bf16[2,224,896]{2,1,0:T(8,128)(2,1)S(1)}, u32[]{:S(2)}, u32[]{:S(2)}) collective-permute-start(bf16[2,224,896]{2,1,0:T(8,128)(2,1)S(1)} %collective-permute-done), channel_id=1, source_target_pairs={{0,32},{16,48},{32,64},{48,80},{64,96},{80,112},{96,128},{112,144}... | collective-permute-start | bytes 2408456 | tf_op jit(solution)/shard_map/ppermute | solution.py:109
  79.7 34.4 %collective-permute-start.4 = (bf16[2,224,896]{2,1,0:T(8,128)(2,1)S(1)}, bf16[2,224,896]{2,1,0:T(8,128)(2,1)S(1)}, u32[]{:S(2)}, u32[]{:S(2)}) collective-permute-start(bf16[2,224,896]{2,1,0:T(8,128)(2,1)S(1)} %collective-permute-done.1), channel_id=1, source_target_pairs={{0,224},{16,240},{32,0},{48,16},{64,32},{80,48},{96,64},{112,80},{... | collective-permute-start | bytes 2408456 | tf_op jit(solution)/shard_map/ppermute | solution.py:109
  82.4 15.0 %collective-permute-start.18 = (bf16[1,224,896]{2,1,0:T(8,128)(2,1)S(1)}, bf16[1,224,896]{2,1,0:T(8,128)(2,1)S(1)}, u32[]{:S(2)}, u32[]{:S(2)}) collective-permute-start(bf16[1,224,896]{2,1,0:T(8,128)(2,1)S(1)} %collective-permute-done.15), channel_id=1, source_target_pairs={{0,32},{16,48},{32,64},{48,80},{64,96},{80,112},{96,128},{112,144}... | collective-permute-start | bytes 1204232 | tf_op jit(solution)/shard_map/ppermute | solution.py:109
  83.1 20.2 %collective-permute-start.19 = (bf16[1,224,896]{2,1,0:T(8,128)(2,1)S(1)}, bf16[1,224,896]{2,1,0:T(8,128)(2,1)S(1)}, u32[]{:S(2)}, u32[]{:S(2)}) collective-permute-start(bf16[1,224,896]{2,1,0:T(8,128)(2,1)S(1)} %collective-permute-done.16), channel_id=1, source_target_pairs={{0,224},{16,240},{32,0},{48,16},{64,32},{80,48},{96,64},{112,80},{... | collective-permute-start | bytes 1204232 | tf_op jit(solution)/shard_map/ppermute | solution.py:109
  88.0 17.6 %collective-permute-start.20 = (bf16[1,224,896]{2,1,0:T(8,128)(2,1)S(1)}, bf16[1,224,896]{2,1,0:T(8,128)(2,1)S(1)}, u32[]{:S(2)}, u32[]{:S(2)}) collective-permute-start(bf16[1,224,896]{2,1,0:T(8,128)(2,1)S(1)} %collective-permute-done.16), channel_id=1, source_target_pairs={{0,16},{16,0},{32,48},{48,32},{64,80},{80,64},{96,112},{112,96},{1... | collective-permute-start | bytes 1204232 | tf_op jit(solution)/shard_map/ppermute | solution.py:109
  97.4 13.7 %collective-permute-start.23 = (bf16[1,224,896]{2,1,0:T(8,128)(2,1)S(1)}, bf16[1,224,896]{2,1,0:T(8,128)(2,1)S(1)}, u32[]{:S(2)}, u32[]{:S(2)}) collective-permute-start(bf16[1,224,896]{2,1,0:T(8,128)(2,1)S(1)} %collective-permute-done.15), channel_id=1, source_target_pairs={{0,16},{16,0},{32,48},{48,32},{64,80},{80,64},{96,112},{112,96},{1... | collective-permute-start | bytes 1204232 | tf_op jit(solution)/shard_map/ppermute | solution.py:109
  103.3 27.1 %collective-permute-start.5 = (bf16[2,224,896]{2,1,0:T(8,128)(2,1)S(1)}, bf16[2,224,896]{2,1,0:T(8,128)(2,1)S(1)}, u32[]{:S(2)}, u32[]{:S(2)}) collective-permute-start(bf16[2,224,896]{2,1,0:T(8,128)(2,1)S(1)} %collective-permute-done), channel_id=1, source_target_pairs={{0,16},{16,0},{32,48},{48,32},{64,80},{80,64},{96,112},{112,96},{1... | collective-permute-start | bytes 2408456 | tf_op jit(solution)/shard_map/ppermute | solution.py:109
  105.5 13.4 %collective-permute-start.21 = (bf16[1,224,896]{2,1,0:T(8,128)(2,1)S(1)}, bf16[1,224,896]{2,1,0:T(8,128)(2,1)S(1)}, u32[]{:S(2)}, u32[]{:S(2)}) collective-permute-start(bf16[1,224,896]{2,1,0:T(8,128)(2,1)S(1)} %collective-permute-done.18), channel_id=1, source_target_pairs={{0,32},{16,48},{32,64},{48,80},{64,96},{80,112},{96,128},{112,144}... | collective-permute-start | bytes 1204232 | tf_op jit(solution)/shard_map/ppermute | solution.py:109
  111.1 16.4 %collective-permute-start.24 = (bf16[1,224,896]{2,1,0:T(8,128)(2,1)S(1)}, bf16[1,224,896]{2,1,0:T(8,128)(2,1)S(1)}, u32[]{:S(2)}, u32[]{:S(2)}) collective-permute-start(bf16[1,224,896]{2,1,0:T(8,128)(2,1)S(1)} %collective-permute-done.23), channel_id=1, source_target_pairs={{0,32},{16,48},{32,64},{48,80},{64,96},{80,112},{96,128},{112,144}... | collective-permute-start | bytes 1204232 | tf_op jit(solution)/shard_map/ppermute | solution.py:109
  114.1 44.1 %collective-permute-start.6 = (bf16[2,224,896]{2,1,0:T(8,128)(2,1)S(1)}, bf16[2,224,896]{2,1,0:T(8,128)(2,1)S(1)}, u32[]{:S(2)}, u32[]{:S(2)}) collective-permute-start(bf16[2,224,896]{2,1,0:T(8,128)(2,1)S(1)} %collective-permute-done.3), channel_id=1, source_target_pairs={{0,32},{16,48},{32,64},{48,80},{64,96},{80,112},{96,128},{112,144}... | collective-permute-start | bytes 2408456 | tf_op jit(solution)/shard_map/ppermute | solution.py:109
  118.9 39.2 %collective-permute-start.8 = (bf16[2,224,896]{2,1,0:T(8,128)(2,1)S(1)}, bf16[2,224,896]{2,1,0:T(8,128)(2,1)S(1)}, u32[]{:S(2)}, u32[]{:S(2)}) collective-permute-start(bf16[2,224,896]{2,1,0:T(8,128)(2,1)S(1)} %collective-permute-done.4), channel_id=1, source_target_pairs={{0,16},{16,0},{32,48},{48,32},{64,80},{80,64},{96,112},{112,96},{1... | collective-permute-start | bytes 2408456 | tf_op jit(solution)/shard_map/ppermute | solution.py:109
  121.0 12.9 %collective-permute-start.25 = (bf16[1,224,896]{2,1,0:T(8,128)(2,1)S(1)}, bf16[1,224,896]{2,1,0:T(8,128)(2,1)S(1)}, u32[]{:S(2)}, u32[]{:S(2)}) collective-permute-start(bf16[1,224,896]{2,1,0:T(8,128)(2,1)S(1)} %collective-permute-done.22), channel_id=1, source_target_pairs={{0,224},{16,240},{32,0},{48,16},{64,32},{80,48},{96,64},{112,80},{... | collective-permute-start | bytes 1204232 | tf_op jit(solution)/shard_map/ppermute | solution.py:109
  127.5 26.6 %collective-permute-start.26 = (bf16[1,224,896]{2,1,0:T(8,128)(2,1)S(1)}, bf16[1,224,896]{2,1,0:T(8,128)(2,1)S(1)}, u32[]{:S(2)}, u32[]{:S(2)}) collective-permute-start(bf16[1,224,896]{2,1,0:T(8,128)(2,1)S(1)} %collective-permute-done.13), channel_id=1, source_target_pairs={{0,16},{16,0},{32,48},{48,32},{64,80},{80,64},{96,112},{112,96},{1... | collective-permute-start | bytes 1204232 | tf_op jit(solution)/shard_map/ppermute | solution.py:109
  130.4 72.4 %collective-permute-start.29 = (bf16[2,224,896]{2,1,0:T(8,128)(2,1)S(1)}, bf16[2,224,896]{2,1,0:T(8,128)(2,1)S(1)}, u32[]{:S(2)}, u32[]{:S(2)}) collective-permute-start(bf16[2,224,896]{2,1,0:T(8,128)(2,1)S(1)} %collective-permute-done.1), channel_id=1, source_target_pairs={{0,16},{16,0},{32,48},{48,32},{64,80},{80,64},{96,112},{112,96},{1... | collective-permute-start | bytes 2408456 | tf_op jit(solution)/shard_map/ppermute | solution.py:109
  133.9 50.6 %collective-permute-start.7 = (bf16[2,224,896]{2,1,0:T(8,128)(2,1)S(1)}, bf16[2,224,896]{2,1,0:T(8,128)(2,1)S(1)}, u32[]{:S(2)}, u32[]{:S(2)}) collective-permute-start(bf16[2,224,896]{2,1,0:T(8,128)(2,1)S(1)} %collective-permute-done.4), channel_id=1, source_target_pairs={{0,224},{16,240},{32,0},{48,16},{64,32},{80,48},{96,64},{112,80},{... | collective-permute-start | bytes 2408456 | tf_op jit(solution)/shard_map/ppermute | solution.py:109
  154.1 29.4 %collective-permute-start.11 = (bf16[2,224,896]{2,1,0:T(8,128)(2,1)S(1)}, bf16[2,224,896]{2,1,0:T(8,128)(2,1)S(1)}, u32[]{:S(2)}, u32[]{:S(2)}) collective-permute-start(bf16[2,224,896]{2,1,0:T(8,128)(2,1)S(1)} %collective-permute-done.3), channel_id=1, source_target_pairs={{0,16},{16,0},{32,48},{48,32},{64,80},{80,64},{96,112},{112,96},{1... | collective-permute-start | bytes 2408456 | tf_op jit(solution)/shard_map/ppermute | solution.py:109
  158.1 31.5 %collective-permute-start.9 = (bf16[2,224,896]{2,1,0:T(8,128)(2,1)S(1)}, bf16[2,224,896]{2,1,0:T(8,128)(2,1)S(1)}, u32[]{:S(2)}, u32[]{:S(2)}) collective-permute-start(bf16[2,224,896]{2,1,0:T(8,128)(2,1)S(1)} %collective-permute-done.6), channel_id=1, source_target_pairs={{0,32},{16,48},{32,64},{48,80},{64,96},{80,112},{96,128},{112,144}... | collective-permute-start | bytes 2408456 | tf_op jit(solution)/shard_map/ppermute | solution.py:109
  158.1 28.3 %collective-permute-start.10 = (bf16[2,224,896]{2,1,0:T(8,128)(2,1)S(1)}, bf16[2,224,896]{2,1,0:T(8,128)(2,1)S(1)}, u32[]{:S(2)}, u32[]{:S(2)}) collective-permute-start(bf16[2,224,896]{2,1,0:T(8,128)(2,1)S(1)} %collective-permute-done.8), channel_id=1, source_target_pairs={{0,224},{16,240},{32,0},{48,16},{64,32},{80,48},{96,64},{112,80},{... | collective-permute-start | bytes 2408456 | tf_op jit(solution)/shard_map/ppermute | solution.py:109
  183.5 16.2 %collective-permute-start.27 = (bf16[2,224,896]{2,1,0:T(8,128)(2,1)S(1)}, bf16[2,224,896]{2,1,0:T(8,128)(2,1)S(1)}, u32[]{:S(2)}, u32[]{:S(2)}) collective-permute-start(bf16[2,224,896]{2,1,0:T(8,128)(2,1)S(1)} %collective-permute-done.11), channel_id=1, source_target_pairs={{0,32},{16,48},{32,64},{48,80},{64,96},{80,112},{96,128},{112,144}... | collective-permute-start | bytes 2408456 | tf_op jit(solution)/shard_map/ppermute | solution.py:109
  186.4 15.4 %collective-permute-start.28 = (bf16[2,224,896]{2,1,0:T(8,128)(2,1)S(1)}, bf16[2,224,896]{2,1,0:T(8,128)(2,1)S(1)}, u32[]{:S(2)}, u32[]{:S(2)}) collective-permute-start(bf16[2,224,896]{2,1,0:T(8,128)(2,1)S(1)} %collective-permute-done.10), channel_id=1, source_target_pairs={{0,224},{16,240},{32,0},{48,16},{64,32},{80,48},{96,64},{112,80},{... | collective-permute-start | bytes 2408456 | tf_op jit(solution)/shard_map/ppermute | solution.py:109
  (9 other events, 53.5 us)

commit v4 on v3

--- a/solution.py
+++ b/solution.py
@@ -12,20 +12,29 @@
 
 ROUNDS = (
     ((0, 0), (0, 0), (0, 0)),
-    ((1, 0), (-1, 0), (1, 0)),
-    ((2, 0), (-2, 0), (-2, 0)),
-    ((3, 0), (-2, 1), (2, 0)),
-    ((2, 1), (-3, 1), (-1, 0)),
+    ((1, 0), (1, 0), (-1, 0)),
+    ((-2, 0), (2, 0), (-2, 0)),
+    ((2, 0), (3, 0), (-2, 1)),
+    ((-1, 0), (2, 1), (-3, 1)),
 )
-UP = [(z * H + h, (z + 1) % Z * H + h) for z in range(Z) for h in range(H)]
-DOWN = [(z * H + h, (z - 1) % Z * H + h) for z in range(Z) for h in range(H)]
-ACROSS = [(z * H + h, z * H + 1 - h) for z in range(Z) for h in range(H)]
-HOPS = (UP, DOWN, ACROSS)
+
+
+def along(step):
+    pairs = []
+    for i in range(256):
+        z, h, c = i // 32, i // 16 % H, i % 16
+        pairs.append((i, ((z + (-step if c % 2 else step)) % Z * H + h) * 16 + c))
+    return ("fsdp", "cols"), pairs
+
+
+ACROSS = "fsdp", [(i, i ^ 1) for i in range(16)]
+HOPS = (ACROSS, along(1), along(-1))
+TURNS = ((1, 0, 2), (2, 0, 1))
 
 
 def reached(direction, place):
     dz, h = place
-    return ((dz + 1, h), (dz - 1, h), (dz, 1 - h))[direction]
+    return ((dz, 1 - h), (dz + 1, h), (dz - 1, h))[direction]
 
 
 def merged(base, low, high):
@@ -43,6 +52,52 @@
     ("fsdp", (2, 4, 6)),
     ("fsdp", (8,)),
 )
+
+
+def merge_kernel(base_hbm, lhs_hbm, rhs_hbm, out_ref, base, lhs, rhs, sems):
+    loads = [
+        pltpu.make_async_copy(lhs_hbm, lhs, sems.at[0]),
+        pltpu.make_async_copy(rhs_hbm, rhs, sems.at[1]),
+    ]
+    parts = (slice(0, 384), slice(384, COLS))
+    for i, part in enumerate(parts):
+        loads.append(
+            pltpu.make_async_copy(
+                base_hbm.at[:, part], base.at[:, part], sems.at[2 + i]
+            )
+        )
+    for load in loads:
+        load.start()
+    loads[0].wait()
+    loads[1].wait()
+    for i, part in enumerate(parts):
+        added = lax.dot_general(
+            lhs[...],
+            rhs[:, part],
+            (((0,), (0,)), ((), ())),
+            preferred_element_type=jnp.float32,
+        )
+        loads[2 + i].wait()
+        out_ref[0, :, part] = (
+            base[:, part].astype(jnp.float32) + mix_rate * added
+        ).astype(jnp.bfloat16)
+
+
+def merged_by_kernel(base, lhs, rhs):
+    operands = (base, lhs, rhs)
+    return pl.pallas_call(
+        merge_kernel,
+        in_specs=[pl.BlockSpec(memory_space=pltpu.HBM)] * 3,
+        out_specs=pl.BlockSpec(memory_space=pltpu.VMEM),
+        out_shape=pltpu.VMEM((1, ROWS, COLS), jnp.bfloat16),
+        scratch_shapes=[pltpu.VMEM(x.shape, x.dtype) for x in operands]
+        + [pltpu.SemaphoreType.DMA((4,))],
+        compiler_params=pltpu.CompilerParams(vmem_limit_bytes=8 << 20),
+        cost_estimate=pl.CostEstimate(
+            flops=2 * ROWS * COLS * 16, bytes_accessed=1 << 20, transcendentals=0
+        ),
+        name="merge",
+    )(*(pltpu.with_memory_space_constraint(x, pltpu.HBM) for x in operands))
 
 
 def flipped(name, bits):
@@ -80,12 +135,15 @@
     norm_step,
 ):
     me = lax.axis_index("fsdp").astype(jnp.uint32)
+    core = lax.axis_index("cols").astype(jnp.uint32) & 1
+    back = 1 - 2 * core
 
     def slot(place):
-        return (((me >> 1) + (Z - place[0])) & 7) * 2 + ((me & 1) ^ place[1])
+        z = ((me >> 1) + back * (Z - place[0])) & (Z - 1)
+        return z * H + ((me & 1) ^ place[1])
 
     serve_norm = gather_norm(norm_train, norm_step)
-    own_down = merged(train_down.T, high_down.T, low_down.T)[None]
+    own_down = merged_by_kernel(train_down.T, high_down, low_down.T)
     own_rest = jnp.stack(
         [
             merged(train_gate, low_gate, high_gate),
@@ -106,9 +164,17 @@
     for number, senders in enumerate(ROUNDS):
         for k in range(2):
             for direction, place in enumerate(senders):
-                got = lax.ppermute(held[k][place], "fsdp", HOPS[direction])
-                there = reached(direction, place)
-                held[k][there] = got
+                got = lax.ppermute(held[k][place], *HOPS[direction])
+                held[k][reached(direction, place)] = got
+            if (number, k) == (4, 1):
+                there = [reached(d, place) for d, place in enumerate(senders)]
+                gate, up = put_last(
+                    gate, up, [held[1][t] for t in there], [slot(t) for t in there]
+                )
+                break
+            for direction in TURNS[0]:
+                there = reached(direction, senders[direction])
+                got = held[k][there]
                 if k == 0:
                     down = put(down, got, there)
                 else:
@@ -122,6 +188,36 @@
                 )
                 gate, up, down = lax.optimization_barrier((gate, up, down))
     return gate.reshape(3584, COLS), up.reshape(3584, COLS), down, serve_norm
+
+
+def put_last_kernel(slots, *refs):
+    pieces, stacks, sems = refs[2:5], refs[5:7], refs[7]
+    copies = [
+        pltpu.make_async_copy(piece.at[i], stack.at[slots[d]], sems.at[d, i])
+        for d, piece in enumerate(pieces)
+        for i, stack in enumerate(stacks)
+    ]
+    for copy in copies:
+        copy.start()
+    for copy in copies:
+        copy.wait()
+
+
+def put_last(gate, up, pieces, slots):
+    anywhere = pl.BlockSpec(memory_space=pl.ANY)
+    return pl.pallas_call(
+        put_last_kernel,
+        in_specs=[pl.BlockSpec(memory_space=pltpu.SMEM)] + [anywhere] * 5,
+        out_specs=[anywhere] * 2,
+        out_shape=[jax.ShapeDtypeStruct(x.shape, x.dtype) for x in (gate, up)],
+        input_output_aliases={1: 0, 2: 1},
+        scratch_shapes=[pltpu.SemaphoreType.DMA((3, 2))],
+        compiler_params=pltpu.CompilerParams(vmem_limit_bytes=1 << 20),
+        cost_estimate=pl.CostEstimate(
+            flops=1 << 20, bytes_accessed=12 * ROWS * COLS * 2, transcendentals=0
+        ),
+        name="put_last",
+    )(jnp.stack(slots).astype(jnp.int32), gate, up, *pieces)
 
 
 def empty(count):

time: 204 us -> 185 us (0.907)
  the two profiles are of different devices: /device:TPU:24 before, /device:TPU:36 now
where the time goes in v4:
time: 185 us
  starting transfers between devices  72.5 us (39%)
  waiting for transfers between devices  67.4 us (36%)
  local copies, waits for them, and re-layouts  27.3 us (15%)
  Pallas kernels  12.2 us (7%)
  matrix products  2.64 us (1%)
    ppermute x30, starting transfers between devices, per_device(): got = lax.ppermute(held[k][place], *HOPS[direction])  57.6 us
    ppermute x30, waiting for transfers between devices, per_device(): got = lax.ppermute(held[k][place], *HOPS[direction])  54.9 us
    dynamic_update_slice x29, local copies, waits for them, and re-layouts, put(): return lax.dynamic_update_slice(stack, piece, (slot(place), zero, zero))  26.9 us
    ppermute x10, starting transfers between devices, gather_norm(): got.append(lax.ppermute(total, *flipped(name, bits)))  14.9 us
    ppermute x10, waiting for transfers between devices, gather_norm(): got.append(lax.ppermute(total, *flipped(name, bits)))  12.5 us
    pallas_call x1, Pallas kernels, turned(): pl.pallas_call(turn_kernel, grid=(rows // 512,), in_specs=[pl.BlockSpec((...  8.83 us
  transfers between devices with their start and end apart: 40, of which 16 were waited for; matrix products, arithmetic and copies ran while one was open for 16% of the time, Pallas kernels for 6%

profile of v4, /device:TPU:36, one launch (start us, length us, event | category | flops | bytes accessed | tf_op | source)
XLA Modules:
  0.0 184.5 jit_solution(13034277886732291008)
XLA Ops:
  4.3 2.5 %collective-permute-done.31 = bf16[3584]{0:T(1024)(128)(2,1)S(1)} collective-permute-done((bf16[3584]{0:T(1024)(128)(2,1)S(1)}, bf16[3584]{0:T(1024)(128)(2,1)S(1)}, u32[]{:S(2)}, u32[]{:S(2)}) %collective-permute-start.31) | collective-permute-done | bytes 7200 | tf_op jit(solution)/shard_map/ppermute | solution.py:119
  8.6 3.3 %collective-permute-done.32 = bf16[3584]{0:T(1024)(128)(2,1)S(1)} collective-permute-done((bf16[3584]{0:T(1024)(128)(2,1)S(1)}, bf16[3584]{0:T(1024)(128)(2,1)S(1)}, u32[]{:S(2)}, u32[]{:S(2)}) %collective-permute-start.32) | collective-permute-done | bytes 7200 | tf_op jit(solution)/shard_map/ppermute | solution.py:119
  13.5 2.9 %collective-permute-start.34 = (bf16[3584]{0:T(1024)(128)(2,1)S(1)}, bf16[3584]{0:T(1024)(128)(2,1)S(1)}, u32[]{:S(2)}, u32[]{:S(2)}) collective-permute-start(bf16[3584]{0:T(1024)(128)(2,1)S(1)} %add.214), channel_id=1, source_target_pairs={{0,16},{1,17},{2,18},{3,19},{4,20},{5,21},{6,22},{7,23},{8,24},{9,... | collective-permute-start | bytes 21512 | tf_op jit(solution)/shard_map/ppermute | solution.py:119
  18.6 2.6 %collective-permute-done.35 = bf16[3584]{0:T(1024)(128)(2,1)S(1)} collective-permute-done((bf16[3584]{0:T(1024)(128)(2,1)S(1)}, bf16[3584]{0:T(1024)(128)(2,1)S(1)}, u32[]{:S(2)}, u32[]{:S(2)}) %collective-permute-start.35) | collective-permute-done | bytes 7200 | tf_op jit(solution)/shard_map/ppermute | solution.py:119
  21.3 3.3 %collective-permute-start.37 = (bf16[3584]{0:T(1024)(128)(2,1)S(1)}, bf16[3584]{0:T(1024)(128)(2,1)S(1)}, u32[]{:S(2)}, u32[]{:S(2)}) collective-permute-start(bf16[3584]{0:T(1024)(128)(2,1)S(1)} %add_add_fusion.1), channel_id=1, source_target_pairs={{0,64},{16,80},{32,96},{48,112},{64,0},{80,16},{96,32},{112,48},{1... | collective-permute-start | bytes 21512 | tf_op jit(solution)/shard_map/ppermute | solution.py:119
  28.5 2.9 %collective-permute-start.12 = (bf16[1,224,896]{2,1,0:T(8,128)(2,1)S(1)}, bf16[1,224,896]{2,1,0:T(8,128)(2,1)}, u32[]{:S(2)}, u32[]{:S(2)}) collective-permute-start(bf16[1,224,896]{2,1,0:T(8,128)(2,1)S(1)} %merge.1), channel_id=1, source_target_pairs={{0,32},{1,225},{2,34},{3,227},{4,36},{5,229},{6,38},{7,231},{8,40}... | collective-permute-start | bytes 1204232 | tf_op jit(solution)/shard_map/ppermute | solution.py:167
  31.4 3.1 %collective-permute-start.13 = (bf16[1,224,896]{2,1,0:T(8,128)(2,1)S(1)}, bf16[1,224,896]{2,1,0:T(8,128)(2,1)}, u32[]{:S(2)}, u32[]{:S(2)}) collective-permute-start(bf16[1,224,896]{2,1,0:T(8,128)(2,1)S(1)} %merge.1), channel_id=1, source_target_pairs={{0,16},{16,0},{32,48},{48,32},{64,80},{80,64},{96,112},{112,96},{1... | collective-permute-start | bytes 1204232 | tf_op jit(solution)/shard_map/ppermute | solution.py:167
  34.6 4.6 %collective-permute-start.39 = (bf16[3584]{0:T(1024)(128)(2,1)S(1)}, bf16[3584]{0:T(1024)(128)(2,1)S(1)}, u32[]{:S(2)}, u32[]{:S(2)}) collective-permute-start(bf16[3584]{0:T(1024)(128)(2,1)S(1)} %add_add_fusion), channel_id=1, source_target_pairs={{0,128},{16,144},{32,160},{48,176},{64,192},{80,208},{96,224},{112... | collective-permute-start | bytes 21512 | tf_op jit(solution)/shard_map/ppermute | solution.py:119
  40.1 2.2 %collective-permute-done.39 = bf16[3584]{0:T(1024)(128)(2,1)S(1)} collective-permute-done((bf16[3584]{0:T(1024)(128)(2,1)S(1)}, bf16[3584]{0:T(1024)(128)(2,1)S(1)}, u32[]{:S(2)}, u32[]{:S(2)}) %collective-permute-start.39) | collective-permute-done | bytes 7200 | tf_op jit(solution)/shard_map/ppermute | solution.py:119
  42.3 8.9 %collective-permute-start.14 = (bf16[1,224,896]{2,1,0:T(8,128)(2,1)S(1)}, bf16[1,224,896]{2,1,0:T(8,128)(2,1)S(1)}, u32[]{:S(2)}, u32[]{:S(2)}) collective-permute-start(bf16[1,224,896]{2,1,0:T(8,128)(2,1)S(1)} %merge.1), channel_id=1, source_target_pairs={{0,224},{1,33},{2,226},{3,35},{4,228},{5,37},{6,230},{7,39},{8,232... | collective-permute-start | bytes 1204232 | tf_op jit(solution)/shard_map/ppermute | solution.py:167
  52.7 1.8 constant_dynamic-update-slice_fusion.14
  54.5 2.0 %collective-permute-start.15 = (bf16[1,224,896]{2,1,0:T(8,128)(2,1)}, bf16[1,224,896]{2,1,0:T(8,128)(2,1)S(1)}, u32[]{:S(2)}, u32[]{:S(2)}) collective-permute-start(bf16[1,224,896]{2,1,0:T(8,128)(2,1)} %collective-permute-done.12), channel_id=1, source_target_pairs={{0,32},{1,225},{2,34},{3,227},{4,36},{5,229},{6,38},{7,231},{8,40}... | collective-permute-start | bytes 1204232 | tf_op jit(solution)/shard_map/ppermute | solution.py:167
  61.7 2.3 %collective-permute-start.3 = (bf16[2,224,896]{2,1,0:T(8,128)(2,1)S(1)}, bf16[2,224,896]{2,1,0:T(8,128)(2,1)S(1)}, u32[]{:S(2)}, u32[]{:S(2)}) collective-permute-start(bf16[2,224,896]{2,1,0:T(8,128)(2,1)S(1)} %collective-permute-done), channel_id=1, source_target_pairs={{0,32},{1,225},{2,34},{3,227},{4,36},{5,229},{6,38},{7,231},{8,40}... | collective-permute-start | bytes 2408456 | tf_op jit(solution)/shard_map/ppermute | solution.py:167
  64.9 9.7 %collective-permute-done.2 = bf16[2,224,896]{2,1,0:T(8,128)(2,1)S(1)} collective-permute-done((bf16[2,224,896]{2,1,0:T(8,128)(2,1)S(1)}, bf16[2,224,896]{2,1,0:T(8,128)(2,1)S(1)}, u32[]{:S(2)}, u32[]{:S(2)}) %collective-permute-start.2) | collective-permute-done | bytes 802848 | tf_op jit(solution)/shard_map/ppermute | solution.py:167
  74.7 4.8 %collective-permute-start.18 = (bf16[1,224,896]{2,1,0:T(8,128)(2,1)S(1)}, bf16[1,224,896]{2,1,0:T(8,128)(2,1)S(1)}, u32[]{:S(2)}, u32[]{:S(2)}) collective-permute-start(bf16[1,224,896]{2,1,0:T(8,128)(2,1)S(1)} %collective-permute-done.15), channel_id=1, source_target_pairs={{0,32},{1,225},{2,34},{3,227},{4,36},{5,229},{6,38},{7,231},{8,40}... | collective-permute-start | bytes 1204232 | tf_op jit(solution)/shard_map/ppermute | solution.py:167
  79.5 3.8 %collective-permute-done.17 = bf16[1,224,896]{2,1,0:T(8,128)(2,1)S(1)} collective-permute-done((bf16[1,224,896]{2,1,0:T(8,128)(2,1)S(1)}, bf16[1,224,896]{2,1,0:T(8,128)(2,1)S(1)}, u32[]{:S(2)}, u32[]{:S(2)}) %collective-permute-start.17) | collective-permute-done | bytes 401440 | tf_op jit(solution)/shard_map/ppermute | solution.py:167
  85.0 2.5 %collective-permute-start.20 = (bf16[1,224,896]{2,1,0:T(8,128)(2,1)S(1)}, bf16[1,224,896]{2,1,0:T(8,128)(2,1)S(1)}, u32[]{:S(2)}, u32[]{:S(2)}) collective-permute-start(bf16[1,224,896]{2,1,0:T(8,128)(2,1)S(1)} %collective-permute-done.17), channel_id=1, source_target_pairs={{0,224},{1,33},{2,226},{3,35},{4,228},{5,37},{6,230},{7,39},{8,232... | collective-permute-start | bytes 1204232 | tf_op jit(solution)/shard_map/ppermute | solution.py:167
  90.8 8.8 %collective-permute-done.19 = bf16[1,224,896]{2,1,0:T(8,128)(2,1)S(1)} collective-permute-done((bf16[1,224,896]{2,1,0:T(8,128)(2,1)S(1)}, bf16[1,224,896]{2,1,0:T(8,128)(2,1)S(1)}, u32[]{:S(2)}, u32[]{:S(2)}) %collective-permute-start.19) | collective-permute-done | bytes 401440 | tf_op jit(solution)/shard_map/ppermute | solution.py:167
  102.0 1.9 %collective-permute-start.25 = (bf16[1,224,896]{2,1,0:T(8,128)(2,1)S(1)}, bf16[1,224,896]{2,1,0:T(8,128)(2,1)S(1)}, u32[]{:S(2)}, u32[]{:S(2)}) collective-permute-start(bf16[1,224,896]{2,1,0:T(8,128)(2,1)S(1)} %collective-permute-done.14), channel_id=1, source_target_pairs={{0,16},{16,0},{32,48},{48,32},{64,80},{80,64},{96,112},{112,96},{1... | collective-permute-start | bytes 1204232 | tf_op jit(solution)/shard_map/ppermute | solution.py:167
  104.7 4.2 %collective-permute-start.21 = (bf16[1,224,896]{2,1,0:T(8,128)(2,1)S(1)}, bf16[1,224,896]{2,1,0:T(8,128)(2,1)S(1)}, u32[]{:S(2)}, u32[]{:S(2)}) collective-permute-start(bf16[1,224,896]{2,1,0:T(8,128)(2,1)S(1)} %collective-permute-done.18), channel_id=1, source_target_pairs={{0,32},{1,225},{2,34},{3,227},{4,36},{5,229},{6,38},{7,231},{8,40}... | collective-permute-start | bytes 1204232 | tf_op jit(solution)/shard_map/ppermute | solution.py:167
  110.3 7.1 %collective-permute-start.24 = (bf16[1,224,896]{2,1,0:T(8,128)(2,1)S(1)}, bf16[1,224,896]{2,1,0:T(8,128)(2,1)S(1)}, u32[]{:S(2)}, u32[]{:S(2)}) collective-permute-start(bf16[1,224,896]{2,1,0:T(8,128)(2,1)S(1)} %collective-permute-done.22), channel_id=1, source_target_pairs={{0,32},{1,225},{2,34},{3,227},{4,36},{5,229},{6,38},{7,231},{8,40}... | collective-permute-start | bytes 1204232 | tf_op jit(solution)/shard_map/ppermute | solution.py:167
  118.4 2.0 %collective-permute-start.6 = (bf16[2,224,896]{2,1,0:T(8,128)(2,1)S(1)}, bf16[2,224,896]{2,1,0:T(8,128)(2,1)S(1)}, u32[]{:S(2)}, u32[]{:S(2)}) collective-permute-start(bf16[2,224,896]{2,1,0:T(8,128)(2,1)S(1)} %collective-permute-done.3), channel_id=1, source_target_pairs={{0,32},{1,225},{2,34},{3,227},{4,36},{5,229},{6,38},{7,231},{8,40}... | collective-permute-start | bytes 2408456 | tf_op jit(solution)/shard_map/ppermute | solution.py:167
  123.4 3.5 %collective-permute-start.27 = (bf16[2,224,896]{2,1,0:T(8,128)(2,1)S(1)}, bf16[2,224,896]{2,1,0:T(8,128)(2,1)S(1)}, u32[]{:S(2)}, u32[]{:S(2)}) collective-permute-start(bf16[2,224,896]{2,1,0:T(8,128)(2,1)S(1)} %collective-permute-done.2), channel_id=1, source_target_pairs={{0,16},{16,0},{32,48},{48,32},{64,80},{80,64},{96,112},{112,96},{1... | collective-permute-start | bytes 2408456 | tf_op jit(solution)/shard_map/ppermute | solution.py:167
  130.3 9.6 %collective-permute-done.26 = bf16[1,224,896]{2,1,0:T(8,128)(2,1)S(1)} collective-permute-done((bf16[1,224,896]{2,1,0:T(8,128)(2,1)S(1)}, bf16[1,224,896]{2,1,0:T(8,128)(2,1)S(1)}, u32[]{:S(2)}, u32[]{:S(2)}) %collective-permute-start.26) | collective-permute-done | bytes 401440 | tf_op jit(solution)/shard_map/ppermute | solution.py:167
  140.7 3.6 %collective-permute-done.6 = bf16[2,224,896]{2,1,0:T(8,128)(2,1)S(1)} collective-permute-done((bf16[2,224,896]{2,1,0:T(8,128)(2,1)S(1)}, bf16[2,224,896]{2,1,0:T(8,128)(2,1)S(1)}, u32[]{:S(2)}, u32[]{:S(2)}) %collective-permute-start.6) | collective-permute-done | bytes 802848 | tf_op jit(solution)/shard_map/ppermute | solution.py:167
  144.3 2.5 %collective-permute-start.9 = (bf16[2,224,896]{2,1,0:T(8,128)(2,1)S(1)}, bf16[2,224,896]{2,1,0:T(8,128)(2,1)S(1)}, u32[]{:S(2)}, u32[]{:S(2)}) collective-permute-start(bf16[2,224,896]{2,1,0:T(8,128)(2,1)S(1)} %collective-permute-done.6), channel_id=1, source_target_pairs={{0,32},{1,225},{2,34},{3,227},{4,36},{5,229},{6,38},{7,231},{8,40}... | collective-permute-start | bytes 2408456 | tf_op jit(solution)/shard_map/ppermute | solution.py:167
  146.8 8.8 %turn.1 = bf16[896,3584]{1,0:T(8,128)(2,1)} custom-call(bf16[3584,896]{1,0:T(8,128)(2,1)} %bitcast.20), custom_call_target="tpu_custom_call" | custom-call | flops 8589934592 | bytes 12845056 | tf_op jit(solution)/shard_map/turn/pallas_call | solution.py:241
  155.7 9.2 %collective-permute-done.10 = bf16[2,224,896]{2,1,0:T(8,128)(2,1)S(1)} collective-permute-done((bf16[2,224,896]{2,1,0:T(8,128)(2,1)S(1)}, bf16[2,224,896]{2,1,0:T(8,128)(2,1)S(1)}, u32[]{:S(2)}, u32[]{:S(2)}) %collective-permute-start.10) | collective-permute-done | bytes 802848 | tf_op jit(solution)/shard_map/ppermute | solution.py:167
  164.9 3.4 %collective-permute-start.28 = (bf16[2,224,896]{2,1,0:T(8,128)(2,1)S(1)}, bf16[2,224,896]{2,1,0:T(8,128)(2,1)S(1)}, u32[]{:S(2)}, u32[]{:S(2)}) collective-permute-start(bf16[2,224,896]{2,1,0:T(8,128)(2,1)S(1)} %collective-permute-done.10), channel_id=1, source_target_pairs={{0,32},{1,225},{2,34},{3,227},{4,36},{5,229},{6,38},{7,231},{8,40}... | collective-permute-start | bytes 2408456 | tf_op jit(solution)/shard_map/ppermute | solution.py:167
  174.0 4.2 %collective-permute-done.28.refs_3_ = bf16[2,224,896]{2,1,0:T(8,128)(2,1)S(1)} collective-permute-done((bf16[2,224,896]{2,1,0:T(8,128)(2,1)S(1)}, bf16[2,224,896]{2,1,0:T(8,128)(2,1)S(1)}, u32[]{:S(2)}, u32[]{:S(2)}) %collective-permute-start.28) | collective-permute-done | bytes 802848 | tf_op jit(solution)/shard_map/ppermute | solution.py:167
  178.2 4.1 %collective-permute-done.29.refs_4_ = bf16[2,224,896]{2,1,0:T(8,128)(2,1)S(1)} collective-permute-done((bf16[2,224,896]{2,1,0:T(8,128)(2,1)S(1)}, bf16[2,224,896]{2,1,0:T(8,128)(2,1)S(1)}, u32[]{:S(2)}, u32[]{:S(2)}) %collective-permute-start.29) | collective-permute-done | bytes 802848 | tf_op jit(solution)/shard_map/ppermute | solution.py:167
  182.3 2.0 %put_last.1 = (bf16[16,224,896]{2,1,0:T(8,128)(2,1)}, bf16[16,224,896]{2,1,0:T(8,128)(2,1)}) custom-call(s32[3]{0:T(128)S(1)} %add_convert_fusion.slots, bf16[16,224,896]{2,1,0:T(8,128)(2,1)} %get-tuple-element.15.refs_0_, bf16[16,224,896]{2,1,0:T(8,128)(2,1)} %get-tuple-element.16.refs_1_, ...), custom_call_target="tpu_custom_call", output_to_operand_aliasing={{0}: (1, {}), {1}: (2, {})} | custom-call | flops 1048576 | bytes 4816896 | tf_op jit(solution)/shard_map/put_last/pallas_call | solution.py:208
  (97 shorter events, 45.3 us)
Async XLA Ops:
  21.3 10.1 %collective-permute-start.37 = (bf16[3584]{0:T(1024)(128)(2,1)S(1)}, bf16[3584]{0:T(1024)(128)(2,1)S(1)}, u32[]{:S(2)}, u32[]{:S(2)}) collective-permute-start(bf16[3584]{0:T(1024)(128)(2,1)S(1)} %add_add_fusion.1), channel_id=1, source_target_pairs={{0,64},{16,80},{32,96},{48,112},{64,0},{80,16},{96,32},{112,48},{1... | collective-permute-start | bytes 21512 | tf_op jit(solution)/shard_map/ppermute | solution.py:119
  24.6 10.0 %collective-permute-start.38 = (bf16[3584]{0:T(1024)(128)(2,1)S(1)}, bf16[3584]{0:T(1024)(128)(2,1)S(1)}, u32[]{:S(2)}, u32[]{:S(2)}) collective-permute-start(bf16[3584]{0:T(1024)(128)(2,1)S(1)} %add_add_fusion.1), channel_id=1, source_target_pairs={{0,96},{16,112},{32,64},{48,80},{64,32},{80,48},{96,0},{112,16},{1... | collective-permute-start | bytes 21512 | tf_op jit(solution)/shard_map/ppermute | solution.py:119
  25.2 34.3 %collective-permute-start = (bf16[2,224,896]{2,1,0:T(8,128)(2,1)S(1)}, bf16[2,224,896]{2,1,0:T(8,128)(2,1)S(1)}, u32[]{:S(2)}, u32[]{:S(2)}) collective-permute-start(bf16[2,224,896]{2,1,0:T(8,128)(2,1)S(1)} %pad_maximum_fusion), channel_id=1, source_target_pairs={{0,32},{1,225},{2,34},{3,227},{4,36},{5,229},{6,38},{7,231},{8,40}... | collective-permute-start | bytes 2408456 | tf_op jit(solution)/shard_map/ppermute | solution.py:167
  26.8 34.9 %collective-permute-start.1 = (bf16[2,224,896]{2,1,0:T(8,128)(2,1)S(1)}, bf16[2,224,896]{2,1,0:T(8,128)(2,1)S(1)}, u32[]{:S(2)}, u32[]{:S(2)}) collective-permute-start(bf16[2,224,896]{2,1,0:T(8,128)(2,1)S(1)} %pad_maximum_fusion), channel_id=1, source_target_pairs={{0,16},{16,0},{32,48},{48,32},{64,80},{80,64},{96,112},{112,96},{1... | collective-permute-start | bytes 2408456 | tf_op jit(solution)/shard_map/ppermute | solution.py:167
  28.5 24.2 %collective-permute-start.12 = (bf16[1,224,896]{2,1,0:T(8,128)(2,1)S(1)}, bf16[1,224,896]{2,1,0:T(8,128)(2,1)}, u32[]{:S(2)}, u32[]{:S(2)}) collective-permute-start(bf16[1,224,896]{2,1,0:T(8,128)(2,1)S(1)} %merge.1), channel_id=1, source_target_pairs={{0,32},{1,225},{2,34},{3,227},{4,36},{5,229},{6,38},{7,231},{8,40}... | collective-permute-start | bytes 1204232 | tf_op jit(solution)/shard_map/ppermute | solution.py:167
  31.4 23.1 %collective-permute-start.13 = (bf16[1,224,896]{2,1,0:T(8,128)(2,1)S(1)}, bf16[1,224,896]{2,1,0:T(8,128)(2,1)}, u32[]{:S(2)}, u32[]{:S(2)}) collective-permute-start(bf16[1,224,896]{2,1,0:T(8,128)(2,1)S(1)} %merge.1), channel_id=1, source_target_pairs={{0,16},{16,0},{32,48},{48,32},{64,80},{80,64},{96,112},{112,96},{1... | collective-permute-start | bytes 1204232 | tf_op jit(solution)/shard_map/ppermute | solution.py:167
  42.3 16.0 %collective-permute-start.14 = (bf16[1,224,896]{2,1,0:T(8,128)(2,1)S(1)}, bf16[1,224,896]{2,1,0:T(8,128)(2,1)S(1)}, u32[]{:S(2)}, u32[]{:S(2)}) collective-permute-start(bf16[1,224,896]{2,1,0:T(8,128)(2,1)S(1)} %merge.1), channel_id=1, source_target_pairs={{0,224},{1,33},{2,226},{3,35},{4,228},{5,37},{6,230},{7,39},{8,232... | collective-permute-start | bytes 1204232 | tf_op jit(solution)/shard_map/ppermute | solution.py:167
  52.7 22.0 %collective-permute-start.2 = (bf16[2,224,896]{2,1,0:T(8,128)(2,1)S(1)}, bf16[2,224,896]{2,1,0:T(8,128)(2,1)S(1)}, u32[]{:S(2)}, u32[]{:S(2)}) collective-permute-start(bf16[2,224,896]{2,1,0:T(8,128)(2,1)S(1)} %pad_maximum_fusion), channel_id=1, source_target_pairs={{0,224},{1,33},{2,226},{3,35},{4,228},{5,37},{6,230},{7,39},{8,232... | collective-permute-start | bytes 2408456 | tf_op jit(solution)/shard_map/ppermute | solution.py:167
  54.5 20.2 %collective-permute-start.15 = (bf16[1,224,896]{2,1,0:T(8,128)(2,1)}, bf16[1,224,896]{2,1,0:T(8,128)(2,1)S(1)}, u32[]{:S(2)}, u32[]{:S(2)}) collective-permute-start(bf16[1,224,896]{2,1,0:T(8,128)(2,1)} %collective-permute-done.12), channel_id=1, source_target_pairs={{0,32},{1,225},{2,34},{3,227},{4,36},{5,229},{6,38},{7,231},{8,40}... | collective-permute-start | bytes 1204232 | tf_op jit(solution)/shard_map/ppermute | solution.py:167
  58.3 26.7 %collective-permute-start.16 = (bf16[1,224,896]{2,1,0:T(8,128)(2,1)}, bf16[1,224,896]{2,1,0:T(8,128)(2,1)S(1)}, u32[]{:S(2)}, u32[]{:S(2)}) collective-permute-start(bf16[1,224,896]{2,1,0:T(8,128)(2,1)} %collective-permute-done.12), channel_id=1, source_target_pairs={{0,16},{16,0},{32,48},{48,32},{64,80},{80,64},{96,112},{112,96},{1... | collective-permute-start | bytes 1204232 | tf_op jit(solution)/shard_map/ppermute | solution.py:167
  59.4 23.8 %collective-permute-start.17 = (bf16[1,224,896]{2,1,0:T(8,128)(2,1)S(1)}, bf16[1,224,896]{2,1,0:T(8,128)(2,1)S(1)}, u32[]{:S(2)}, u32[]{:S(2)}) collective-permute-start(bf16[1,224,896]{2,1,0:T(8,128)(2,1)S(1)} %collective-permute-done.14), channel_id=1, source_target_pairs={{0,224},{1,33},{2,226},{3,35},{4,228},{5,37},{6,230},{7,39},{8,232... | collective-permute-start | bytes 1204232 | tf_op jit(solution)/shard_map/ppermute | solution.py:167
  61.7 43.0 %collective-permute-start.3 = (bf16[2,224,896]{2,1,0:T(8,128)(2,1)S(1)}, bf16[2,224,896]{2,1,0:T(8,128)(2,1)S(1)}, u32[]{:S(2)}, u32[]{:S(2)}) collective-permute-start(bf16[2,224,896]{2,1,0:T(8,128)(2,1)S(1)} %collective-permute-done), channel_id=1, source_target_pairs={{0,32},{1,225},{2,34},{3,227},{4,36},{5,229},{6,38},{7,231},{8,40}... | collective-permute-start | bytes 2408456 | tf_op jit(solution)/shard_map/ppermute | solution.py:167
  74.7 35.7 %collective-permute-start.4 = (bf16[2,224,896]{2,1,0:T(8,128)(2,1)S(1)}, bf16[2,224,896]{2,1,0:T(8,128)(2,1)S(1)}, u32[]{:S(2)}, u32[]{:S(2)}) collective-permute-start(bf16[2,224,896]{2,1,0:T(8,128)(2,1)S(1)} %collective-permute-done), channel_id=1, source_target_pairs={{0,16},{16,0},{32,48},{48,32},{64,80},{80,64},{96,112},{112,96},{1... | collective-permute-start | bytes 2408456 | tf_op jit(solution)/shard_map/ppermute | solution.py:167
  74.7 14.4 %collective-permute-start.18 = (bf16[1,224,896]{2,1,0:T(8,128)(2,1)S(1)}, bf16[1,224,896]{2,1,0:T(8,128)(2,1)S(1)}, u32[]{:S(2)}, u32[]{:S(2)}) collective-permute-start(bf16[1,224,896]{2,1,0:T(8,128)(2,1)S(1)} %collective-permute-done.15), channel_id=1, source_target_pairs={{0,32},{1,225},{2,34},{3,227},{4,36},{5,229},{6,38},{7,231},{8,40}... | collective-permute-start | bytes 1204232 | tf_op jit(solution)/shard_map/ppermute | solution.py:167
  83.3 16.3 %collective-permute-start.19 = (bf16[1,224,896]{2,1,0:T(8,128)(2,1)S(1)}, bf16[1,224,896]{2,1,0:T(8,128)(2,1)S(1)}, u32[]{:S(2)}, u32[]{:S(2)}) collective-permute-start(bf16[1,224,896]{2,1,0:T(8,128)(2,1)S(1)} %collective-permute-done.17), channel_id=1, source_target_pairs={{0,16},{16,0},{32,48},{48,32},{64,80},{80,64},{96,112},{112,96},{1... | collective-permute-start | bytes 1204232 | tf_op jit(solution)/shard_map/ppermute | solution.py:167
  85.0 17.0 %collective-permute-start.20 = (bf16[1,224,896]{2,1,0:T(8,128)(2,1)S(1)}, bf16[1,224,896]{2,1,0:T(8,128)(2,1)S(1)}, u32[]{:S(2)}, u32[]{:S(2)}) collective-permute-start(bf16[1,224,896]{2,1,0:T(8,128)(2,1)S(1)} %collective-permute-done.17), channel_id=1, source_target_pairs={{0,224},{1,33},{2,226},{3,35},{4,228},{5,37},{6,230},{7,39},{8,232... | collective-permute-start | bytes 1204232 | tf_op jit(solution)/shard_map/ppermute | solution.py:167
  89.1 29.3 %collective-permute-start.5 = (bf16[2,224,896]{2,1,0:T(8,128)(2,1)S(1)}, bf16[2,224,896]{2,1,0:T(8,128)(2,1)S(1)}, u32[]{:S(2)}, u32[]{:S(2)}) collective-permute-start(bf16[2,224,896]{2,1,0:T(8,128)(2,1)S(1)} %collective-permute-done.2), channel_id=1, source_target_pairs={{0,224},{1,33},{2,226},{3,35},{4,228},{5,37},{6,230},{7,39},{8,232... | collective-permute-start | bytes 2408456 | tf_op jit(solution)/shard_map/ppermute | solution.py:167
  99.6 10.7 %collective-permute-start.22 = (bf16[1,224,896]{2,1,0:T(8,128)(2,1)S(1)}, bf16[1,224,896]{2,1,0:T(8,128)(2,1)S(1)}, u32[]{:S(2)}, u32[]{:S(2)}) collective-permute-start(bf16[1,224,896]{2,1,0:T(8,128)(2,1)S(1)} %collective-permute-done.15), channel_id=1, source_target_pairs={{0,16},{16,0},{32,48},{48,32},{64,80},{80,64},{96,112},{112,96},{1... | collective-permute-start | bytes 1204232 | tf_op jit(solution)/shard_map/ppermute | solution.py:167
  102.0 26.6 %collective-permute-start.25 = (bf16[1,224,896]{2,1,0:T(8,128)(2,1)S(1)}, bf16[1,224,896]{2,1,0:T(8,128)(2,1)S(1)}, u32[]{:S(2)}, u32[]{:S(2)}) collective-permute-start(bf16[1,224,896]{2,1,0:T(8,128)(2,1)S(1)} %collective-permute-done.14), channel_id=1, source_target_pairs={{0,16},{16,0},{32,48},{48,32},{64,80},{80,64},{96,112},{112,96},{1... | collective-permute-start | bytes 1204232 | tf_op jit(solution)/shard_map/ppermute | solution.py:167
  104.7 15.7 %collective-permute-start.21 = (bf16[1,224,896]{2,1,0:T(8,128)(2,1)S(1)}, bf16[1,224,896]{2,1,0:T(8,128)(2,1)S(1)}, u32[]{:S(2)}, u32[]{:S(2)}) collective-permute-start(bf16[1,224,896]{2,1,0:T(8,128)(2,1)S(1)} %collective-permute-done.18), channel_id=1, source_target_pairs={{0,32},{1,225},{2,34},{3,227},{4,36},{5,229},{6,38},{7,231},{8,40}... | collective-permute-start | bytes 1204232 | tf_op jit(solution)/shard_map/ppermute | solution.py:167
  110.3 13.1 %collective-permute-start.23 = (bf16[1,224,896]{2,1,0:T(8,128)(2,1)S(1)}, bf16[1,224,896]{2,1,0:T(8,128)(2,1)S(1)}, u32[]{:S(2)}, u32[]{:S(2)}) collective-permute-start(bf16[1,224,896]{2,1,0:T(8,128)(2,1)S(1)} %collective-permute-done.19), channel_id=1, source_target_pairs={{0,224},{1,33},{2,226},{3,35},{4,228},{5,37},{6,230},{7,39},{8,232... | collective-permute-start | bytes 1204232 | tf_op jit(solution)/shard_map/ppermute | solution.py:167
  110.3 17.4 %collective-permute-start.24 = (bf16[1,224,896]{2,1,0:T(8,128)(2,1)S(1)}, bf16[1,224,896]{2,1,0:T(8,128)(2,1)S(1)}, u32[]{:S(2)}, u32[]{:S(2)}) collective-permute-start(bf16[1,224,896]{2,1,0:T(8,128)(2,1)S(1)} %collective-permute-done.22), channel_id=1, source_target_pairs={{0,32},{1,225},{2,34},{3,227},{4,36},{5,229},{6,38},{7,231},{8,40}... | collective-permute-start | bytes 1204232 | tf_op jit(solution)/shard_map/ppermute | solution.py:167
  118.4 25.9 %collective-permute-start.6 = (bf16[2,224,896]{2,1,0:T(8,128)(2,1)S(1)}, bf16[2,224,896]{2,1,0:T(8,128)(2,1)S(1)}, u32[]{:S(2)}, u32[]{:S(2)}) collective-permute-start(bf16[2,224,896]{2,1,0:T(8,128)(2,1)S(1)} %collective-permute-done.3), channel_id=1, source_target_pairs={{0,32},{1,225},{2,34},{3,227},{4,36},{5,229},{6,38},{7,231},{8,40}... | collective-permute-start | bytes 2408456 | tf_op jit(solution)/shard_map/ppermute | solution.py:167
  120.4 26.4 %collective-permute-start.7 = (bf16[2,224,896]{2,1,0:T(8,128)(2,1)S(1)}, bf16[2,224,896]{2,1,0:T(8,128)(2,1)S(1)}, u32[]{:S(2)}, u32[]{:S(2)}) collective-permute-start(bf16[2,224,896]{2,1,0:T(8,128)(2,1)S(1)} %collective-permute-done.5), channel_id=1, source_target_pairs={{0,16},{16,0},{32,48},{48,32},{64,80},{80,64},{96,112},{112,96},{1... | collective-permute-start | bytes 2408456 | tf_op jit(solution)/shard_map/ppermute | solution.py:167
  123.4 50.5 %collective-permute-start.27 = (bf16[2,224,896]{2,1,0:T(8,128)(2,1)S(1)}, bf16[2,224,896]{2,1,0:T(8,128)(2,1)S(1)}, u32[]{:S(2)}, u32[]{:S(2)}) collective-permute-start(bf16[2,224,896]{2,1,0:T(8,128)(2,1)S(1)} %collective-permute-done.2), channel_id=1, source_target_pairs={{0,16},{16,0},{32,48},{48,32},{64,80},{80,64},{96,112},{112,96},{1... | collective-permute-start | bytes 2408456 | tf_op jit(solution)/shard_map/ppermute | solution.py:167
  127.8 12.2 %collective-permute-start.26 = (bf16[1,224,896]{2,1,0:T(8,128)(2,1)S(1)}, bf16[1,224,896]{2,1,0:T(8,128)(2,1)S(1)}, u32[]{:S(2)}, u32[]{:S(2)}) collective-permute-start(bf16[1,224,896]{2,1,0:T(8,128)(2,1)S(1)} %collective-permute-done.23), channel_id=1, source_target_pairs={{0,224},{1,33},{2,226},{3,35},{4,228},{5,37},{6,230},{7,39},{8,232... | collective-permute-start | bytes 1204232 | tf_op jit(solution)/shard_map/ppermute | solution.py:167
  128.6 41.6 %collective-permute-start.8 = (bf16[2,224,896]{2,1,0:T(8,128)(2,1)S(1)}, bf16[2,224,896]{2,1,0:T(8,128)(2,1)S(1)}, u32[]{:S(2)}, u32[]{:S(2)}) collective-permute-start(bf16[2,224,896]{2,1,0:T(8,128)(2,1)S(1)} %collective-permute-done.5), channel_id=1, source_target_pairs={{0,224},{1,33},{2,226},{3,35},{4,228},{5,37},{6,230},{7,39},{8,232... | collective-permute-start | bytes 2408456 | tf_op jit(solution)/shard_map/ppermute | solution.py:167
  139.9 24.9 %collective-permute-start.10 = (bf16[2,224,896]{2,1,0:T(8,128)(2,1)S(1)}, bf16[2,224,896]{2,1,0:T(8,128)(2,1)S(1)}, u32[]{:S(2)}, u32[]{:S(2)}) collective-permute-start(bf16[2,224,896]{2,1,0:T(8,128)(2,1)S(1)} %collective-permute-done.3), channel_id=1, source_target_pairs={{0,16},{16,0},{32,48},{48,32},{64,80},{80,64},{96,112},{112,96},{1... | collective-permute-start | bytes 2408456 | tf_op jit(solution)/shard_map/ppermute | solution.py:167
  144.3 26.8 %collective-permute-start.9 = (bf16[2,224,896]{2,1,0:T(8,128)(2,1)S(1)}, bf16[2,224,896]{2,1,0:T(8,128)(2,1)S(1)}, u32[]{:S(2)}, u32[]{:S(2)}) collective-permute-start(bf16[2,224,896]{2,1,0:T(8,128)(2,1)S(1)} %collective-permute-done.6), channel_id=1, source_target_pairs={{0,32},{1,225},{2,34},{3,227},{4,36},{5,229},{6,38},{7,231},{8,40}... | collective-permute-start | bytes 2408456 | tf_op jit(solution)/shard_map/ppermute | solution.py:167
  146.8 23.3 %collective-permute-start.11 = (bf16[2,224,896]{2,1,0:T(8,128)(2,1)S(1)}, bf16[2,224,896]{2,1,0:T(8,128)(2,1)S(1)}, u32[]{:S(2)}, u32[]{:S(2)}) collective-permute-start(bf16[2,224,896]{2,1,0:T(8,128)(2,1)S(1)} %collective-permute-done.7), channel_id=1, source_target_pairs={{0,224},{1,33},{2,226},{3,35},{4,228},{5,37},{6,230},{7,39},{8,232... | collective-permute-start | bytes 2408456 | tf_op jit(solution)/shard_map/ppermute | solution.py:167
  164.9 13.3 %collective-permute-start.28 = (bf16[2,224,896]{2,1,0:T(8,128)(2,1)S(1)}, bf16[2,224,896]{2,1,0:T(8,128)(2,1)S(1)}, u32[]{:S(2)}, u32[]{:S(2)}) collective-permute-start(bf16[2,224,896]{2,1,0:T(8,128)(2,1)S(1)} %collective-permute-done.10), channel_id=1, source_target_pairs={{0,32},{1,225},{2,34},{3,227},{4,36},{5,229},{6,38},{7,231},{8,40}... | collective-permute-start | bytes 2408456 | tf_op jit(solution)/shard_map/ppermute | solution.py:167
  170.2 12.2 %collective-permute-start.29 = (bf16[2,224,896]{2,1,0:T(8,128)(2,1)S(1)}, bf16[2,224,896]{2,1,0:T(8,128)(2,1)S(1)}, u32[]{:S(2)}, u32[]{:S(2)}) collective-permute-start(bf16[2,224,896]{2,1,0:T(8,128)(2,1)S(1)} %collective-permute-done.11), channel_id=1, source_target_pairs={{0,224},{1,33},{2,226},{3,35},{4,228},{5,37},{6,230},{7,39},{8,232... | collective-permute-start | bytes 2408456 | tf_op jit(solution)/shard_map/ppermute | solution.py:167
  (9 other events, 47.8 us)

commit v5 on v4

--- a/solution.py
+++ b/solution.py
@@ -29,7 +29,6 @@
 
 ACROSS = "fsdp", [(i, i ^ 1) for i in range(16)]
 HOPS = (ACROSS, along(1), along(-1))
-TURNS = ((1, 0, 2), (2, 0, 1))
 
 
 def reached(direction, place):
@@ -54,12 +53,12 @@
 )
 
 
-def merge_kernel(base_hbm, lhs_hbm, rhs_hbm, out_ref, base, lhs, rhs, sems):
+def merge_kernel(base_hbm, lhs_hbm, rhs_hbm, out_ref, base, lhs, rhs, added, sems):
     loads = [
         pltpu.make_async_copy(lhs_hbm, lhs, sems.at[0]),
         pltpu.make_async_copy(rhs_hbm, rhs, sems.at[1]),
     ]
-    parts = (slice(0, 384), slice(384, COLS))
+    parts = [slice(at, min(at + 256, COLS)) for at in range(0, COLS, 256)]
     for i, part in enumerate(parts):
         loads.append(
             pltpu.make_async_copy(
@@ -70,16 +69,13 @@
         load.start()
     loads[0].wait()
     loads[1].wait()
+    added[...] = lax.dot_general(
+        lhs[...], rhs[...], (((0,), (0,)), ((), ())), preferred_element_type=jnp.float32
+    )
     for i, part in enumerate(parts):
-        added = lax.dot_general(
-            lhs[...],
-            rhs[:, part],
-            (((0,), (0,)), ((), ())),
-            preferred_element_type=jnp.float32,
-        )
         loads[2 + i].wait()
         out_ref[0, :, part] = (
-            base[:, part].astype(jnp.float32) + mix_rate * added
+            base[:, part].astype(jnp.float32) + mix_rate * added[:, part]
         ).astype(jnp.bfloat16)
 
 
@@ -91,7 +87,7 @@
         out_specs=pl.BlockSpec(memory_space=pltpu.VMEM),
         out_shape=pltpu.VMEM((1, ROWS, COLS), jnp.bfloat16),
         scratch_shapes=[pltpu.VMEM(x.shape, x.dtype) for x in operands]
-        + [pltpu.SemaphoreType.DMA((4,))],
+        + [pltpu.VMEM((ROWS, COLS), jnp.float32), pltpu.SemaphoreType.DMA((6,))],
         compiler_params=pltpu.CompilerParams(vmem_limit_bytes=8 << 20),
         cost_estimate=pl.CostEstimate(
             flops=2 * ROWS * COLS * 16, bytes_accessed=1 << 20, transcendentals=0
@@ -166,13 +162,7 @@
             for direction, place in enumerate(senders):
                 got = lax.ppermute(held[k][place], *HOPS[direction])
                 held[k][reached(direction, place)] = got
-            if (number, k) == (4, 1):
-                there = [reached(d, place) for d, place in enumerate(senders)]
-                gate, up = put_last(
-                    gate, up, [held[1][t] for t in there], [slot(t) for t in there]
-                )
-                break
-            for direction in TURNS[0]:
+            for direction in (2, 0, 1):
                 there = reached(direction, senders[direction])
                 got = held[k][there]
                 if k == 0:
@@ -188,36 +178,6 @@
                 )
                 gate, up, down = lax.optimization_barrier((gate, up, down))
     return gate.reshape(3584, COLS), up.reshape(3584, COLS), down, serve_norm
-
-
-def put_last_kernel(slots, *refs):
-    pieces, stacks, sems = refs[2:5], refs[5:7], refs[7]
-    copies = [
-        pltpu.make_async_copy(piece.at[i], stack.at[slots[d]], sems.at[d, i])
-        for d, piece in enumerate(pieces)
-        for i, stack in enumerate(stacks)
-    ]
-    for copy in copies:
-        copy.start()
-    for copy in copies:
-        copy.wait()
-
-
-def put_last(gate, up, pieces, slots):
-    anywhere = pl.BlockSpec(memory_space=pl.ANY)
-    return pl.pallas_call(
-        put_last_kernel,
-        in_specs=[pl.BlockSpec(memory_space=pltpu.SMEM)] + [anywhere] * 5,
-        out_specs=[anywhere] * 2,
-        out_shape=[jax.ShapeDtypeStruct(x.shape, x.dtype) for x in (gate, up)],
-        input_output_aliases={1: 0, 2: 1},
-        scratch_shapes=[pltpu.SemaphoreType.DMA((3, 2))],
-        compiler_params=pltpu.CompilerParams(vmem_limit_bytes=1 << 20),
-        cost_estimate=pl.CostEstimate(
-            flops=1 << 20, bytes_accessed=12 * ROWS * COLS * 2, transcendentals=0
-        ),
-        name="put_last",
-    )(jnp.stack(slots).astype(jnp.int32), gate, up, *pieces)
 
 
 def empty(count):

time: 185 us -> 190 us (1.027)
  the two profiles are of different devices: /device:TPU:36 before, /device:TPU:1 now
where the time goes in v5:
time: 190 us
  waiting for transfers between devices  90.5 us (48%)
  starting transfers between devices  54.2 us (29%)
  local copies, waits for them, and re-layouts  30.2 us (16%)
  Pallas kernels  10 us (5%)
  matrix products  2.64 us (1%)
    ppermute x30, waiting for transfers between devices, per_device(): got = lax.ppermute(held[k][place], *HOPS[direction])  74.5 us
    ppermute x30, starting transfers between devices, per_device(): got = lax.ppermute(held[k][place], *HOPS[direction])  37.2 us
    dynamic_update_slice x32, local copies, waits for them, and re-layouts, put(): return lax.dynamic_update_slice(stack, piece, (slot(place), zero, zero))  29.7 us
    ppermute x10, starting transfers between devices, gather_norm(): got.append(lax.ppermute(total, *flipped(name, bits)))  17 us
    ppermute x10, waiting for transfers between devices, gather_norm(): got.append(lax.ppermute(total, *flipped(name, bits)))  16 us
    pallas_call x1, Pallas kernels, turned(): pl.pallas_call(turn_kernel, grid=(rows // 512,), in_specs=[pl.BlockSpec((...  8.83 us
  transfers between devices with their start and end apart: 40, of which 15 were waited for; matrix products, arithmetic and copies ran while one was open for 17% of the time, Pallas kernels for 5%

profile of v5, /device:TPU:1, one launch (start us, length us, event | category | flops | bytes accessed | tf_op | source)
XLA Modules:
  0.0 189.8 jit_solution(15005742530192770875)
XLA Ops:
  1.5 3.2 %collective-permute-start.30 = (bf16[3584]{0:T(1024)(128)(2,1)S(1)}, bf16[3584]{0:T(1024)(128)(2,1)S(1)}, u32[]{:S(2)}, u32[]{:S(2)}) collective-permute-start(bf16[3584]{0:T(1024)(128)(2,1)S(1)} %dynamic_update_slice.197), channel_id=1, source_target_pairs={{0,1},{1,0},{2,3},{3,2},{4,5},{5,4},{6,7},{7,6},{8,9},{9,8},{10,11... | collective-permute-start | bytes 21512 | tf_op jit(solution)/shard_map/ppermute | solution.py:115
  5.9 2.5 %collective-permute-done.31 = bf16[3584]{0:T(1024)(128)(2,1)S(1)} collective-permute-done((bf16[3584]{0:T(1024)(128)(2,1)S(1)}, bf16[3584]{0:T(1024)(128)(2,1)S(1)}, u32[]{:S(2)}, u32[]{:S(2)}) %collective-permute-start.31) | collective-permute-done | bytes 7200 | tf_op jit(solution)/shard_map/ppermute | solution.py:115
  10.8 1.6 collective-permute-done.32
  12.4 2.4 %collective-permute-start.34 = (bf16[3584]{0:T(1024)(128)(2,1)S(1)}, bf16[3584]{0:T(1024)(128)(2,1)S(1)}, u32[]{:S(2)}, u32[]{:S(2)}) collective-permute-start(bf16[3584]{0:T(1024)(128)(2,1)S(1)} %add.220), channel_id=1, source_target_pairs={{0,16},{1,17},{2,18},{3,19},{4,20},{5,21},{6,22},{7,23},{8,24},{9,... | collective-permute-start | bytes 21512 | tf_op jit(solution)/shard_map/ppermute | solution.py:115
  18.5 1.6 collective-permute-start.36
  20.2 3.0 %collective-permute-start.37 = (bf16[3584]{0:T(1024)(128)(2,1)S(1)}, bf16[3584]{0:T(1024)(128)(2,1)S(1)}, u32[]{:S(2)}, u32[]{:S(2)}) collective-permute-start(bf16[3584]{0:T(1024)(128)(2,1)S(1)} %add_add_fusion.1), channel_id=1, source_target_pairs={{0,64},{16,80},{32,96},{48,112},{64,0},{80,16},{96,32},{112,48},{1... | collective-permute-start | bytes 21512 | tf_op jit(solution)/shard_map/ppermute | solution.py:115
  27.5 4.2 %collective-permute-start.39 = (bf16[3584]{0:T(1024)(128)(2,1)S(1)}, bf16[3584]{0:T(1024)(128)(2,1)S(1)}, u32[]{:S(2)}, u32[]{:S(2)}) collective-permute-start(bf16[3584]{0:T(1024)(128)(2,1)S(1)} %add_add_fusion), channel_id=1, source_target_pairs={{0,128},{16,144},{32,160},{48,176},{64,192},{80,208},{96,224},{112... | collective-permute-start | bytes 21512 | tf_op jit(solution)/shard_map/ppermute | solution.py:115
  32.1 2.6 %collective-permute-start.13 = (bf16[1,224,896]{2,1,0:T(8,128)(2,1)S(1)}, bf16[1,224,896]{2,1,0:T(8,128)(2,1)}, u32[]{:S(2)}, u32[]{:S(2)}) collective-permute-start(bf16[1,224,896]{2,1,0:T(8,128)(2,1)S(1)} %merge.1), channel_id=1, source_target_pairs={{0,16},{16,0},{32,48},{48,32},{64,80},{80,64},{96,112},{112,96},{1... | collective-permute-start | bytes 1204232 | tf_op jit(solution)/shard_map/ppermute | solution.py:163
  34.6 8.9 %collective-permute-done.39 = bf16[3584]{0:T(1024)(128)(2,1)S(1)} collective-permute-done((bf16[3584]{0:T(1024)(128)(2,1)S(1)}, bf16[3584]{0:T(1024)(128)(2,1)S(1)}, u32[]{:S(2)}, u32[]{:S(2)}) %collective-permute-start.39) | collective-permute-done | bytes 7200 | tf_op jit(solution)/shard_map/ppermute | solution.py:115
  48.0 7.0 %collective-permute-done.13 = bf16[1,224,896]{2,1,0:T(8,128)(2,1)} collective-permute-done((bf16[1,224,896]{2,1,0:T(8,128)(2,1)S(1)}, bf16[1,224,896]{2,1,0:T(8,128)(2,1)}, u32[]{:S(2)}, u32[]{:S(2)}) %collective-permute-start.13) | collective-permute-done | bytes 401440 | tf_op jit(solution)/shard_map/ppermute | solution.py:163
  54.9 2.4 %collective-permute-start.15 = (bf16[1,224,896]{2,1,0:T(8,128)(2,1)S(1)}, bf16[1,224,896]{2,1,0:T(8,128)(2,1)S(1)}, u32[]{:S(2)}, u32[]{:S(2)}) collective-permute-start(bf16[1,224,896]{2,1,0:T(8,128)(2,1)S(1)} %collective-permute-done.12), channel_id=1, source_target_pairs={{0,224},{1,33},{2,226},{3,35},{4,228},{5,37},{6,230},{7,39},{8,232... | collective-permute-start | bytes 1204232 | tf_op jit(solution)/shard_map/ppermute | solution.py:163
  58.0 1.8 constant_dynamic-update-slice_fusion.13
  59.8 1.8 constant_dynamic-update-slice_fusion.12
  61.6 2.5 %collective-permute-start.17 = (bf16[1,224,896]{2,1,0:T(8,128)(2,1)}, bf16[1,224,896]{2,1,0:T(8,128)(2,1)S(1)}, u32[]{:S(2)}, u32[]{:S(2)}) collective-permute-start(bf16[1,224,896]{2,1,0:T(8,128)(2,1)} %collective-permute-done.14), channel_id=1, source_target_pairs={{0,32},{1,225},{2,34},{3,227},{4,36},{5,229},{6,38},{7,231},{8,40}... | collective-permute-start | bytes 1204232 | tf_op jit(solution)/shard_map/ppermute | solution.py:163
  65.0 3.4 %collective-permute-done.15 = bf16[1,224,896]{2,1,0:T(8,128)(2,1)S(1)} collective-permute-done((bf16[1,224,896]{2,1,0:T(8,128)(2,1)S(1)}, bf16[1,224,896]{2,1,0:T(8,128)(2,1)S(1)}, u32[]{:S(2)}, u32[]{:S(2)}) %collective-permute-start.15) | collective-permute-done | bytes 401440 | tf_op jit(solution)/shard_map/ppermute | solution.py:163
  72.6 1.7 collective-permute-start.4
  74.3 2.5 %collective-permute-start.20 = (bf16[1,224,896]{2,1,0:T(8,128)(2,1)S(1)}, bf16[1,224,896]{2,1,0:T(8,128)(2,1)S(1)}, u32[]{:S(2)}, u32[]{:S(2)}) collective-permute-start(bf16[1,224,896]{2,1,0:T(8,128)(2,1)S(1)} %collective-permute-done.17), channel_id=1, source_target_pairs={{0,32},{1,225},{2,34},{3,227},{4,36},{5,229},{6,38},{7,231},{8,40}... | collective-permute-start | bytes 1204232 | tf_op jit(solution)/shard_map/ppermute | solution.py:163
  78.4 12.8 %collective-permute-done.18 = bf16[1,224,896]{2,1,0:T(8,128)(2,1)S(1)} collective-permute-done((bf16[1,224,896]{2,1,0:T(8,128)(2,1)S(1)}, bf16[1,224,896]{2,1,0:T(8,128)(2,1)S(1)}, u32[]{:S(2)}, u32[]{:S(2)}) %collective-permute-start.18) | collective-permute-done | bytes 401440 | tf_op jit(solution)/shard_map/ppermute | solution.py:163
  93.3 2.4 %collective-permute-start.25 = (bf16[1,224,896]{2,1,0:T(8,128)(2,1)S(1)}, bf16[1,224,896]{2,1,0:T(8,128)(2,1)S(1)}, u32[]{:S(2)}, u32[]{:S(2)}) collective-permute-start(bf16[1,224,896]{2,1,0:T(8,128)(2,1)S(1)} %collective-permute-done.12), channel_id=1, source_target_pairs={{0,16},{16,0},{32,48},{48,32},{64,80},{80,64},{96,112},{112,96},{1... | collective-permute-start | bytes 1204232 | tf_op jit(solution)/shard_map/ppermute | solution.py:163
  96.5 1.7 collective-permute-start.21
  99.1 5.6 %collective-permute-done.22 = bf16[1,224,896]{2,1,0:T(8,128)(2,1)S(1)} collective-permute-done((bf16[1,224,896]{2,1,0:T(8,128)(2,1)S(1)}, bf16[1,224,896]{2,1,0:T(8,128)(2,1)S(1)}, u32[]{:S(2)}, u32[]{:S(2)}) %collective-permute-start.22) | collective-permute-done | bytes 401440 | tf_op jit(solution)/shard_map/ppermute | solution.py:163
  105.4 1.7 collective-permute-start.26
  112.1 2.4 %collective-permute-start.28 = (bf16[2,224,896]{2,1,0:T(8,128)(2,1)S(1)}, bf16[2,224,896]{2,1,0:T(8,128)(2,1)S(1)}, u32[]{:S(2)}, u32[]{:S(2)}) collective-permute-start(bf16[2,224,896]{2,1,0:T(8,128)(2,1)S(1)} %collective-permute-done), channel_id=1, source_target_pairs={{0,16},{16,0},{32,48},{48,32},{64,80},{80,64},{96,112},{112,96},{1... | collective-permute-start | bytes 2408456 | tf_op jit(solution)/shard_map/ppermute | solution.py:163
  115.2 2.0 %collective-permute-done.24 = bf16[1,224,896]{2,1,0:T(8,128)(2,1)S(1)} collective-permute-done((bf16[1,224,896]{2,1,0:T(8,128)(2,1)S(1)}, bf16[1,224,896]{2,1,0:T(8,128)(2,1)S(1)}, u32[]{:S(2)}, u32[]{:S(2)}) %collective-permute-start.24) | collective-permute-done | bytes 401440 | tf_op jit(solution)/shard_map/ppermute | solution.py:163
  119.0 1.7 collective-permute-start.8
  121.5 2.0 %collective-permute-start.10 = (bf16[2,224,896]{2,1,0:T(8,128)(2,1)S(1)}, bf16[2,224,896]{2,1,0:T(8,128)(2,1)S(1)}, u32[]{:S(2)}, u32[]{:S(2)}) collective-permute-start(bf16[2,224,896]{2,1,0:T(8,128)(2,1)S(1)} %collective-permute-done.5), channel_id=1, source_target_pairs={{0,16},{16,0},{32,48},{48,32},{64,80},{80,64},{96,112},{112,96},{1... | collective-permute-start | bytes 2408456 | tf_op jit(solution)/shard_map/ppermute | solution.py:163
  124.3 5.2 %collective-permute-done.7 = bf16[2,224,896]{2,1,0:T(8,128)(2,1)S(1)} collective-permute-done((bf16[2,224,896]{2,1,0:T(8,128)(2,1)S(1)}, bf16[2,224,896]{2,1,0:T(8,128)(2,1)S(1)}, u32[]{:S(2)}, u32[]{:S(2)}) %collective-permute-start.7) | collective-permute-done | bytes 802848 | tf_op jit(solution)/shard_map/ppermute | solution.py:163
  129.5 2.7 %collective-permute-start.9 = (bf16[2,224,896]{2,1,0:T(8,128)(2,1)S(1)}, bf16[2,224,896]{2,1,0:T(8,128)(2,1)S(1)}, u32[]{:S(2)}, u32[]{:S(2)}) collective-permute-start(bf16[2,224,896]{2,1,0:T(8,128)(2,1)S(1)} %collective-permute-done.7), channel_id=1, source_target_pairs={{0,224},{1,33},{2,226},{3,35},{4,228},{5,37},{6,230},{7,39},{8,232... | collective-permute-start | bytes 2408456 | tf_op jit(solution)/shard_map/ppermute | solution.py:163
  132.2 8.8 %turn.1 = bf16[896,3584]{1,0:T(8,128)(2,1)} custom-call(bf16[3584,896]{1,0:T(8,128)(2,1)} %bitcast.15), custom_call_target="tpu_custom_call" | custom-call | flops 8589934592 | bytes 12845056 | tf_op jit(solution)/shard_map/turn/pallas_call | solution.py:201
  141.1 22.9 %collective-permute-done.10 = bf16[2,224,896]{2,1,0:T(8,128)(2,1)S(1)} collective-permute-done((bf16[2,224,896]{2,1,0:T(8,128)(2,1)S(1)}, bf16[2,224,896]{2,1,0:T(8,128)(2,1)S(1)}, u32[]{:S(2)}, u32[]{:S(2)}) %collective-permute-start.10) | collective-permute-done | bytes 802848 | tf_op jit(solution)/shard_map/ppermute | solution.py:163
  164.0 1.7 collective-permute-start.29
  172.3 14.6 %collective-permute-done.27 = bf16[2,224,896]{2,1,0:T(8,128)(2,1)S(1)} collective-permute-done((bf16[2,224,896]{2,1,0:T(8,128)(2,1)S(1)}, bf16[2,224,896]{2,1,0:T(8,128)(2,1)S(1)}, u32[]{:S(2)}, u32[]{:S(2)}) %collective-permute-start.27) | collective-permute-done | bytes 802848 | tf_op jit(solution)/shard_map/ppermute | solution.py:163
  (98 shorter events, 47.7 us)
Async XLA Ops:
  18.5 7.6 %collective-permute-start.36 = (bf16[3584]{0:T(1024)(128)(2,1)S(1)}, bf16[3584]{0:T(1024)(128)(2,1)S(1)}, u32[]{:S(2)}, u32[]{:S(2)}) collective-permute-start(bf16[3584]{0:T(1024)(128)(2,1)S(1)} %add_add_fusion.1), channel_id=1, source_target_pairs={{0,32},{16,48},{32,0},{48,16},{64,96},{80,112},{96,64},{112,80},{1... | collective-permute-start | bytes 21512 | tf_op jit(solution)/shard_map/ppermute | solution.py:115
  23.3 38.3 %collective-permute-start = (bf16[2,224,896]{2,1,0:T(8,128)(2,1)S(1)}, bf16[2,224,896]{2,1,0:T(8,128)(2,1)S(1)}, u32[]{:S(2)}, u32[]{:S(2)}) collective-permute-start(bf16[2,224,896]{2,1,0:T(8,128)(2,1)S(1)} %pad_maximum_fusion), channel_id=1, source_target_pairs={{0,224},{1,33},{2,226},{3,35},{4,228},{5,37},{6,230},{7,39},{8,232... | collective-permute-start | bytes 2408456 | tf_op jit(solution)/shard_map/ppermute | solution.py:163
  24.8 21.1 %collective-permute-start.12 = (bf16[1,224,896]{2,1,0:T(8,128)(2,1)S(1)}, bf16[1,224,896]{2,1,0:T(8,128)(2,1)S(1)}, u32[]{:S(2)}, u32[]{:S(2)}) collective-permute-start(bf16[1,224,896]{2,1,0:T(8,128)(2,1)S(1)} %merge.1), channel_id=1, source_target_pairs={{0,224},{1,33},{2,226},{3,35},{4,228},{5,37},{6,230},{7,39},{8,232... | collective-permute-start | bytes 1204232 | tf_op jit(solution)/shard_map/ppermute | solution.py:163
  27.5 16.1 %collective-permute-start.39 = (bf16[3584]{0:T(1024)(128)(2,1)S(1)}, bf16[3584]{0:T(1024)(128)(2,1)S(1)}, u32[]{:S(2)}, u32[]{:S(2)}) collective-permute-start(bf16[3584]{0:T(1024)(128)(2,1)S(1)} %add_add_fusion), channel_id=1, source_target_pairs={{0,128},{16,144},{32,160},{48,176},{64,192},{80,208},{96,224},{112... | collective-permute-start | bytes 21512 | tf_op jit(solution)/shard_map/ppermute | solution.py:115
  31.7 33.3 %collective-permute-start.1 = (bf16[2,224,896]{2,1,0:T(8,128)(2,1)S(1)}, bf16[2,224,896]{2,1,0:T(8,128)(2,1)S(1)}, u32[]{:S(2)}, u32[]{:S(2)}) collective-permute-start(bf16[2,224,896]{2,1,0:T(8,128)(2,1)S(1)} %pad_maximum_fusion), channel_id=1, source_target_pairs={{0,16},{16,0},{32,48},{48,32},{64,80},{80,64},{96,112},{112,96},{1... | collective-permute-start | bytes 2408456 | tf_op jit(solution)/shard_map/ppermute | solution.py:163
  32.1 22.9 %collective-permute-start.13 = (bf16[1,224,896]{2,1,0:T(8,128)(2,1)S(1)}, bf16[1,224,896]{2,1,0:T(8,128)(2,1)}, u32[]{:S(2)}, u32[]{:S(2)}) collective-permute-start(bf16[1,224,896]{2,1,0:T(8,128)(2,1)S(1)} %merge.1), channel_id=1, source_target_pairs={{0,16},{16,0},{32,48},{48,32},{64,80},{80,64},{96,112},{112,96},{1... | collective-permute-start | bytes 1204232 | tf_op jit(solution)/shard_map/ppermute | solution.py:163
  43.5 13.8 %collective-permute-start.14 = (bf16[1,224,896]{2,1,0:T(8,128)(2,1)S(1)}, bf16[1,224,896]{2,1,0:T(8,128)(2,1)}, u32[]{:S(2)}, u32[]{:S(2)}) collective-permute-start(bf16[1,224,896]{2,1,0:T(8,128)(2,1)S(1)} %merge.1), channel_id=1, source_target_pairs={{0,32},{1,225},{2,34},{3,227},{4,36},{5,229},{6,38},{7,231},{8,40}... | collective-permute-start | bytes 1204232 | tf_op jit(solution)/shard_map/ppermute | solution.py:163
  45.9 23.7 %collective-permute-start.2 = (bf16[2,224,896]{2,1,0:T(8,128)(2,1)S(1)}, bf16[2,224,896]{2,1,0:T(8,128)(2,1)S(1)}, u32[]{:S(2)}, u32[]{:S(2)}) collective-permute-start(bf16[2,224,896]{2,1,0:T(8,128)(2,1)S(1)} %pad_maximum_fusion), channel_id=1, source_target_pairs={{0,32},{1,225},{2,34},{3,227},{4,36},{5,229},{6,38},{7,231},{8,40}... | collective-permute-start | bytes 2408456 | tf_op jit(solution)/shard_map/ppermute | solution.py:163
  54.9 13.5 %collective-permute-start.15 = (bf16[1,224,896]{2,1,0:T(8,128)(2,1)S(1)}, bf16[1,224,896]{2,1,0:T(8,128)(2,1)S(1)}, u32[]{:S(2)}, u32[]{:S(2)}) collective-permute-start(bf16[1,224,896]{2,1,0:T(8,128)(2,1)S(1)} %collective-permute-done.12), channel_id=1, source_target_pairs={{0,224},{1,33},{2,226},{3,35},{4,228},{5,37},{6,230},{7,39},{8,232... | collective-permute-start | bytes 1204232 | tf_op jit(solution)/shard_map/ppermute | solution.py:163
  57.3 15.3 %collective-permute-start.16 = (bf16[1,224,896]{2,1,0:T(8,128)(2,1)}, bf16[1,224,896]{2,1,0:T(8,128)(2,1)S(1)}, u32[]{:S(2)}, u32[]{:S(2)}) collective-permute-start(bf16[1,224,896]{2,1,0:T(8,128)(2,1)} %collective-permute-done.14), channel_id=1, source_target_pairs={{0,16},{16,0},{32,48},{48,32},{64,80},{80,64},{96,112},{112,96},{1... | collective-permute-start | bytes 1204232 | tf_op jit(solution)/shard_map/ppermute | solution.py:163
  61.6 12.7 %collective-permute-start.17 = (bf16[1,224,896]{2,1,0:T(8,128)(2,1)}, bf16[1,224,896]{2,1,0:T(8,128)(2,1)S(1)}, u32[]{:S(2)}, u32[]{:S(2)}) collective-permute-start(bf16[1,224,896]{2,1,0:T(8,128)(2,1)} %collective-permute-done.14), channel_id=1, source_target_pairs={{0,32},{1,225},{2,34},{3,227},{4,36},{5,229},{6,38},{7,231},{8,40}... | collective-permute-start | bytes 1204232 | tf_op jit(solution)/shard_map/ppermute | solution.py:163
  65.0 31.5 %collective-permute-start.3 = (bf16[2,224,896]{2,1,0:T(8,128)(2,1)S(1)}, bf16[2,224,896]{2,1,0:T(8,128)(2,1)S(1)}, u32[]{:S(2)}, u32[]{:S(2)}) collective-permute-start(bf16[2,224,896]{2,1,0:T(8,128)(2,1)S(1)} %collective-permute-done), channel_id=1, source_target_pairs={{0,224},{1,33},{2,226},{3,35},{4,228},{5,37},{6,230},{7,39},{8,232... | collective-permute-start | bytes 2408456 | tf_op jit(solution)/shard_map/ppermute | solution.py:163
  68.4 22.7 %collective-permute-start.18 = (bf16[1,224,896]{2,1,0:T(8,128)(2,1)S(1)}, bf16[1,224,896]{2,1,0:T(8,128)(2,1)S(1)}, u32[]{:S(2)}, u32[]{:S(2)}) collective-permute-start(bf16[1,224,896]{2,1,0:T(8,128)(2,1)S(1)} %collective-permute-done.15), channel_id=1, source_target_pairs={{0,224},{1,33},{2,226},{3,35},{4,228},{5,37},{6,230},{7,39},{8,232... | collective-permute-start | bytes 1204232 | tf_op jit(solution)/shard_map/ppermute | solution.py:163
  69.6 22.4 %collective-permute-start.19 = (bf16[1,224,896]{2,1,0:T(8,128)(2,1)S(1)}, bf16[1,224,896]{2,1,0:T(8,128)(2,1)S(1)}, u32[]{:S(2)}, u32[]{:S(2)}) collective-permute-start(bf16[1,224,896]{2,1,0:T(8,128)(2,1)S(1)} %collective-permute-done.15), channel_id=1, source_target_pairs={{0,16},{16,0},{32,48},{48,32},{64,80},{80,64},{96,112},{112,96},{1... | collective-permute-start | bytes 1204232 | tf_op jit(solution)/shard_map/ppermute | solution.py:163
  72.6 32.8 %collective-permute-start.4 = (bf16[2,224,896]{2,1,0:T(8,128)(2,1)S(1)}, bf16[2,224,896]{2,1,0:T(8,128)(2,1)S(1)}, u32[]{:S(2)}, u32[]{:S(2)}) collective-permute-start(bf16[2,224,896]{2,1,0:T(8,128)(2,1)S(1)} %collective-permute-done.2), channel_id=1, source_target_pairs={{0,16},{16,0},{32,48},{48,32},{64,80},{80,64},{96,112},{112,96},{1... | collective-permute-start | bytes 2408456 | tf_op jit(solution)/shard_map/ppermute | solution.py:163
  74.3 19.0 %collective-permute-start.20 = (bf16[1,224,896]{2,1,0:T(8,128)(2,1)S(1)}, bf16[1,224,896]{2,1,0:T(8,128)(2,1)S(1)}, u32[]{:S(2)}, u32[]{:S(2)}) collective-permute-start(bf16[1,224,896]{2,1,0:T(8,128)(2,1)S(1)} %collective-permute-done.17), channel_id=1, source_target_pairs={{0,32},{1,225},{2,34},{3,227},{4,36},{5,229},{6,38},{7,231},{8,40}... | collective-permute-start | bytes 1204232 | tf_op jit(solution)/shard_map/ppermute | solution.py:163
  91.2 16.9 %collective-permute-start.5 = (bf16[2,224,896]{2,1,0:T(8,128)(2,1)S(1)}, bf16[2,224,896]{2,1,0:T(8,128)(2,1)S(1)}, u32[]{:S(2)}, u32[]{:S(2)}) collective-permute-start(bf16[2,224,896]{2,1,0:T(8,128)(2,1)S(1)} %collective-permute-done.2), channel_id=1, source_target_pairs={{0,32},{1,225},{2,34},{3,227},{4,36},{5,229},{6,38},{7,231},{8,40}... | collective-permute-start | bytes 2408456 | tf_op jit(solution)/shard_map/ppermute | solution.py:163
  91.9 12.8 %collective-permute-start.22 = (bf16[1,224,896]{2,1,0:T(8,128)(2,1)S(1)}, bf16[1,224,896]{2,1,0:T(8,128)(2,1)S(1)}, u32[]{:S(2)}, u32[]{:S(2)}) collective-permute-start(bf16[1,224,896]{2,1,0:T(8,128)(2,1)S(1)} %collective-permute-done.17), channel_id=1, source_target_pairs={{0,16},{16,0},{32,48},{48,32},{64,80},{80,64},{96,112},{112,96},{1... | collective-permute-start | bytes 1204232 | tf_op jit(solution)/shard_map/ppermute | solution.py:163
  93.3 25.8 %collective-permute-start.25 = (bf16[1,224,896]{2,1,0:T(8,128)(2,1)S(1)}, bf16[1,224,896]{2,1,0:T(8,128)(2,1)S(1)}, u32[]{:S(2)}, u32[]{:S(2)}) collective-permute-start(bf16[1,224,896]{2,1,0:T(8,128)(2,1)S(1)} %collective-permute-done.12), channel_id=1, source_target_pairs={{0,16},{16,0},{32,48},{48,32},{64,80},{80,64},{96,112},{112,96},{1... | collective-permute-start | bytes 1204232 | tf_op jit(solution)/shard_map/ppermute | solution.py:163
  96.5 12.5 %collective-permute-start.21 = (bf16[1,224,896]{2,1,0:T(8,128)(2,1)S(1)}, bf16[1,224,896]{2,1,0:T(8,128)(2,1)S(1)}, u32[]{:S(2)}, u32[]{:S(2)}) collective-permute-start(bf16[1,224,896]{2,1,0:T(8,128)(2,1)S(1)} %collective-permute-done.19), channel_id=1, source_target_pairs={{0,224},{1,33},{2,226},{3,35},{4,228},{5,37},{6,230},{7,39},{8,232... | collective-permute-start | bytes 1204232 | tf_op jit(solution)/shard_map/ppermute | solution.py:163
  104.8 7.3 %collective-permute-start.23 = (bf16[1,224,896]{2,1,0:T(8,128)(2,1)S(1)}, bf16[1,224,896]{2,1,0:T(8,128)(2,1)S(1)}, u32[]{:S(2)}, u32[]{:S(2)}) collective-permute-start(bf16[1,224,896]{2,1,0:T(8,128)(2,1)S(1)} %collective-permute-done.20), channel_id=1, source_target_pairs={{0,32},{1,225},{2,34},{3,227},{4,36},{5,229},{6,38},{7,231},{8,40}... | collective-permute-start | bytes 1204232 | tf_op jit(solution)/shard_map/ppermute | solution.py:163
  105.4 16.1 %collective-permute-start.26 = (bf16[1,224,896]{2,1,0:T(8,128)(2,1)S(1)}, bf16[1,224,896]{2,1,0:T(8,128)(2,1)S(1)}, u32[]{:S(2)}, u32[]{:S(2)}) collective-permute-start(bf16[1,224,896]{2,1,0:T(8,128)(2,1)S(1)} %collective-permute-done.22), channel_id=1, source_target_pairs={{0,32},{1,225},{2,34},{3,227},{4,36},{5,229},{6,38},{7,231},{8,40}... | collective-permute-start | bytes 1204232 | tf_op jit(solution)/shard_map/ppermute | solution.py:163
  108.1 21.5 %collective-permute-start.7 = (bf16[2,224,896]{2,1,0:T(8,128)(2,1)S(1)}, bf16[2,224,896]{2,1,0:T(8,128)(2,1)S(1)}, u32[]{:S(2)}, u32[]{:S(2)}) collective-permute-start(bf16[2,224,896]{2,1,0:T(8,128)(2,1)S(1)} %collective-permute-done.3), channel_id=1, source_target_pairs={{0,16},{16,0},{32,48},{48,32},{64,80},{80,64},{96,112},{112,96},{1... | collective-permute-start | bytes 2408456 | tf_op jit(solution)/shard_map/ppermute | solution.py:163
  109.0 8.2 %collective-permute-start.24 = (bf16[1,224,896]{2,1,0:T(8,128)(2,1)S(1)}, bf16[1,224,896]{2,1,0:T(8,128)(2,1)S(1)}, u32[]{:S(2)}, u32[]{:S(2)}) collective-permute-start(bf16[1,224,896]{2,1,0:T(8,128)(2,1)S(1)} %collective-permute-done.21), channel_id=1, source_target_pairs={{0,224},{1,33},{2,226},{3,35},{4,228},{5,37},{6,230},{7,39},{8,232... | collective-permute-start | bytes 1204232 | tf_op jit(solution)/shard_map/ppermute | solution.py:163
  112.1 75.8 %collective-permute-start.28 = (bf16[2,224,896]{2,1,0:T(8,128)(2,1)S(1)}, bf16[2,224,896]{2,1,0:T(8,128)(2,1)S(1)}, u32[]{:S(2)}, u32[]{:S(2)}) collective-permute-start(bf16[2,224,896]{2,1,0:T(8,128)(2,1)S(1)} %collective-permute-done), channel_id=1, source_target_pairs={{0,16},{16,0},{32,48},{48,32},{64,80},{80,64},{96,112},{112,96},{1... | collective-permute-start | bytes 2408456 | tf_op jit(solution)/shard_map/ppermute | solution.py:163
  117.2 48.4 %collective-permute-start.6 = (bf16[2,224,896]{2,1,0:T(8,128)(2,1)S(1)}, bf16[2,224,896]{2,1,0:T(8,128)(2,1)S(1)}, u32[]{:S(2)}, u32[]{:S(2)}) collective-permute-start(bf16[2,224,896]{2,1,0:T(8,128)(2,1)S(1)} %collective-permute-done.3), channel_id=1, source_target_pairs={{0,224},{1,33},{2,226},{3,35},{4,228},{5,37},{6,230},{7,39},{8,232... | collective-permute-start | bytes 2408456 | tf_op jit(solution)/shard_map/ppermute | solution.py:163
  119.0 22.0 %collective-permute-start.8 = (bf16[2,224,896]{2,1,0:T(8,128)(2,1)S(1)}, bf16[2,224,896]{2,1,0:T(8,128)(2,1)S(1)}, u32[]{:S(2)}, u32[]{:S(2)}) collective-permute-start(bf16[2,224,896]{2,1,0:T(8,128)(2,1)S(1)} %collective-permute-done.5), channel_id=1, source_target_pairs={{0,32},{1,225},{2,34},{3,227},{4,36},{5,229},{6,38},{7,231},{8,40}... | collective-permute-start | bytes 2408456 | tf_op jit(solution)/shard_map/ppermute | solution.py:163
  121.5 42.4 %collective-permute-start.10 = (bf16[2,224,896]{2,1,0:T(8,128)(2,1)S(1)}, bf16[2,224,896]{2,1,0:T(8,128)(2,1)S(1)}, u32[]{:S(2)}, u32[]{:S(2)}) collective-permute-start(bf16[2,224,896]{2,1,0:T(8,128)(2,1)S(1)} %collective-permute-done.5), channel_id=1, source_target_pairs={{0,16},{16,0},{32,48},{48,32},{64,80},{80,64},{96,112},{112,96},{1... | collective-permute-start | bytes 2408456 | tf_op jit(solution)/shard_map/ppermute | solution.py:163
  129.5 38.0 %collective-permute-start.9 = (bf16[2,224,896]{2,1,0:T(8,128)(2,1)S(1)}, bf16[2,224,896]{2,1,0:T(8,128)(2,1)S(1)}, u32[]{:S(2)}, u32[]{:S(2)}) collective-permute-start(bf16[2,224,896]{2,1,0:T(8,128)(2,1)S(1)} %collective-permute-done.7), channel_id=1, source_target_pairs={{0,224},{1,33},{2,226},{3,35},{4,228},{5,37},{6,230},{7,39},{8,232... | collective-permute-start | bytes 2408456 | tf_op jit(solution)/shard_map/ppermute | solution.py:163
  141.1 30.3 %collective-permute-start.11 = (bf16[2,224,896]{2,1,0:T(8,128)(2,1)S(1)}, bf16[2,224,896]{2,1,0:T(8,128)(2,1)S(1)}, u32[]{:S(2)}, u32[]{:S(2)}) collective-permute-start(bf16[2,224,896]{2,1,0:T(8,128)(2,1)S(1)} %collective-permute-done.8), channel_id=1, source_target_pairs={{0,32},{1,225},{2,34},{3,227},{4,36},{5,229},{6,38},{7,231},{8,40}... | collective-permute-start | bytes 2408456 | tf_op jit(solution)/shard_map/ppermute | solution.py:163
  164.0 24.9 %collective-permute-start.29 = (bf16[2,224,896]{2,1,0:T(8,128)(2,1)S(1)}, bf16[2,224,896]{2,1,0:T(8,128)(2,1)S(1)}, u32[]{:S(2)}, u32[]{:S(2)}) collective-permute-start(bf16[2,224,896]{2,1,0:T(8,128)(2,1)S(1)} %collective-permute-done.10), channel_id=1, source_target_pairs={{0,32},{1,225},{2,34},{3,227},{4,36},{5,229},{6,38},{7,231},{8,40}... | collective-permute-start | bytes 2408456 | tf_op jit(solution)/shard_map/ppermute | solution.py:163
  167.6 19.4 %collective-permute-start.27 = (bf16[2,224,896]{2,1,0:T(8,128)(2,1)S(1)}, bf16[2,224,896]{2,1,0:T(8,128)(2,1)S(1)}, u32[]{:S(2)}, u32[]{:S(2)}) collective-permute-start(bf16[2,224,896]{2,1,0:T(8,128)(2,1)S(1)} %collective-permute-done.9), channel_id=1, source_target_pairs={{0,224},{1,33},{2,226},{3,35},{4,228},{5,37},{6,230},{7,39},{8,232... | collective-permute-start | bytes 2408456 | tf_op jit(solution)/shard_map/ppermute | solution.py:163
  (9 other events, 43.9 us)

commit v6 on v5

--- a/solution.py
+++ b/solution.py
@@ -1,3 +1,5 @@
+import functools
+
 import jax
 import jax.numpy as jnp
 from jax import lax
@@ -34,13 +36,6 @@
 def reached(direction, place):
     dz, h = place
     return ((dz, 1 - h), (dz + 1, h), (dz - 1, h))[direction]
-
-
-def merged(base, low, high):
-    return (
-        base.astype(jnp.float32)
-        + mix_rate * jnp.dot(low, high, preferred_element_type=jnp.float32)
-    ).astype(jnp.bfloat16)
 
 
 STAGES = (
@@ -53,46 +48,65 @@
 )
 
 
-def merge_kernel(base_hbm, lhs_hbm, rhs_hbm, out_ref, base, lhs, rhs, added, sems):
-    loads = [
-        pltpu.make_async_copy(lhs_hbm, lhs, sems.at[0]),
-        pltpu.make_async_copy(rhs_hbm, rhs, sems.at[1]),
-    ]
-    parts = [slice(at, min(at + 256, COLS)) for at in range(0, COLS, 256)]
-    for i, part in enumerate(parts):
+PARTS = [slice(at, min(at + 256, COLS)) for at in range(0, COLS, 256)]
+
+
+def merge_kernel(count, *refs):
+    sources, out_ref = refs[: 3 * count], refs[3 * count]
+    held, (added, sems) = refs[3 * count + 1 : 6 * count + 1], refs[6 * count + 1 :]
+    loads = []
+    for n in range(count):
+        base_hbm, lhs_hbm, rhs_hbm = sources[3 * n : 3 * n + 3]
+        base, lhs, rhs = held[3 * n : 3 * n + 3]
         loads.append(
-            pltpu.make_async_copy(
-                base_hbm.at[:, part], base.at[:, part], sems.at[2 + i]
-            )
+            [
+                pltpu.make_async_copy(lhs_hbm, lhs, sems.at[n, 0]),
+                pltpu.make_async_copy(rhs_hbm, rhs, sems.at[n, 1]),
+            ]
+            + [
+                pltpu.make_async_copy(
+                    base_hbm.at[:, part], base.at[:, part], sems.at[n, 2 + i]
+                )
+                for i, part in enumerate(PARTS)
+            ]
         )
-    for load in loads:
-        load.start()
-    loads[0].wait()
-    loads[1].wait()
-    added[...] = lax.dot_general(
-        lhs[...], rhs[...], (((0,), (0,)), ((), ())), preferred_element_type=jnp.float32
-    )
-    for i, part in enumerate(parts):
-        loads[2 + i].wait()
-        out_ref[0, :, part] = (
-            base[:, part].astype(jnp.float32) + mix_rate * added[:, part]
-        ).astype(jnp.bfloat16)
-
-
-def merged_by_kernel(base, lhs, rhs):
-    operands = (base, lhs, rhs)
+        for load in loads[n]:
+            load.start()
+    for n in range(count):
+        base, lhs, rhs = held[3 * n : 3 * n + 3]
+        loads[n][0].wait()
+        loads[n][1].wait()
+        added[...] = lax.dot_general(
+            lhs[...],
+            rhs[...],
+            (((0,), (0,)), ((), ())),
+            preferred_element_type=jnp.float32,
+        )
+        for i, part in enumerate(PARTS):
+            loads[n][2 + i].wait()
+            out_ref[n, :, part] = (
+                base[:, part].astype(jnp.float32) + mix_rate * added[:, part]
+            ).astype(jnp.bfloat16)
+
+
+def merged_by_kernel(*operands):
+    count = len(operands) // 3
     return pl.pallas_call(
-        merge_kernel,
-        in_specs=[pl.BlockSpec(memory_space=pltpu.HBM)] * 3,
+        functools.partial(merge_kernel, count),
+        in_specs=[pl.BlockSpec(memory_space=pltpu.HBM)] * len(operands),
         out_specs=pl.BlockSpec(memory_space=pltpu.VMEM),
-        out_shape=pltpu.VMEM((1, ROWS, COLS), jnp.bfloat16),
+        out_shape=pltpu.VMEM((count, ROWS, COLS), jnp.bfloat16),
         scratch_shapes=[pltpu.VMEM(x.shape, x.dtype) for x in operands]
-        + [pltpu.VMEM((ROWS, COLS), jnp.float32), pltpu.SemaphoreType.DMA((6,))],
+        + [
+            pltpu.VMEM((ROWS, COLS), jnp.float32),
+            pltpu.SemaphoreType.DMA((count, 2 + len(PARTS))),
+        ],
         compiler_params=pltpu.CompilerParams(vmem_limit_bytes=8 << 20),
         cost_estimate=pl.CostEstimate(
-            flops=2 * ROWS * COLS * 16, bytes_accessed=1 << 20, transcendentals=0
-        ),
-        name="merge",
+            flops=2 * count * ROWS * COLS * 16,
+            bytes_accessed=count << 20,
+            transcendentals=0,
+        ),
     )(*(pltpu.with_memory_space_constraint(x, pltpu.HBM) for x in operands))
 
 
@@ -140,11 +154,8 @@
 
     serve_norm = gather_norm(norm_train, norm_step)
     own_down = merged_by_kernel(train_down.T, high_down, low_down.T)
-    own_rest = jnp.stack(
-        [
-            merged(train_gate, low_gate, high_gate),
-            merged(train_up, low_up, high_up),
-        ]
+    own_rest = merged_by_kernel(
+        train_gate, low_gate.T, high_gate, train_up, low_up.T, high_up
     )
     own = tuple(map(lax.optimization_barrier, (own_down, own_rest)))
     zero = jnp.uint32(0)

time: 190 us -> 194 us (1.021)
  waiting for transfers between devices: 90.5 us -> 94.3 us
  matrix products: 2.64 us -> 0 us
    dot_general x2 -> x0, matrix products: 2.64 us -> none  [merged(): jnp.dot(low, high, preferred_element_type=jnp.float32)]
    ppermute x30, waiting for transfers between devices: 74.5 us -> 76.5 us  [per_device(): got = lax.ppermute(held[k][place], *HOPS[direction])]
  transfers between devices with their start and end apart: 40 -> 40, of which waited for: 15 -> 15; matrix products, arithmetic and copies ran while one was open for 17% -> 15% of each run, Pallas kernels for 5% -> 6%
where the time goes in v6:
time: 194 us
  waiting for transfers between devices  94.3 us (49%)
  starting transfers between devices  55.3 us (29%)
  local copies, waits for them, and re-layouts  30.1 us (16%)
  Pallas kernels  11.7 us (6%)
    ppermute x30, waiting for transfers between devices, per_device(): got = lax.ppermute(held[k][place], *HOPS[direction])  76.5 us
    ppermute x30, starting transfers between devices, per_device(): got = lax.ppermute(held[k][place], *HOPS[direction])  37.5 us
    dynamic_update_slice x32, local copies, waits for them, and re-layouts, put(): return lax.dynamic_update_slice(stack, piece, (slot(place), zero, zero))  29.7 us
    ppermute x10, waiting for transfers between devices, gather_norm(): got.append(lax.ppermute(total, *flipped(name, bits)))  17.8 us
    ppermute x10, starting transfers between devices, gather_norm(): got.append(lax.ppermute(total, *flipped(name, bits)))  17.8 us
    pallas_call x1, Pallas kernels, turned(): pl.pallas_call(turn_kernel, grid=(rows // 512,), in_specs=[pl.BlockSpec((...  8.83 us
  transfers between devices with their start and end apart: 40, of which 15 were waited for; matrix products, arithmetic and copies ran while one was open for 15% of the time, Pallas kernels for 6%

profile of v6, /device:TPU:1, one launch (start us, length us, event | category | flops | bytes accessed | tf_op | source)
XLA Modules:
  0.0 193.5 jit_solution(16202209453530219657)
XLA Ops:
  1.5 3.2 %collective-permute-start.30 = (bf16[3584]{0:T(1024)(128)(2,1)S(1)}, bf16[3584]{0:T(1024)(128)(2,1)S(1)}, u32[]{:S(2)}, u32[]{:S(2)}) collective-permute-start(bf16[3584]{0:T(1024)(128)(2,1)S(1)} %dynamic_update_slice.197), channel_id=1, source_target_pairs={{0,1},{1,0},{2,3},{3,2},{4,5},{5,4},{6,7},{7,6},{8,9},{9,8},{10,11... | collective-permute-start | bytes 21512 | tf_op jit(solution)/shard_map/ppermute | solution.py:129
  5.9 2.5 %collective-permute-done.31 = bf16[3584]{0:T(1024)(128)(2,1)S(1)} collective-permute-done((bf16[3584]{0:T(1024)(128)(2,1)S(1)}, bf16[3584]{0:T(1024)(128)(2,1)S(1)}, u32[]{:S(2)}, u32[]{:S(2)}) %collective-permute-start.31) | collective-permute-done | bytes 7200 | tf_op jit(solution)/shard_map/ppermute | solution.py:129
  9.5 3.0 %collective-permute-done.32 = bf16[3584]{0:T(1024)(128)(2,1)S(1)} collective-permute-done((bf16[3584]{0:T(1024)(128)(2,1)S(1)}, bf16[3584]{0:T(1024)(128)(2,1)S(1)}, u32[]{:S(2)}, u32[]{:S(2)}) %collective-permute-start.32) | collective-permute-done | bytes 7200 | tf_op jit(solution)/shard_map/ppermute | solution.py:129
  12.4 2.2 %collective-permute-start.34 = (bf16[3584]{0:T(1024)(128)(2,1)S(1)}, bf16[3584]{0:T(1024)(128)(2,1)S(1)}, u32[]{:S(2)}, u32[]{:S(2)}) collective-permute-start(bf16[3584]{0:T(1024)(128)(2,1)S(1)} %add.104), channel_id=1, source_target_pairs={{0,16},{1,17},{2,18},{3,19},{4,20},{5,21},{6,22},{7,23},{8,24},{9,... | collective-permute-start | bytes 21512 | tf_op jit(solution)/shard_map/ppermute | solution.py:129
  14.6 1.6 collective-permute-start.35
  16.5 1.8 collective-permute-done.35
  18.4 1.6 collective-permute-start.36
  20.0 3.0 %collective-permute-start.37 = (bf16[3584]{0:T(1024)(128)(2,1)S(1)}, bf16[3584]{0:T(1024)(128)(2,1)S(1)}, u32[]{:S(2)}, u32[]{:S(2)}) collective-permute-start(bf16[3584]{0:T(1024)(128)(2,1)S(1)} %add_add_fusion.1), channel_id=1, source_target_pairs={{0,64},{16,80},{32,96},{48,112},{64,0},{80,16},{96,32},{112,48},{1... | collective-permute-start | bytes 21512 | tf_op jit(solution)/shard_map/ppermute | solution.py:129
  23.0 1.6 shard_map.138
  27.6 4.9 %collective-permute-start.39 = (bf16[3584]{0:T(1024)(128)(2,1)S(1)}, bf16[3584]{0:T(1024)(128)(2,1)S(1)}, u32[]{:S(2)}, u32[]{:S(2)}) collective-permute-start(bf16[3584]{0:T(1024)(128)(2,1)S(1)} %add_add_fusion), channel_id=1, source_target_pairs={{0,128},{16,144},{32,160},{48,176},{64,192},{80,208},{96,224},{112... | collective-permute-start | bytes 21512 | tf_op jit(solution)/shard_map/ppermute | solution.py:129
  32.9 2.6 %collective-permute-start.13 = (bf16[1,224,896]{2,1,0:T(8,128)(2,1)S(1)}, bf16[1,224,896]{2,1,0:T(8,128)(2,1)}, u32[]{:S(2)}, u32[]{:S(2)}) collective-permute-start(bf16[1,224,896]{2,1,0:T(8,128)(2,1)S(1)} %shard_map.139), channel_id=1, source_target_pairs={{0,16},{16,0},{32,48},{48,32},{64,80},{80,64},{96,112},{112,96},{1... | collective-permute-start | bytes 1204232 | tf_op jit(solution)/shard_map/ppermute | solution.py:174
  35.5 9.4 %collective-permute-done.39 = bf16[3584]{0:T(1024)(128)(2,1)S(1)} collective-permute-done((bf16[3584]{0:T(1024)(128)(2,1)S(1)}, bf16[3584]{0:T(1024)(128)(2,1)S(1)}, u32[]{:S(2)}, u32[]{:S(2)}) %collective-permute-start.39) | collective-permute-done | bytes 7200 | tf_op jit(solution)/shard_map/ppermute | solution.py:129
  49.4 7.4 %collective-permute-done.13 = bf16[1,224,896]{2,1,0:T(8,128)(2,1)} collective-permute-done((bf16[1,224,896]{2,1,0:T(8,128)(2,1)S(1)}, bf16[1,224,896]{2,1,0:T(8,128)(2,1)}, u32[]{:S(2)}, u32[]{:S(2)}) %collective-permute-start.13) | collective-permute-done | bytes 401440 | tf_op jit(solution)/shard_map/ppermute | solution.py:174
  56.8 1.8 collective-permute-start.15
  59.2 1.8 constant_dynamic-update-slice_fusion.13
  61.0 1.8 constant_dynamic-update-slice_fusion.12
  62.8 3.1 %collective-permute-start.17 = (bf16[1,224,896]{2,1,0:T(8,128)(2,1)}, bf16[1,224,896]{2,1,0:T(8,128)(2,1)S(1)}, u32[]{:S(2)}, u32[]{:S(2)}) collective-permute-start(bf16[1,224,896]{2,1,0:T(8,128)(2,1)} %collective-permute-done.14), channel_id=1, source_target_pairs={{0,32},{1,225},{2,34},{3,227},{4,36},{5,229},{6,38},{7,231},{8,40}... | collective-permute-start | bytes 1204232 | tf_op jit(solution)/shard_map/ppermute | solution.py:174
  66.9 3.6 %collective-permute-done.15 = bf16[1,224,896]{2,1,0:T(8,128)(2,1)S(1)} collective-permute-done((bf16[1,224,896]{2,1,0:T(8,128)(2,1)S(1)}, bf16[1,224,896]{2,1,0:T(8,128)(2,1)S(1)}, u32[]{:S(2)}, u32[]{:S(2)}) %collective-permute-start.15) | collective-permute-done | bytes 401440 | tf_op jit(solution)/shard_map/ppermute | solution.py:174
  76.1 2.7 %collective-permute-start.20 = (bf16[1,224,896]{2,1,0:T(8,128)(2,1)S(1)}, bf16[1,224,896]{2,1,0:T(8,128)(2,1)S(1)}, u32[]{:S(2)}, u32[]{:S(2)}) collective-permute-start(bf16[1,224,896]{2,1,0:T(8,128)(2,1)S(1)} %collective-permute-done.17), channel_id=1, source_target_pairs={{0,32},{1,225},{2,34},{3,227},{4,36},{5,229},{6,38},{7,231},{8,40}... | collective-permute-start | bytes 1204232 | tf_op jit(solution)/shard_map/ppermute | solution.py:174
  80.4 12.6 %collective-permute-done.18 = bf16[1,224,896]{2,1,0:T(8,128)(2,1)S(1)} collective-permute-done((bf16[1,224,896]{2,1,0:T(8,128)(2,1)S(1)}, bf16[1,224,896]{2,1,0:T(8,128)(2,1)S(1)}, u32[]{:S(2)}, u32[]{:S(2)}) %collective-permute-start.18) | collective-permute-done | bytes 401440 | tf_op jit(solution)/shard_map/ppermute | solution.py:174
  95.1 2.4 %collective-permute-start.25 = (bf16[1,224,896]{2,1,0:T(8,128)(2,1)S(1)}, bf16[1,224,896]{2,1,0:T(8,128)(2,1)S(1)}, u32[]{:S(2)}, u32[]{:S(2)}) collective-permute-start(bf16[1,224,896]{2,1,0:T(8,128)(2,1)S(1)} %collective-permute-done.12), channel_id=1, source_target_pairs={{0,16},{16,0},{32,48},{48,32},{64,80},{80,64},{96,112},{112,96},{1... | collective-permute-start | bytes 1204232 | tf_op jit(solution)/shard_map/ppermute | solution.py:174
  100.8 5.8 %collective-permute-done.22 = bf16[1,224,896]{2,1,0:T(8,128)(2,1)S(1)} collective-permute-done((bf16[1,224,896]{2,1,0:T(8,128)(2,1)S(1)}, bf16[1,224,896]{2,1,0:T(8,128)(2,1)S(1)}, u32[]{:S(2)}, u32[]{:S(2)}) %collective-permute-start.22) | collective-permute-done | bytes 401440 | tf_op jit(solution)/shard_map/ppermute | solution.py:174
  106.7 2.6 %collective-permute-start.26 = (bf16[1,224,896]{2,1,0:T(8,128)(2,1)S(1)}, bf16[1,224,896]{2,1,0:T(8,128)(2,1)S(1)}, u32[]{:S(2)}, u32[]{:S(2)}) collective-permute-start(bf16[1,224,896]{2,1,0:T(8,128)(2,1)S(1)} %collective-permute-done.22), channel_id=1, source_target_pairs={{0,32},{1,225},{2,34},{3,227},{4,36},{5,229},{6,38},{7,231},{8,40}... | collective-permute-start | bytes 1204232 | tf_op jit(solution)/shard_map/ppermute | solution.py:174
  114.1 2.4 %collective-permute-start.28 = (bf16[2,224,896]{2,1,0:T(8,128)(2,1)S(1)}, bf16[2,224,896]{2,1,0:T(8,128)(2,1)S(1)}, u32[]{:S(2)}, u32[]{:S(2)}) collective-permute-start(bf16[2,224,896]{2,1,0:T(8,128)(2,1)S(1)} %collective-permute-done), channel_id=1, source_target_pairs={{0,16},{16,0},{32,48},{48,32},{64,80},{80,64},{96,112},{112,96},{1... | collective-permute-start | bytes 2408456 | tf_op jit(solution)/shard_map/ppermute | solution.py:174
  117.3 1.8 collective-permute-done.24
  121.1 1.5 collective-permute-start.8
  123.4 2.7 %collective-permute-start.10 = (bf16[2,224,896]{2,1,0:T(8,128)(2,1)S(1)}, bf16[2,224,896]{2,1,0:T(8,128)(2,1)S(1)}, u32[]{:S(2)}, u32[]{:S(2)}) collective-permute-start(bf16[2,224,896]{2,1,0:T(8,128)(2,1)S(1)} %collective-permute-done.5), channel_id=1, source_target_pairs={{0,16},{16,0},{32,48},{48,32},{64,80},{80,64},{96,112},{112,96},{1... | collective-permute-start | bytes 2408456 | tf_op jit(solution)/shard_map/ppermute | solution.py:174
  126.9 5.5 %collective-permute-done.7 = bf16[2,224,896]{2,1,0:T(8,128)(2,1)S(1)} collective-permute-done((bf16[2,224,896]{2,1,0:T(8,128)(2,1)S(1)}, bf16[2,224,896]{2,1,0:T(8,128)(2,1)S(1)}, u32[]{:S(2)}, u32[]{:S(2)}) %collective-permute-start.7) | collective-permute-done | bytes 802848 | tf_op jit(solution)/shard_map/ppermute | solution.py:174
  133.9 8.8 %turn.1 = bf16[896,3584]{1,0:T(8,128)(2,1)} custom-call(bf16[3584,896]{1,0:T(8,128)(2,1)} %bitcast.11), custom_call_target="tpu_custom_call" | custom-call | flops 8589934592 | bytes 12845056 | tf_op jit(solution)/shard_map/turn/pallas_call | solution.py:212
  143.9 22.9 %collective-permute-done.10 = bf16[2,224,896]{2,1,0:T(8,128)(2,1)S(1)} collective-permute-done((bf16[2,224,896]{2,1,0:T(8,128)(2,1)S(1)}, bf16[2,224,896]{2,1,0:T(8,128)(2,1)S(1)}, u32[]{:S(2)}, u32[]{:S(2)}) %collective-permute-start.10) | collective-permute-done | bytes 802848 | tf_op jit(solution)/shard_map/ppermute | solution.py:174
  166.8 1.6 collective-permute-start.29
  174.1 16.6 %collective-permute-done.27 = bf16[2,224,896]{2,1,0:T(8,128)(2,1)S(1)} collective-permute-done((bf16[2,224,896]{2,1,0:T(8,128)(2,1)S(1)}, bf16[2,224,896]{2,1,0:T(8,128)(2,1)S(1)}, u32[]{:S(2)}, u32[]{:S(2)}) %collective-permute-start.27) | collective-permute-done | bytes 802848 | tf_op jit(solution)/shard_map/ppermute | solution.py:174
  (94 shorter events, 45.6 us)
Async XLA Ops:
  18.4 9.2 %collective-permute-start.36 = (bf16[3584]{0:T(1024)(128)(2,1)S(1)}, bf16[3584]{0:T(1024)(128)(2,1)S(1)}, u32[]{:S(2)}, u32[]{:S(2)}) collective-permute-start(bf16[3584]{0:T(1024)(128)(2,1)S(1)} %add_add_fusion.1), channel_id=1, source_target_pairs={{0,32},{16,48},{32,0},{48,16},{64,96},{80,112},{96,64},{112,80},{1... | collective-permute-start | bytes 21512 | tf_op jit(solution)/shard_map/ppermute | solution.py:129
  20.0 7.6 %collective-permute-start.37 = (bf16[3584]{0:T(1024)(128)(2,1)S(1)}, bf16[3584]{0:T(1024)(128)(2,1)S(1)}, u32[]{:S(2)}, u32[]{:S(2)}) collective-permute-start(bf16[3584]{0:T(1024)(128)(2,1)S(1)} %add_add_fusion.1), channel_id=1, source_target_pairs={{0,64},{16,80},{32,96},{48,112},{64,0},{80,16},{96,32},{112,48},{1... | collective-permute-start | bytes 21512 | tf_op jit(solution)/shard_map/ppermute | solution.py:129
  24.6 38.2 %collective-permute-start = (bf16[2,224,896]{2,1,0:T(8,128)(2,1)S(1)}, bf16[2,224,896]{2,1,0:T(8,128)(2,1)S(1)}, u32[]{:S(2)}, u32[]{:S(2)}) collective-permute-start(bf16[2,224,896]{2,1,0:T(8,128)(2,1)S(1)} %shard_map.138), channel_id=1, source_target_pairs={{0,224},{1,33},{2,226},{3,35},{4,228},{5,37},{6,230},{7,39},{8,232... | collective-permute-start | bytes 2408456 | tf_op jit(solution)/shard_map/ppermute | solution.py:174
  26.2 21.1 %collective-permute-start.12 = (bf16[1,224,896]{2,1,0:T(8,128)(2,1)S(1)}, bf16[1,224,896]{2,1,0:T(8,128)(2,1)S(1)}, u32[]{:S(2)}, u32[]{:S(2)}) collective-permute-start(bf16[1,224,896]{2,1,0:T(8,128)(2,1)S(1)} %shard_map.139), channel_id=1, source_target_pairs={{0,224},{1,33},{2,226},{3,35},{4,228},{5,37},{6,230},{7,39},{8,232... | collective-permute-start | bytes 1204232 | tf_op jit(solution)/shard_map/ppermute | solution.py:174
  27.6 17.3 %collective-permute-start.39 = (bf16[3584]{0:T(1024)(128)(2,1)S(1)}, bf16[3584]{0:T(1024)(128)(2,1)S(1)}, u32[]{:S(2)}, u32[]{:S(2)}) collective-permute-start(bf16[3584]{0:T(1024)(128)(2,1)S(1)} %add_add_fusion), channel_id=1, source_target_pairs={{0,128},{16,144},{32,160},{48,176},{64,192},{80,208},{96,224},{112... | collective-permute-start | bytes 21512 | tf_op jit(solution)/shard_map/ppermute | solution.py:129
  32.5 34.4 %collective-permute-start.1 = (bf16[2,224,896]{2,1,0:T(8,128)(2,1)S(1)}, bf16[2,224,896]{2,1,0:T(8,128)(2,1)S(1)}, u32[]{:S(2)}, u32[]{:S(2)}) collective-permute-start(bf16[2,224,896]{2,1,0:T(8,128)(2,1)S(1)} %shard_map.138), channel_id=1, source_target_pairs={{0,16},{16,0},{32,48},{48,32},{64,80},{80,64},{96,112},{112,96},{1... | collective-permute-start | bytes 2408456 | tf_op jit(solution)/shard_map/ppermute | solution.py:174
  32.9 23.9 %collective-permute-start.13 = (bf16[1,224,896]{2,1,0:T(8,128)(2,1)S(1)}, bf16[1,224,896]{2,1,0:T(8,128)(2,1)}, u32[]{:S(2)}, u32[]{:S(2)}) collective-permute-start(bf16[1,224,896]{2,1,0:T(8,128)(2,1)S(1)} %shard_map.139), channel_id=1, source_target_pairs={{0,16},{16,0},{32,48},{48,32},{64,80},{80,64},{96,112},{112,96},{1... | collective-permute-start | bytes 1204232 | tf_op jit(solution)/shard_map/ppermute | solution.py:174
  44.9 13.7 %collective-permute-start.14 = (bf16[1,224,896]{2,1,0:T(8,128)(2,1)S(1)}, bf16[1,224,896]{2,1,0:T(8,128)(2,1)}, u32[]{:S(2)}, u32[]{:S(2)}) collective-permute-start(bf16[1,224,896]{2,1,0:T(8,128)(2,1)S(1)} %shard_map.139), channel_id=1, source_target_pairs={{0,32},{1,225},{2,34},{3,227},{4,36},{5,229},{6,38},{7,231},{8,40}... | collective-permute-start | bytes 1204232 | tf_op jit(solution)/shard_map/ppermute | solution.py:174
  47.3 24.2 %collective-permute-start.2 = (bf16[2,224,896]{2,1,0:T(8,128)(2,1)S(1)}, bf16[2,224,896]{2,1,0:T(8,128)(2,1)S(1)}, u32[]{:S(2)}, u32[]{:S(2)}) collective-permute-start(bf16[2,224,896]{2,1,0:T(8,128)(2,1)S(1)} %shard_map.138), channel_id=1, source_target_pairs={{0,32},{1,225},{2,34},{3,227},{4,36},{5,229},{6,38},{7,231},{8,40}... | collective-permute-start | bytes 2408456 | tf_op jit(solution)/shard_map/ppermute | solution.py:174
  56.8 13.7 %collective-permute-start.15 = (bf16[1,224,896]{2,1,0:T(8,128)(2,1)S(1)}, bf16[1,224,896]{2,1,0:T(8,128)(2,1)S(1)}, u32[]{:S(2)}, u32[]{:S(2)}) collective-permute-start(bf16[1,224,896]{2,1,0:T(8,128)(2,1)S(1)} %collective-permute-done.12), channel_id=1, source_target_pairs={{0,224},{1,33},{2,226},{3,35},{4,228},{5,37},{6,230},{7,39},{8,232... | collective-permute-start | bytes 1204232 | tf_op jit(solution)/shard_map/ppermute | solution.py:174
  58.6 16.1 %collective-permute-start.16 = (bf16[1,224,896]{2,1,0:T(8,128)(2,1)}, bf16[1,224,896]{2,1,0:T(8,128)(2,1)S(1)}, u32[]{:S(2)}, u32[]{:S(2)}) collective-permute-start(bf16[1,224,896]{2,1,0:T(8,128)(2,1)} %collective-permute-done.14), channel_id=1, source_target_pairs={{0,16},{16,0},{32,48},{48,32},{64,80},{80,64},{96,112},{112,96},{1... | collective-permute-start | bytes 1204232 | tf_op jit(solution)/shard_map/ppermute | solution.py:174
  62.8 13.3 %collective-permute-start.17 = (bf16[1,224,896]{2,1,0:T(8,128)(2,1)}, bf16[1,224,896]{2,1,0:T(8,128)(2,1)S(1)}, u32[]{:S(2)}, u32[]{:S(2)}) collective-permute-start(bf16[1,224,896]{2,1,0:T(8,128)(2,1)} %collective-permute-done.14), channel_id=1, source_target_pairs={{0,32},{1,225},{2,34},{3,227},{4,36},{5,229},{6,38},{7,231},{8,40}... | collective-permute-start | bytes 1204232 | tf_op jit(solution)/shard_map/ppermute | solution.py:174
  66.9 31.5 %collective-permute-start.3 = (bf16[2,224,896]{2,1,0:T(8,128)(2,1)S(1)}, bf16[2,224,896]{2,1,0:T(8,128)(2,1)S(1)}, u32[]{:S(2)}, u32[]{:S(2)}) collective-permute-start(bf16[2,224,896]{2,1,0:T(8,128)(2,1)S(1)} %collective-permute-done), channel_id=1, source_target_pairs={{0,224},{1,33},{2,226},{3,35},{4,228},{5,37},{6,230},{7,39},{8,232... | collective-permute-start | bytes 2408456 | tf_op jit(solution)/shard_map/ppermute | solution.py:174
  70.5 22.5 %collective-permute-start.18 = (bf16[1,224,896]{2,1,0:T(8,128)(2,1)S(1)}, bf16[1,224,896]{2,1,0:T(8,128)(2,1)S(1)}, u32[]{:S(2)}, u32[]{:S(2)}) collective-permute-start(bf16[1,224,896]{2,1,0:T(8,128)(2,1)S(1)} %collective-permute-done.15), channel_id=1, source_target_pairs={{0,224},{1,33},{2,226},{3,35},{4,228},{5,37},{6,230},{7,39},{8,232... | collective-permute-start | bytes 1204232 | tf_op jit(solution)/shard_map/ppermute | solution.py:174
  71.4 22.4 %collective-permute-start.19 = (bf16[1,224,896]{2,1,0:T(8,128)(2,1)S(1)}, bf16[1,224,896]{2,1,0:T(8,128)(2,1)S(1)}, u32[]{:S(2)}, u32[]{:S(2)}) collective-permute-start(bf16[1,224,896]{2,1,0:T(8,128)(2,1)S(1)} %collective-permute-done.15), channel_id=1, source_target_pairs={{0,16},{16,0},{32,48},{48,32},{64,80},{80,64},{96,112},{112,96},{1... | collective-permute-start | bytes 1204232 | tf_op jit(solution)/shard_map/ppermute | solution.py:174
  74.6 32.0 %collective-permute-start.4 = (bf16[2,224,896]{2,1,0:T(8,128)(2,1)S(1)}, bf16[2,224,896]{2,1,0:T(8,128)(2,1)S(1)}, u32[]{:S(2)}, u32[]{:S(2)}) collective-permute-start(bf16[2,224,896]{2,1,0:T(8,128)(2,1)S(1)} %collective-permute-done.2), channel_id=1, source_target_pairs={{0,16},{16,0},{32,48},{48,32},{64,80},{80,64},{96,112},{112,96},{1... | collective-permute-start | bytes 2408456 | tf_op jit(solution)/shard_map/ppermute | solution.py:174
  76.1 19.0 %collective-permute-start.20 = (bf16[1,224,896]{2,1,0:T(8,128)(2,1)S(1)}, bf16[1,224,896]{2,1,0:T(8,128)(2,1)S(1)}, u32[]{:S(2)}, u32[]{:S(2)}) collective-permute-start(bf16[1,224,896]{2,1,0:T(8,128)(2,1)S(1)} %collective-permute-done.17), channel_id=1, source_target_pairs={{0,32},{1,225},{2,34},{3,227},{4,36},{5,229},{6,38},{7,231},{8,40}... | collective-permute-start | bytes 1204232 | tf_op jit(solution)/shard_map/ppermute | solution.py:174
  93.0 17.3 %collective-permute-start.5 = (bf16[2,224,896]{2,1,0:T(8,128)(2,1)S(1)}, bf16[2,224,896]{2,1,0:T(8,128)(2,1)S(1)}, u32[]{:S(2)}, u32[]{:S(2)}) collective-permute-start(bf16[2,224,896]{2,1,0:T(8,128)(2,1)S(1)} %collective-permute-done.2), channel_id=1, source_target_pairs={{0,32},{1,225},{2,34},{3,227},{4,36},{5,229},{6,38},{7,231},{8,40}... | collective-permute-start | bytes 2408456 | tf_op jit(solution)/shard_map/ppermute | solution.py:174
  93.8 12.8 %collective-permute-start.22 = (bf16[1,224,896]{2,1,0:T(8,128)(2,1)S(1)}, bf16[1,224,896]{2,1,0:T(8,128)(2,1)S(1)}, u32[]{:S(2)}, u32[]{:S(2)}) collective-permute-start(bf16[1,224,896]{2,1,0:T(8,128)(2,1)S(1)} %collective-permute-done.17), channel_id=1, source_target_pairs={{0,16},{16,0},{32,48},{48,32},{64,80},{80,64},{96,112},{112,96},{1... | collective-permute-start | bytes 1204232 | tf_op jit(solution)/shard_map/ppermute | solution.py:174
  95.1 26.0 %collective-permute-start.25 = (bf16[1,224,896]{2,1,0:T(8,128)(2,1)S(1)}, bf16[1,224,896]{2,1,0:T(8,128)(2,1)S(1)}, u32[]{:S(2)}, u32[]{:S(2)}) collective-permute-start(bf16[1,224,896]{2,1,0:T(8,128)(2,1)S(1)} %collective-permute-done.12), channel_id=1, source_target_pairs={{0,16},{16,0},{32,48},{48,32},{64,80},{80,64},{96,112},{112,96},{1... | collective-permute-start | bytes 1204232 | tf_op jit(solution)/shard_map/ppermute | solution.py:174
  98.4 12.5 %collective-permute-start.21 = (bf16[1,224,896]{2,1,0:T(8,128)(2,1)S(1)}, bf16[1,224,896]{2,1,0:T(8,128)(2,1)S(1)}, u32[]{:S(2)}, u32[]{:S(2)}) collective-permute-start(bf16[1,224,896]{2,1,0:T(8,128)(2,1)S(1)} %collective-permute-done.19), channel_id=1, source_target_pairs={{0,224},{1,33},{2,226},{3,35},{4,228},{5,37},{6,230},{7,39},{8,232... | collective-permute-start | bytes 1204232 | tf_op jit(solution)/shard_map/ppermute | solution.py:174
  106.7 16.7 %collective-permute-start.26 = (bf16[1,224,896]{2,1,0:T(8,128)(2,1)S(1)}, bf16[1,224,896]{2,1,0:T(8,128)(2,1)S(1)}, u32[]{:S(2)}, u32[]{:S(2)}) collective-permute-start(bf16[1,224,896]{2,1,0:T(8,128)(2,1)S(1)} %collective-permute-done.22), channel_id=1, source_target_pairs={{0,32},{1,225},{2,34},{3,227},{4,36},{5,229},{6,38},{7,231},{8,40}... | collective-permute-start | bytes 1204232 | tf_op jit(solution)/shard_map/ppermute | solution.py:174
  110.3 22.2 %collective-permute-start.7 = (bf16[2,224,896]{2,1,0:T(8,128)(2,1)S(1)}, bf16[2,224,896]{2,1,0:T(8,128)(2,1)S(1)}, u32[]{:S(2)}, u32[]{:S(2)}) collective-permute-start(bf16[2,224,896]{2,1,0:T(8,128)(2,1)S(1)} %collective-permute-done.3), channel_id=1, source_target_pairs={{0,16},{16,0},{32,48},{48,32},{64,80},{80,64},{96,112},{112,96},{1... | collective-permute-start | bytes 2408456 | tf_op jit(solution)/shard_map/ppermute | solution.py:174
  110.9 8.3 %collective-permute-start.24 = (bf16[1,224,896]{2,1,0:T(8,128)(2,1)S(1)}, bf16[1,224,896]{2,1,0:T(8,128)(2,1)S(1)}, u32[]{:S(2)}, u32[]{:S(2)}) collective-permute-start(bf16[1,224,896]{2,1,0:T(8,128)(2,1)S(1)} %collective-permute-done.21), channel_id=1, source_target_pairs={{0,224},{1,33},{2,226},{3,35},{4,228},{5,37},{6,230},{7,39},{8,232... | collective-permute-start | bytes 1204232 | tf_op jit(solution)/shard_map/ppermute | solution.py:174
  114.1 77.5 %collective-permute-start.28 = (bf16[2,224,896]{2,1,0:T(8,128)(2,1)S(1)}, bf16[2,224,896]{2,1,0:T(8,128)(2,1)S(1)}, u32[]{:S(2)}, u32[]{:S(2)}) collective-permute-start(bf16[2,224,896]{2,1,0:T(8,128)(2,1)S(1)} %collective-permute-done), channel_id=1, source_target_pairs={{0,16},{16,0},{32,48},{48,32},{64,80},{80,64},{96,112},{112,96},{1... | collective-permute-start | bytes 2408456 | tf_op jit(solution)/shard_map/ppermute | solution.py:174
  119.1 49.3 %collective-permute-start.6 = (bf16[2,224,896]{2,1,0:T(8,128)(2,1)S(1)}, bf16[2,224,896]{2,1,0:T(8,128)(2,1)S(1)}, u32[]{:S(2)}, u32[]{:S(2)}) collective-permute-start(bf16[2,224,896]{2,1,0:T(8,128)(2,1)S(1)} %collective-permute-done.3), channel_id=1, source_target_pairs={{0,224},{1,33},{2,226},{3,35},{4,228},{5,37},{6,230},{7,39},{8,232... | collective-permute-start | bytes 2408456 | tf_op jit(solution)/shard_map/ppermute | solution.py:174
  121.1 21.6 %collective-permute-start.8 = (bf16[2,224,896]{2,1,0:T(8,128)(2,1)S(1)}, bf16[2,224,896]{2,1,0:T(8,128)(2,1)S(1)}, u32[]{:S(2)}, u32[]{:S(2)}) collective-permute-start(bf16[2,224,896]{2,1,0:T(8,128)(2,1)S(1)} %collective-permute-done.5), channel_id=1, source_target_pairs={{0,32},{1,225},{2,34},{3,227},{4,36},{5,229},{6,38},{7,231},{8,40}... | collective-permute-start | bytes 2408456 | tf_op jit(solution)/shard_map/ppermute | solution.py:174
  123.4 43.4 %collective-permute-start.10 = (bf16[2,224,896]{2,1,0:T(8,128)(2,1)S(1)}, bf16[2,224,896]{2,1,0:T(8,128)(2,1)S(1)}, u32[]{:S(2)}, u32[]{:S(2)}) collective-permute-start(bf16[2,224,896]{2,1,0:T(8,128)(2,1)S(1)} %collective-permute-done.5), channel_id=1, source_target_pairs={{0,16},{16,0},{32,48},{48,32},{64,80},{80,64},{96,112},{112,96},{1... | collective-permute-start | bytes 2408456 | tf_op jit(solution)/shard_map/ppermute | solution.py:174
  132.4 37.9 %collective-permute-start.9 = (bf16[2,224,896]{2,1,0:T(8,128)(2,1)S(1)}, bf16[2,224,896]{2,1,0:T(8,128)(2,1)S(1)}, u32[]{:S(2)}, u32[]{:S(2)}) collective-permute-start(bf16[2,224,896]{2,1,0:T(8,128)(2,1)S(1)} %collective-permute-done.7), channel_id=1, source_target_pairs={{0,224},{1,33},{2,226},{3,35},{4,228},{5,37},{6,230},{7,39},{8,232... | collective-permute-start | bytes 2408456 | tf_op jit(solution)/shard_map/ppermute | solution.py:174
  142.7 30.5 %collective-permute-start.11 = (bf16[2,224,896]{2,1,0:T(8,128)(2,1)S(1)}, bf16[2,224,896]{2,1,0:T(8,128)(2,1)S(1)}, u32[]{:S(2)}, u32[]{:S(2)}) collective-permute-start(bf16[2,224,896]{2,1,0:T(8,128)(2,1)S(1)} %collective-permute-done.8), channel_id=1, source_target_pairs={{0,32},{1,225},{2,34},{3,227},{4,36},{5,229},{6,38},{7,231},{8,40}... | collective-permute-start | bytes 2408456 | tf_op jit(solution)/shard_map/ppermute | solution.py:174
  166.8 25.8 %collective-permute-start.29 = (bf16[2,224,896]{2,1,0:T(8,128)(2,1)S(1)}, bf16[2,224,896]{2,1,0:T(8,128)(2,1)S(1)}, u32[]{:S(2)}, u32[]{:S(2)}) collective-permute-start(bf16[2,224,896]{2,1,0:T(8,128)(2,1)S(1)} %collective-permute-done.10), channel_id=1, source_target_pairs={{0,32},{1,225},{2,34},{3,227},{4,36},{5,229},{6,38},{7,231},{8,40}... | collective-permute-start | bytes 2408456 | tf_op jit(solution)/shard_map/ppermute | solution.py:174
  170.4 20.3 %collective-permute-start.27 = (bf16[2,224,896]{2,1,0:T(8,128)(2,1)S(1)}, bf16[2,224,896]{2,1,0:T(8,128)(2,1)S(1)}, u32[]{:S(2)}, u32[]{:S(2)}) collective-permute-start(bf16[2,224,896]{2,1,0:T(8,128)(2,1)S(1)} %collective-permute-done.9), channel_id=1, source_target_pairs={{0,224},{1,33},{2,226},{3,35},{4,228},{5,37},{6,230},{7,39},{8,232... | collective-permute-start | bytes 2408456 | tf_op jit(solution)/shard_map/ppermute | solution.py:174
  (8 other events, 34.3 us)
